TPU v7x, 128 devices: a whole 4x4x4 slice. The times are simulated.
128 devices in a mesh: slab: 32 (over z, y, core), sub: 4 (over x).
Axes of the slice: x: 4, y: 4, z: 4, core: 2. Of those that a mesh axis runs over, the one named last changes fastest.
Arguments:
- factor_obs: float32 [128, 64, 64, 512], P('slab', 'sub'), may hold values from -0.1484375 to 0.1484375
- factor_ctrl: float32 [128, 64, 64, 512], P('slab', 'sub'), may hold values from -0.1484375 to 0.1484375
- diffusivity: float32 [128, 4096], P('slab', 'sub'), may hold values from 0.5 to 2
- input_map: float32 [4, 128, 4096], P(None, 'slab', 'sub'), may hold values from -1 to 1
- output_map: float32 [4, 128, 4096], P(None, 'slab', 'sub'), may hold values from -1 to 1
- start_block: float32 [512, 128], replicated, may hold values from -6 to 6
- order: int32 [1], replicated, may hold values from 64 to 128
Outputs:
- reduced_mass: float32 [128, 128], replicated
- reduced_state: float32 [128, 128], replicated
- reduced_input: float32 [128, 4], replicated
- reduced_output: float32 [4, 128], replicated
All inputs are finite; a program needn't handle non-finite values.
Results may differ from a plain program's by a relative error of at most 0.00017.
Values sent between devices are 32-bit elements; how exact they have to be, the bound alone decides.
No kernel may reach another device: no remote copies, remote signals or barrier semaphores. Data moves between devices by JAX's collectives and lax.ppermute only.
A program may use at most 128 MiB of HBM per device.

v0:
```python
import functools

import jax
import jax.numpy as jnp
from jax import lax
from jax.experimental import pallas as pl
from jax.experimental.pallas import tpu as pltpu
from jax.sharding import PartitionSpec as P

ALL = ("slab", "sub")
F32 = jnp.float32
BF16 = jnp.bfloat16
PANEL = 32


def split2(x):
    high = x.astype(BF16)
    return high, (x - high.astype(F32)).astype(BF16)


def split3(x):
    high = x.astype(BF16)
    rest = x - high.astype(F32)
    mid = rest.astype(BF16)
    return high, mid, (rest - mid.astype(F32)).astype(BF16)


def product(a, b, contract=((1,), (0,))):
    return lax.dot_general(a, b, (contract, ((), ())), preferred_element_type=F32)


def product3(a, b, contract=((1,), (0,))):
    ah, al = split2(a)
    bh, bl = split2(b)
    return product(ah, bh, contract) + (product(ah, bl, contract) + product(al, bh, contract))


def product6(a, b, contract=((1,), (0,))):
    a0, a1, a2 = split3(a)
    b0, b1, b2 = split3(b)
    dot = functools.partial(product, contract=contract)
    small = dot(a1, b1) + (dot(a0, b2) + dot(a2, b0))
    return dot(a0, b0) + ((dot(a0, b1) + dot(a1, b0)) + small)


def rows_split(rows):
    both = jnp.concatenate([rows, rows], axis=0)
    high = both.astype(BF16).astype(F32)
    place = lax.broadcasted_iota(jnp.int32, both.shape, 0)
    halves = jnp.where(place < rows.shape[0], high, both - high)
    return jnp.concatenate([halves, jnp.zeros_like(halves)], axis=0).astype(BF16)


def add_products(total, extra, turned, few, right):
    count = turned.shape[0]
    th, tl = split2(turned)
    rh, rl = split2(right)
    first = product(jnp.concatenate([th, tl, few], axis=0), rh)
    second = product(jnp.concatenate([th, few], axis=0), rl)
    total[...] += first[:count] + (first[count : 2 * count] + second[:count])
    extra[...] += first[2 * count :] + second[count:]


def gram_kernel(steps, obs, ctrl, sense, gram, few, zlow, zhigh, ylow, yhigh, total, extra):
    step = pl.program_id(0)

    @pl.when(step == 0)
    def _():
        total[...] = jnp.zeros_like(total)
        extra[...] = jnp.zeros_like(extra)

    right = ctrl[...]
    side = ylow.shape[0]

    @pl.when(step < 2)
    def _():
        zlow[...] = right

    @pl.when(step >= steps - 2)
    def _():
        zhigh[...] = right

    @pl.when(step % 2 == 0)
    def _():
        ylow[...] = right[:side]

    @pl.when(step % 2 == 1)
    def _():
        yhigh[...] = right[right.shape[0] - side :]

    add_products(total, extra, obs[...].T, rows_split(sense[...]), right)

    @pl.when(step == steps - 1)
    def _():
        half = gram.shape[3]
        for side_index in range(2):
            cols = total[:, side_index * half : (side_index + 1) * half]
            gram[:, side_index] = cols.reshape(gram.shape[0], gram.shape[2], half)
        few[...] = extra[:8]


def local_gram(observe, control, sense, lines, points):
    cells, rank = control.shape
    steps = 8
    rows = cells // steps
    plane = 2 * rows
    block = pl.BlockSpec((rows, rank), lambda i: (i, 0))
    return pl.pallas_call(
        functools.partial(gram_kernel, steps),
        grid=(steps,),
        in_specs=[block, block, pl.BlockSpec((sense.shape[0], rows), lambda i: (0, i))],
        out_specs=[
            pl.BlockSpec((64, 2, 8, rank // 2), lambda i: (0, 0, 0, 0)),
            pl.BlockSpec((8, rank), lambda i: (0, 0)),
            pl.BlockSpec((rows, rank), lambda i: (jnp.minimum(i, 1), 0)),
            pl.BlockSpec((rows, rank), lambda i: (jnp.maximum(i - (steps - 2), 0), 0)),
            pl.BlockSpec((points, rank), lambda i: (i // 2, 0)),
            pl.BlockSpec((points, rank), lambda i: (i // 2, 0)),
        ],
        out_shape=[
            jax.ShapeDtypeStruct((64, 2, 8, rank // 2), F32),
            jax.ShapeDtypeStruct((8, rank), F32),
            jax.ShapeDtypeStruct((plane, rank), F32),
            jax.ShapeDtypeStruct((plane, rank), F32),
            jax.ShapeDtypeStruct((steps // 2 * points, rank), F32),
            jax.ShapeDtypeStruct((steps // 2 * points, rank), F32),
        ],
        scratch_shapes=[pltpu.VMEM((rank, rank), F32), pltpu.VMEM((16, rank), F32)],
        compiler_params=pltpu.CompilerParams(vmem_limit_bytes=40 << 20),
        cost_estimate=pl.CostEstimate(
            flops=6 * cells * rank * rank, bytes_accessed=24 << 20, transcendentals=0
        ),
        name="local_gram",
    )(observe, control, sense)


def stencil_kernel(
    steps, lines, points,
    obs, conduct, drive, few_ctrl, ctrl, zlow, zhigh, ylow, yhigh,
    out, field, total, extra, sems,
):
    step = pl.program_id(0)
    planes = steps // 2
    inner = pl.ds(1, lines)
    copies = [pltpu.make_async_copy(zlow, field.at[0, inner], sems.at[0])]
    for p in range(planes):
        copies.append(pltpu.make_async_copy(ctrl.at[p], field.at[p + 1, inner], sems.at[p + 1]))
    copies.append(pltpu.make_async_copy(zhigh, field.at[planes + 1, inner], sems.at[planes + 1]))
    sides = [
        pltpu.make_async_copy(ylow, field.at[pl.ds(1, planes), 0], sems.at[planes + 2]),
        pltpu.make_async_copy(yhigh, field.at[pl.ds(1, planes), lines + 1], sems.at[planes + 3]),
    ]

    @pl.when(step == 0)
    def _():
        for copy in copies[:3] + sides + copies[3:]:
            copy.start()
        total[...] = jnp.zeros_like(total)
        extra[...] = jnp.zeros_like(extra)
        for copy in copies[:3] + sides:
            copy.wait()

    for p in range(1, planes):

        @pl.when(step == 2 * p)
        def _():
            copies[p + 2].wait()

    p = step // 2
    half = lines // 2
    line = (step % 2) * half

    def part(plane, first):
        return field[plane, pl.ds(first, half)]

    center = part(p + 1, line + 1)
    beside = part(p + 2, line + 1) + part(p, line + 1)
    beside = beside + part(p + 1, line + 2) + part(p + 1, line)
    rows = half * points
    rank = center.shape[-1]
    center = center.reshape(rows, rank)
    beside = beside.reshape(rows, rank)
    place = lax.broadcasted_iota(jnp.int32, (rows, rank), 0) % points
    beside = beside + jnp.where(place > 0, pltpu.roll(center, 1, 0), 0.0)
    beside = beside + jnp.where(place < points - 1, pltpu.roll(center, rows - 1, 0), 0.0)
    applied = (beside - 6.0 * center).T * (conduct[0] * (1.0 / 6.0))
    add_products(total, extra, applied, rows_split(drive[...]), obs[...])

    @pl.when(step == steps - 1)
    def _():
        width = rank // 2
        for side_index in range(2):
            cols = total[:, side_index * width : (side_index + 1) * width]
            out[:, side_index, :, :width] = cols.reshape(out.shape[0], out.shape[2], width)
        summed = jnp.concatenate([extra[0:4] + extra[4:8], few_ctrl[0:4] + few_ctrl[4:8]], axis=0)
        wide = jnp.concatenate([summed, jnp.zeros((120, rank), F32)], axis=0).T
        out[:, 0, :, width:] = wide.reshape(out.shape[0], out.shape[2], 128)
        out[:, 1, :, width:] = jnp.zeros((out.shape[0], out.shape[2], 128), F32)


def local_operator(observe, control4, conduct, drive, few_ctrl, zlow, zhigh, ylow, yhigh):
    planes, lines, points, rank = control4.shape
    cells = planes * lines * points
    steps = 2 * planes
    rows = cells // steps
    anywhere = pl.BlockSpec(memory_space=pl.ANY)
    return pl.pallas_call(
        functools.partial(stencil_kernel, steps, lines, points),
        grid=(steps,),
        in_specs=[
            pl.BlockSpec((rows, rank), lambda i: (i, 0)),
            pl.BlockSpec((1, 1, rows), lambda i: (i, 0, 0)),
            pl.BlockSpec((drive.shape[0], rows), lambda i: (0, i)),
            pl.BlockSpec((8, rank), lambda i: (0, 0)),
        ]
        + [anywhere] * 5,
        out_specs=pl.BlockSpec((64, 2, 8, rank // 2 + 128), lambda i: (0, 0, 0, 0)),
        out_shape=jax.ShapeDtypeStruct((64, 2, 8, rank // 2 + 128), F32),
        scratch_shapes=[
            pltpu.VMEM((planes + 2, lines + 2, points, rank), F32),
            pltpu.VMEM((rank, rank), F32),
            pltpu.VMEM((16, rank), F32),
            pltpu.SemaphoreType.DMA((planes + 4,)),
        ],
        compiler_params=pltpu.CompilerParams(vmem_limit_bytes=44 << 20),
        cost_estimate=pl.CostEstimate(
            flops=6 * cells * rank * rank, bytes_accessed=24 << 20, transcendentals=0
        ),
        name="local_operator",
    )(
        observe,
        conduct.reshape(steps, 1, rows),
        drive,
        few_ctrl,
        control4,
        zlow.reshape(lines, points, rank),
        zhigh.reshape(lines, points, rank),
        ylow.reshape(planes, points, rank),
        yhigh.reshape(planes, points, rank),
    )


def sum_kernel(parts, out):
    whole = jnp.sum(parts[...], axis=0, keepdims=True)
    out[...] = jnp.broadcast_to(whole, out.shape)


def summed_everywhere(parts, name):
    shape = parts.shape
    tiles = parts.reshape(shape[0] * shape[1], *shape[2:])
    arrived = lax.all_to_all(tiles, ALL, 0, 0, tiled=True)
    copies = pl.pallas_call(
        sum_kernel,
        out_shape=jax.ShapeDtypeStruct(tiles.shape, F32),
        cost_estimate=pl.CostEstimate(
            flops=tiles.size, bytes_accessed=8 * tiles.size, transcendentals=0
        ),
        name="sum_" + name,
    )(arrived)
    return lax.all_to_all(copies, ALL, 0, 0, tiled=True).reshape(shape)


def inverse_factor(work):
    size = work.shape[0]
    for first in range(0, size, PANEL):
        last = first + PANEL
        panel = [work[first + 8 * g : first + 8 * g + 8, :] for g in range(PANEL // 8)]
        groups = PANEL // 8
        columns = {}
        for k in range(PANEL):
            for g in range(k // 8, groups):
                columns[k, g] = jnp.broadcast_to(
                    panel[g][:, first + k : first + k + 1], (8, 128)
                )
        place = lax.broadcasted_iota(jnp.int32, (8, 128), 0)
        for j in range(PANEL):
            gj, sj = divmod(j, 8)
            pivot = jnp.broadcast_to(columns[j, gj][sj : sj + 1], (8, 128))
            scale = lax.rsqrt(pivot)
            lower = {}
            for g in range(gj, groups):
                lower[g] = columns[j, g] * scale
            row = jnp.broadcast_to(panel[gj][sj : sj + 1], (8, 256))
            row = row * jnp.concatenate([scale, scale], axis=1)
            for k in range(j + 1, PANEL):
                gk, sk = divmod(k, 8)
                across = jnp.broadcast_to(lower[gk][sk : sk + 1], (8, 128))
                for g in range(gk, groups):
                    columns[k, g] = columns[k, g] - lower[g] * across
            for g in range(gj, groups):
                weight = lower[g]
                if g == gj:
                    weight = jnp.where(place > sj, weight, 0.0)
                wide = jnp.concatenate([weight, weight], axis=1)
                panel[g] = panel[g] - wide * row
            wide_place = lax.broadcasted_iota(jnp.int32, (8, 256), 0)
            panel[gj] = jnp.where(wide_place == sj, row, panel[gj])
        for g in range(groups):
            work[first + 8 * g : first + 8 * g + 8, :] = panel[g]
        if last < size:
            done = jnp.concatenate(panel, axis=0)
            u0, u1, u2 = split3(done)
            left = jnp.concatenate([u0, u0, u1, u1, u0, u2], axis=0)[:, :size]
            right = jnp.concatenate([u0, u1, u0, u1, u2, u0], axis=0)
            change = product(left, right, ((0,), (0,)))
            work[last:, :] -= change[last:, :]


def bases_kernel(turn_start, gram, start, right_out, left_out, image_out, cross, basis, image, work):
    rank = cross.shape[0]
    half = rank // 2
    for side_index in range(2):
        cols = gram[:, side_index].reshape(rank, half)
        cross[:, side_index * half : (side_index + 1) * half] = cols
    basis[...] = start[...].T if turn_start else start[...]
    size = basis.shape[0]
    eye = (
        lax.broadcasted_iota(jnp.int32, (size, size), 0)
        == lax.broadcasted_iota(jnp.int32, (size, size), 1)
    ).astype(F32)

    @pl.loop(0, 2)
    def _(turn):
        @pl.when(turn == 0)
        def _():
            image[...] = product3(basis[...], cross[...])

        @pl.when(turn == 1)
        def _():
            image[...] = product3(basis[...], cross[...], ((1,), (1,)))

        held = image[...]
        work[:, :size] = product6(held, held, ((1,), (1,)))
        work[:, size:] = eye
        inverse_factor(work)
        basis[...] = product6(work[:, size:], held)

        @pl.when(turn == 0)
        def _():
            right_out[...] = basis[...]

    left_out[...] = basis[...]
    image_out[...] = image[...]


def two_bases(gram, start, turn_start, name):
    rank = gram.shape[0] * gram.shape[2]
    size = 128
    shape = jax.ShapeDtypeStruct((size, rank), F32)
    return pl.pallas_call(
        functools.partial(bases_kernel, turn_start),
        out_shape=[shape, shape, shape],
        scratch_shapes=[
            pltpu.VMEM((rank, rank), F32),
            pltpu.VMEM((size, rank), F32),
            pltpu.VMEM((size, rank), F32),
            pltpu.VMEM((size, 2 * size), F32),
        ],
        compiler_params=pltpu.CompilerParams(vmem_limit_bytes=24 << 20),
        cost_estimate=pl.CostEstimate(
            flops=10_000_000_000, bytes_accessed=4 << 20, transcendentals=0
        ),
        name=name,
    )(gram, start)


def finish_kernel(order, right, left, image, oper, mass, state, inputs, outputs, turned):
    size, rank = right.shape
    half = rank // 2
    for side_index in range(2):
        cols = oper[:, side_index, :, :half].reshape(rank, half)
        turned[:, side_index * half : (side_index + 1) * half] = cols
    few = oper[:, 0, :, half:].reshape(rank, 128)
    kept_col = lax.broadcasted_iota(jnp.int32, (size, size), 0) < order[0]
    kept_row = lax.broadcasted_iota(jnp.int32, (size, size), 1) < order[0]
    kept = jnp.logical_and(kept_col, kept_row).astype(F32)
    both = ((1,), (1,))
    mass[...] = kept * product6(left[...], image[...], both)
    state[...] = kept * product3(left[...], product3(right[...], turned[...]), both)
    inputs[...] = (kept_col.astype(F32) * product3(left[...], few))[:, :4]
    outputs[...] = (kept_row.astype(F32) * product3(right[...], few).T)[4:8]


def finish(order, right, left, image, oper):
    size, rank = right.shape
    vmem = pl.BlockSpec(memory_space=pltpu.VMEM)
    return pl.pallas_call(
        finish_kernel,
        in_specs=[pl.BlockSpec(memory_space=pltpu.SMEM)] + [vmem] * 4,
        out_specs=[vmem] * 4,
        out_shape=[
            jax.ShapeDtypeStruct((size, size), F32),
            jax.ShapeDtypeStruct((size, size), F32),
            jax.ShapeDtypeStruct((size, 4), F32),
            jax.ShapeDtypeStruct((4, size), F32),
        ],
        scratch_shapes=[pltpu.VMEM((rank, rank), F32)],
        compiler_params=pltpu.CompilerParams(vmem_limit_bytes=24 << 20),
        cost_estimate=pl.CostEstimate(
            flops=1_000_000_000, bytes_accessed=4 << 20, transcendentals=0
        ),
        name="finish",
    )(order, right, left, image, oper)


def from_neighbours(low_face, high_face, axis):
    count = lax.axis_size(axis)
    up = [(i, i + 1) for i in range(count - 1)]
    down = [(b, a) for a, b in up]
    return lax.ppermute(high_face, axis, up), lax.ppermute(low_face, axis, down)


def on_device(factor_obs, factor_ctrl, diffusivity, input_map, output_map, start_block, order):
    planes, lines, points, rank = factor_ctrl.shape
    cells = planes * lines * points
    observe = factor_obs.reshape(cells, rank)
    control = factor_ctrl.reshape(cells, rank)
    drive = input_map.reshape(input_map.shape[0], cells)
    sense = output_map.reshape(output_map.shape[0], cells)
    gram, few_ctrl, zlow, zhigh, ylow, yhigh = local_gram(observe, control, sense, lines, points)
    gram = summed_everywhere(gram, "gram")
    zlow, zhigh = from_neighbours(zlow, zhigh, "slab")
    ylow, yhigh = from_neighbours(ylow, yhigh, "sub")
    oper = local_operator(
        observe, factor_ctrl, diffusivity, drive, few_ctrl, zlow, zhigh, ylow, yhigh
    )
    oper = summed_everywhere(oper, "operator")
    _, left, _ = two_bases(gram, start_block, True, "first_bases")
    right, left, image = two_bases(gram, left, False, "second_bases")
    return finish(order, right, left, image, oper)


def solution(mesh):
    placed = (
        P("slab", "sub", None, None),
        P("slab", "sub", None, None),
        P("slab", "sub"),
        P(None, "slab", "sub"),
        P(None, "slab", "sub"),
        P(),
        P(),
    )
    return jax.shard_map(
        on_device, mesh=mesh, in_specs=placed, out_specs=(P(), P(), P(), P()), check_vma=False
    )
```

profile of v0, /device:TPU:1, one launch (start us, length us, event | category | flops | bytes accessed | tf_op | source)
XLA Modules:
  0.0 166.4 jit_solution(450856182811372839)
XLA Ops:
  0.6 0.9 copy.12
  1.5 14.0 %local_gram.1 = (f32[64,2,8,256]{3,2,1,0:T(8,128)}, f32[8,512]{1,0:T(8,128)S(1)}, f32[1024,512]{1,0:T(8,128)S(1)}, f32[1024,512]{1,0:T(8,128)}, f32[256,512]{1,0:T(8,128)S(1)}, /*index=5*/f32[256,512]{1,0:T(8,128)}) custom-call(f32[4096,512]{1,0:T(8,128)} %bitcast.22, f32[4096,512]{1,0:T(8,128)} %bitcast.24, f32[4,4096]{1,0:T(4,128)S(1)} %bitcast.18), custom_call_target="tpu_custom_call" | custom-call | flops 6442450944 | bytes 25165824 | tf_op jit(solution)/shard_map/local_gram/pallas_call | solution.py:108
  15.6 4.7 %collective-permute-start = (f32[1024,512]{1,0:T(8,128)}, f32[1024,512]{1,0:T(8,128)}, u32[]{:S(2)}, u32[]{:S(2)}) collective-permute-start(f32[1024,512]{1,0:T(8,128)} %get-tuple-element.20), channel_id=1, source_target_pairs={{0,4},{4,8},{8,12},{12,16},{16,20},{20,24},{24,28},{28,32},{32,36}... | collective-permute-start | bytes 6291464 | tf_op jit(solution)/shard_map/ppermute | solution.py:410
  20.3 1.9 %collective-permute-start.1 = (f32[1024,512]{1,0:T(8,128)S(1)}, f32[1024,512]{1,0:T(8,128)}, u32[]{:S(2)}, u32[]{:S(2)}) collective-permute-start(f32[1024,512]{1,0:T(8,128)S(1)} %get-tuple-element.21), channel_id=1, source_target_pairs={{4,0},{8,4},{12,8},{16,12},{20,16},{24,20},{28,24},{32,28},{36,32}... | collective-permute-start | bytes 6291464 | tf_op jit(solution)/shard_map/ppermute | solution.py:410
  22.2 3.1 %collective-permute-start.2 = (f32[256,512]{1,0:T(8,128)}, f32[256,512]{1,0:T(8,128)S(1)}, u32[]{:S(2)}, u32[]{:S(2)}) collective-permute-start(f32[256,512]{1,0:T(8,128)} %get-tuple-element.22), channel_id=1, source_target_pairs={{0,1},{1,2},{2,3},{4,5},{5,6},{6,7},{8,9},{9,10},{10,11},{12,13},{... | collective-permute-start | bytes 1572872 | tf_op jit(solution)/shard_map/ppermute | solution.py:410
  25.3 1.3 collective-permute-start.3
  26.6 13.0 %all-to-all-start = ((f32[128,8,256]{2,1,0:T(8,128)}), f32[128,8,256]{2,1,0:T(8,128)}, u32[]{:S(2)}, u32[]{:S(2)}) async-start(f32[128,8,256]{2,1,0:T(8,128)} %bitcast.2), calls=%async_computation | async-start | bytes 2097152 | tf_op jit(solution)/shard_map/all_to_all | solution.py:251
  39.7 0.0 collective-permute-done.2
  39.7 1.5 collective-permute-done.3
  41.2 12.2 %collective-permute-done = f32[1024,512]{1,0:T(8,128)} collective-permute-done((f32[1024,512]{1,0:T(8,128)}, f32[1024,512]{1,0:T(8,128)}, u32[]{:S(2)}, u32[]{:S(2)}) %collective-permute-start) | collective-permute-done | bytes 2097184 | tf_op jit(solution)/shard_map/ppermute | solution.py:410
  53.4 4.4 %collective-permute-done.1 = f32[1024,512]{1,0:T(8,128)} collective-permute-done((f32[1024,512]{1,0:T(8,128)S(1)}, f32[1024,512]{1,0:T(8,128)}, u32[]{:S(2)}, u32[]{:S(2)}) %collective-permute-start.1) | collective-permute-done | bytes 2097184 | tf_op jit(solution)/shard_map/ppermute | solution.py:410
  57.9 16.1 %local_operator.1 = f32[64,2,8,384]{3,2,1,0:T(8,128)} custom-call(f32[4096,512]{1,0:T(8,128)} %bitcast.23, f32[8,1,512]{2,1,0:T(1,128)S(1)} %reshape.52.conduct, f32[4,4096]{1,0:T(4,128)S(1)} %bitcast.17, f32[8,512]{1,0:T(8,128)S(1)} %get-tuple-element.19.few_ctrl, f32[4,16,64,512]{3,2,1,0:T(8,128)} %ctrl.1, f32[16,64,512]{2,1,0:T(8,128)} %bitcast.4.zlow, ...), custom_call_target="tpu_custom_call" | custom-call | flops 6442450944 | bytes 25165824 | tf_op jit(solution)/shard_map/local_operator/pallas_call | solution.py:207
  74.0 12.4 %all-to-all-start.2 = ((f32[128,8,384]{2,1,0:T(8,128)}), f32[128,8,384]{2,1,0:T(8,128)S(1)}, u32[]{:S(2)}, u32[]{:S(2)}) async-start(f32[128,8,384]{2,1,0:T(8,128)} %bitcast.8), calls=%async_computation.2 | async-start | bytes 3145728 | tf_op jit(solution)/shard_map/all_to_all | solution.py:251
  86.5 2.4 %sum_gram.1 = f32[128,8,256]{2,1,0:T(8,128)} custom-call(f32[128,8,256]{2,1,0:T(8,128)} %all-to-all-done.parts), custom_call_target="tpu_custom_call" | custom-call | flops 262144 | bytes 2097152 | tf_op jit(solution)/shard_map/sum_gram/pallas_call | solution.py:252
  88.9 22.7 %all-to-all-done.2.parts = f32[128,8,384]{2,1,0:T(8,128)S(1)} async-done(((f32[128,8,384]{2,1,0:T(8,128)}), f32[128,8,384]{2,1,0:T(8,128)S(1)}, u32[]{:S(2)}, u32[]{:S(2)}) %all-to-all-start.2) | async-done | bytes 1572896 | tf_op jit(solution)/shard_map/all_to_all | solution.py:251
  111.6 3.8 %all-to-all-start.1 = ((f32[128,8,256]{2,1,0:T(8,128)}), f32[128,8,256]{2,1,0:T(8,128)S(1)}, u32[]{:S(2)}, u32[]{:S(2)}) async-start(f32[128,8,256]{2,1,0:T(8,128)} %sum_gram.1), calls=%async_computation.1 | async-start | bytes 2097152 | tf_op jit(solution)/shard_map/all_to_all | solution.py:260
  116.1 2.8 %sum_operator.1 = f32[128,8,384]{2,1,0:T(8,128)} custom-call(f32[128,8,384]{2,1,0:T(8,128)} %copy-done.1), custom_call_target="tpu_custom_call" | custom-call | flops 393216 | bytes 3145728 | tf_op jit(solution)/shard_map/sum_operator/pallas_call | solution.py:252
  118.9 16.2 %all-to-all-done.1 = f32[128,8,256]{2,1,0:T(8,128)S(1)} async-done(((f32[128,8,256]{2,1,0:T(8,128)}), f32[128,8,256]{2,1,0:T(8,128)S(1)}, u32[]{:S(2)}, u32[]{:S(2)}) %all-to-all-start.1) | async-done | bytes 1048608 | tf_op jit(solution)/shard_map/all_to_all | solution.py:260
  135.1 3.8 %all-to-all-start.3 = ((f32[128,8,384]{2,1,0:T(8,128)}), f32[128,8,384]{2,1,0:T(8,128)S(1)}, u32[]{:S(2)}, u32[]{:S(2)}) async-start(f32[128,8,384]{2,1,0:T(8,128)} %sum_operator.1), calls=%async_computation.3 | async-start | bytes 3145728 | tf_op jit(solution)/shard_map/all_to_all | solution.py:260
  138.9 10.2 %first_bases.1 = (f32[128,512]{1,0:T(8,128)}, f32[128,512]{1,0:T(8,128)S(1)}, f32[128,512]{1,0:T(8,128)}) custom-call(f32[64,2,8,256]{3,2,1,0:T(8,128)S(1)} %bitcast.15, f32[512,128]{1,0:T(8,128)S(1)} %copy-done), custom_call_target="tpu_custom_call" | custom-call | flops 10000000000 | bytes 4194304 | tf_op jit(solution)/shard_map/first_bases/pallas_call | solution.py:350
  149.1 9.3 %second_bases.1 = (f32[128,512]{1,0:T(8,128)S(1)}, f32[128,512]{1,0:T(8,128)S(1)}, f32[128,512]{1,0:T(8,128)S(1)}) custom-call(f32[64,2,8,256]{3,2,1,0:T(8,128)S(1)} %bitcast.16, f32[128,512]{1,0:T(8,128)S(1)} %get-tuple-element.15.start), custom_call_target="tpu_custom_call" | custom-call | flops 10000000000 | bytes 4194304 | tf_op jit(solution)/shard_map/second_bases/pallas_call | solution.py:350
  158.4 5.7 %all-to-all-done.3 = f32[128,8,384]{2,1,0:T(8,128)S(1)} async-done(((f32[128,8,384]{2,1,0:T(8,128)}), f32[128,8,384]{2,1,0:T(8,128)S(1)}, u32[]{:S(2)}, u32[]{:S(2)}) %all-to-all-start.3) | async-done | bytes 1572896 | tf_op jit(solution)/shard_map/all_to_all | solution.py:260
  164.1 1.6 finish.1
  165.8 0.7 copy.11
  (11 shorter events, 0.1 us)
Async XLA Ops:
  15.5 24.1 %copy-start.3 = (f32[4,1024]{1,0:T(4,128)S(1)}, f32[4,1024]{1,0:T(4,128)}, u32[]{:S(2)}) copy-start(f32[4,1024]{1,0:T(4,128)} %param.9) | copy-start | bytes 49156
  15.5 24.1 %copy-start.2 = (f32[4,4,1024]{2,1,0:T(4,128)S(1)}, f32[4,4,1024]{2,1,0:T(4,128)}, u32[]{:S(2)}) copy-start(f32[4,4,1024]{2,1,0:T(4,128)} %param.10) | copy-start | bytes 196612
  15.6 37.9 %collective-permute-start = (f32[1024,512]{1,0:T(8,128)}, f32[1024,512]{1,0:T(8,128)}, u32[]{:S(2)}, u32[]{:S(2)}) collective-permute-start(f32[1024,512]{1,0:T(8,128)} %get-tuple-element.20), channel_id=1, source_target_pairs={{0,4},{4,8},{8,12},{12,16},{16,20},{20,24},{24,28},{28,32},{32,36}... | collective-permute-start | bytes 6291464 | tf_op jit(solution)/shard_map/ppermute | solution.py:410
  20.3 37.6 %collective-permute-start.1 = (f32[1024,512]{1,0:T(8,128)S(1)}, f32[1024,512]{1,0:T(8,128)}, u32[]{:S(2)}, u32[]{:S(2)}) collective-permute-start(f32[1024,512]{1,0:T(8,128)S(1)} %get-tuple-element.21), channel_id=1, source_target_pairs={{4,0},{8,4},{12,8},{16,12},{20,16},{24,20},{28,24},{32,28},{36,32}... | collective-permute-start | bytes 6291464 | tf_op jit(solution)/shard_map/ppermute | solution.py:410
  22.2 17.5 %collective-permute-start.2 = (f32[256,512]{1,0:T(8,128)}, f32[256,512]{1,0:T(8,128)S(1)}, u32[]{:S(2)}, u32[]{:S(2)}) collective-permute-start(f32[256,512]{1,0:T(8,128)} %get-tuple-element.22), channel_id=1, source_target_pairs={{0,1},{1,2},{2,3},{4,5},{5,6},{6,7},{8,9},{9,10},{10,11},{12,13},{... | collective-permute-start | bytes 1572872 | tf_op jit(solution)/shard_map/ppermute | solution.py:410
  25.3 15.9 %collective-permute-start.3 = (f32[256,512]{1,0:T(8,128)S(1)}, f32[256,512]{1,0:T(8,128)}, u32[]{:S(2)}, u32[]{:S(2)}) collective-permute-start(f32[256,512]{1,0:T(8,128)S(1)} %get-tuple-element.23), channel_id=1, source_target_pairs={{1,0},{2,1},{3,2},{5,4},{6,5},{7,6},{9,8},{10,9},{11,10},{13,12},{... | collective-permute-start | bytes 1572872 | tf_op jit(solution)/shard_map/ppermute | solution.py:410
  26.6 47.4 %all-to-all-start = ((f32[128,8,256]{2,1,0:T(8,128)}), f32[128,8,256]{2,1,0:T(8,128)}, u32[]{:S(2)}, u32[]{:S(2)}) async-start(f32[128,8,256]{2,1,0:T(8,128)} %bitcast.2), calls=%async_computation | async-start | bytes 2097152 | tf_op jit(solution)/shard_map/all_to_all | solution.py:251
  74.0 37.6 %all-to-all-start.2 = ((f32[128,8,384]{2,1,0:T(8,128)}), f32[128,8,384]{2,1,0:T(8,128)S(1)}, u32[]{:S(2)}, u32[]{:S(2)}) async-start(f32[128,8,384]{2,1,0:T(8,128)} %bitcast.8), calls=%async_computation.2 | async-start | bytes 3145728 | tf_op jit(solution)/shard_map/all_to_all | solution.py:251
  111.6 4.4 %copy-start.1 = (f32[128,8,384]{2,1,0:T(8,128)}, f32[128,8,384]{2,1,0:T(8,128)S(1)}, u32[]{:S(2)}) copy-start(f32[128,8,384]{2,1,0:T(8,128)S(1)} %all-to-all-done.2.parts) | copy-start | bytes 4718596
  111.6 23.4 %all-to-all-start.1 = ((f32[128,8,256]{2,1,0:T(8,128)}), f32[128,8,256]{2,1,0:T(8,128)S(1)}, u32[]{:S(2)}, u32[]{:S(2)}) async-start(f32[128,8,256]{2,1,0:T(8,128)} %sum_gram.1), calls=%async_computation.1 | async-start | bytes 2097152 | tf_op jit(solution)/shard_map/all_to_all | solution.py:260
  118.9 20.0 %copy-start = (f32[512,128]{1,0:T(8,128)S(1)}, f32[512,128]{1,0:T(8,128)}, u32[]{:S(2)}) copy-start(f32[512,128]{1,0:T(8,128)} %start.1) | copy-start | bytes 786436
  135.1 29.1 %all-to-all-start.3 = ((f32[128,8,384]{2,1,0:T(8,128)}), f32[128,8,384]{2,1,0:T(8,128)S(1)}, u32[]{:S(2)}, u32[]{:S(2)}) async-start(f32[128,8,384]{2,1,0:T(8,128)} %sum_operator.1), calls=%async_computation.3 | async-start | bytes 3145728 | tf_op jit(solution)/shard_map/all_to_all | solution.py:260
where the time goes:
time: 167 us; the launch traced here: 166 us
  waiting for transfers between devices  62.8 us (38%)
  Pallas kernels  56.6 us (34%)
  starting transfers between devices  44 us (26%)
    all_to_all x2, starting transfers between devices, summed_everywhere(): arrived = lax.all_to_all(tiles, ALL, 0, 0, tiled=True)  25.4 us
    all_to_all x2, waiting for transfers between devices, summed_everywhere(): arrived = lax.all_to_all(tiles, ALL, 0, 0, tiled=True)  22.7 us
    all_to_all x2, waiting for transfers between devices, summed_everywhere(): return lax.all_to_all(copies, ALL, 0, 0, tiled=True).reshape(shape)  21.9 us
    pallas_call x2, Pallas kernels, two_bases(): pl.pallas_call(functools.partial(bases_kernel, turn_start), out_shape=[sh...  19.5 us
    pallas_call x1, Pallas kernels, local_operator(): pl.pallas_call(functools.partial(stencil_kernel, steps, lines, points), g...  16.1 us
    pallas_call x1, Pallas kernels, local_gram(): pl.pallas_call(functools.partial(gram_kernel, steps), grid=(steps,), in_s...  14 us
    ppermute x2, waiting for transfers between devices, from_neighbours(): lax.ppermute(high_face, axis, up)  12.2 us
    ppermute x2, starting transfers between devices, from_neighbours(): lax.ppermute(high_face, axis, up)  7.84 us
  transfers between devices with their start and end apart: 8, of which 6 were waited for; matrix products, arithmetic and copies ran while one was open for 0% of the time, Pallas kernels for 25%

commit v1 on v0

v1 whole, which is shorter than its diff:
```python
import functools

import jax
import jax.numpy as jnp
from jax import lax
from jax.experimental import pallas as pl
from jax.experimental.pallas import tpu as pltpu
from jax.sharding import PartitionSpec as P


ALL = ("slab", "sub")
F32 = jnp.float32
BF16 = jnp.bfloat16
PANEL = 32


def split2(x):
    high = x.astype(BF16)
    return high, (x - high.astype(F32)).astype(BF16)


def split3(x):
    high = x.astype(BF16)
    rest = x - high.astype(F32)
    mid = rest.astype(BF16)
    return high, mid, (rest - mid.astype(F32)).astype(BF16)


def product(a, b, contract=((1,), (0,))):
    return lax.dot_general(a, b, (contract, ((), ())), preferred_element_type=F32)


def product3(a, b, contract=((1,), (0,))):
    ah, al = split2(a)
    bh, bl = split2(b)
    return product(ah, bh, contract) + (product(ah, bl, contract) + product(al, bh, contract))


def product6(a, b, contract=((1,), (0,))):
    a0, a1, a2 = split3(a)
    b0, b1, b2 = split3(b)
    dot = functools.partial(product, contract=contract)
    small = dot(a1, b1) + (dot(a0, b2) + dot(a2, b0))
    return dot(a0, b0) + ((dot(a0, b1) + dot(a1, b0)) + small)


def rows_split(rows):
    both = jnp.concatenate([rows, rows], axis=0)
    high = both.astype(BF16).astype(F32)
    place = lax.broadcasted_iota(jnp.int32, both.shape, 0)
    halves = jnp.where(place < rows.shape[0], high, both - high)
    return jnp.concatenate([halves, jnp.zeros_like(halves)], axis=0).astype(BF16)


def add_products(total, extra, turned, few, right):
    count = turned.shape[0]
    th, tl = split2(turned)
    rh, rl = split2(right)
    top = jnp.concatenate([th, tl, th], axis=1)
    bottom = jnp.concatenate([few, jnp.zeros_like(few), few], axis=1)
    result = product(
        jnp.concatenate([top, bottom], axis=0), jnp.concatenate([rh, rh, rl], axis=0)
    )
    total[...] += result[:count]
    extra[...] += result[count:]


def in_chunks(total, out):
    width = total.shape[1] // 2
    for side in range(2):
        cols = total[:, side * width : (side + 1) * width]
        out[:, side, :, :width] = cols.reshape(out.shape[0], out.shape[2], width)


def gram_kernel(obs, ctrl, sense, gram, few, obs_here, ctrl_here, total, extra, obs_sems, ctrl_sems):
    planes = obs.shape[0]

    def copies(p):
        return (
            pltpu.make_async_copy(obs.at[p], obs_here.at[p], obs_sems.at[p]),
            pltpu.make_async_copy(ctrl.at[p], ctrl_here.at[p], ctrl_sems.at[p]),
        )

    for p in range(planes):
        for copy in copies(p):
            copy.start()
    total[...] = jnp.zeros_like(total)
    extra[...] = jnp.zeros_like(extra)

    @pl.loop(0, planes)
    def _(p):
        for copy in copies(p):
            copy.wait()
        rows = rows_split(sense[:, pl.ds(pl.multiple_of(p * obs.shape[1], 128), obs.shape[1])])
        add_products(total, extra, obs_here[p].T, rows, ctrl_here[p])

    in_chunks(total, gram)
    few[...] = extra[:8]


def local_gram(observe, control, sense):
    blocks, rows, rank = observe.shape
    anywhere = pl.BlockSpec(memory_space=pltpu.HBM)
    vmem = pl.BlockSpec(memory_space=pltpu.VMEM)
    return pl.pallas_call(
        gram_kernel,
        in_specs=[anywhere, anywhere, vmem],
        out_specs=[vmem, vmem],
        out_shape=[
            jax.ShapeDtypeStruct((64, 2, 8, rank // 2), F32),
            jax.ShapeDtypeStruct((8, rank), F32),
        ],
        scratch_shapes=[
            pltpu.VMEM((blocks, rows, rank), F32),
            pltpu.VMEM((blocks, rows, rank), F32),
            pltpu.VMEM((rank, rank), F32),
            pltpu.VMEM((16, rank), F32),
            pltpu.SemaphoreType.DMA((blocks,)),
            pltpu.SemaphoreType.DMA((blocks,)),
        ],
        compiler_params=pltpu.CompilerParams(vmem_limit_bytes=60 << 20),
        cost_estimate=pl.CostEstimate(
            flops=6 * blocks * rows * rank * rank, bytes_accessed=18 << 20, transcendentals=0
        ),
        name="local_gram",
    )(observe, control, sense)


def stencil_kernel(
    lines, points,
    obs, conduct, drive, few_ctrl, ctrl, zlow, zhigh, ylow, yhigh,
    out, field, obs_here, total, extra, sems, obs_sems,
):
    steps = obs.shape[0]
    planes = steps // 2
    inner = pl.ds(1, lines)
    copies = [pltpu.make_async_copy(zlow, field.at[0, inner], sems.at[0])]
    for p in range(planes):
        copies.append(pltpu.make_async_copy(ctrl.at[p], field.at[p + 1, inner], sems.at[p + 1]))
    copies.append(pltpu.make_async_copy(zhigh, field.at[planes + 1, inner], sems.at[planes + 1]))
    sides = [
        pltpu.make_async_copy(ylow, field.at[pl.ds(1, planes), 0], sems.at[planes + 2]),
        pltpu.make_async_copy(yhigh, field.at[pl.ds(1, planes), lines + 1], sems.at[planes + 3]),
    ]

    def obs_copy(step):
        return pltpu.make_async_copy(obs.at[step], obs_here.at[step], obs_sems.at[step])

    for copy in copies[:3] + sides:
        copy.start()
    obs_copy(0).start()
    obs_copy(1).start()
    for p in range(1, planes):
        copies[p + 2].start()
        obs_copy(2 * p).start()
        obs_copy(2 * p + 1).start()
    total[...] = jnp.zeros_like(total)
    extra[...] = jnp.zeros_like(extra)
    for copy in copies[:3] + sides:
        copy.wait()

    @pl.loop(0, steps)
    def _(step):
        for p in range(1, planes):

            @pl.when(step == 2 * p)
            def _():
                copies[p + 2].wait()

        obs_copy(step).wait()
        p = step // 2
        half = lines // 2
        line = (step % 2) * half

        def part(plane, first):
            return field[plane, pl.ds(first, half)]

        center = part(p + 1, line + 1)
        beside = part(p + 2, line + 1) + part(p, line + 1)
        beside = beside + part(p + 1, line + 2) + part(p + 1, line)
        rows = half * points
        rank = center.shape[-1]
        center = center.reshape(rows, rank)
        beside = beside.reshape(rows, rank)
        place = lax.broadcasted_iota(jnp.int32, (rows, rank), 0) % points
        beside = beside + jnp.where(place > 0, pltpu.roll(center, 1, 0), 0.0)
        beside = beside + jnp.where(place < points - 1, pltpu.roll(center, rows - 1, 0), 0.0)
        applied = (beside - 6.0 * center).T * (conduct[step] * (1.0 / 6.0))
        some = rows_split(drive[:, pl.ds(pl.multiple_of(step * rows, 128), rows)])
        add_products(total, extra, applied, some, obs_here[step])

    in_chunks(total, out)
    rank = total.shape[1]
    summed = jnp.concatenate([extra[0:4] + extra[4:8], few_ctrl[0:4] + few_ctrl[4:8]], axis=0)
    wide = jnp.concatenate([summed, jnp.zeros((120, rank), F32)], axis=0).T
    out[:, 0, :, rank // 2 :] = wide.reshape(out.shape[0], out.shape[2], 128)
    out[:, 1, :, rank // 2 :] = jnp.zeros((out.shape[0], out.shape[2], 128), F32)


def local_operator(observe, control, conduct, drive, few_ctrl, zlow, zhigh, ylow, yhigh):
    planes, lines, points, rank = control.shape
    steps = 2 * planes
    rows = lines * points // 2
    anywhere = pl.BlockSpec(memory_space=pltpu.HBM)
    vmem = pl.BlockSpec(memory_space=pltpu.VMEM)
    return pl.pallas_call(
        functools.partial(stencil_kernel, lines, points),
        in_specs=[anywhere, vmem, vmem, vmem] + [anywhere] * 5,
        out_specs=vmem,
        out_shape=jax.ShapeDtypeStruct((64, 2, 8, rank // 2 + 128), F32),
        scratch_shapes=[
            pltpu.VMEM((planes + 2, lines + 2, points, rank), F32),
            pltpu.VMEM((steps, rows, rank), F32),
            pltpu.VMEM((rank, rank), F32),
            pltpu.VMEM((16, rank), F32),
            pltpu.SemaphoreType.DMA((planes + 4,)),
            pltpu.SemaphoreType.DMA((steps,)),
        ],
        compiler_params=pltpu.CompilerParams(vmem_limit_bytes=44 << 20),
        cost_estimate=pl.CostEstimate(
            flops=6 * steps * rows * rank * rank, bytes_accessed=24 << 20, transcendentals=0
        ),
        name="local_operator",
    )(
        observe.reshape(steps, rows, rank),
        conduct.reshape(steps, 1, rows),
        drive,
        few_ctrl,
        control,
        zlow.reshape(lines, points, rank),
        zhigh.reshape(lines, points, rank),
        ylow.reshape(planes, points, rank),
        yhigh.reshape(planes, points, rank),
    )


def sum_kernel(parts, out):
    whole = jnp.sum(parts[...], axis=0, keepdims=True)
    out[...] = jnp.broadcast_to(whole, out.shape)


def scattered(parts):
    tiles = parts.reshape(parts.shape[0] * parts.shape[1], *parts.shape[2:])
    return lax.all_to_all(tiles, ALL, 0, 0, tiled=True)


def summed_copies(arrived):
    return pl.pallas_call(
        sum_kernel,
        out_shape=jax.ShapeDtypeStruct(arrived.shape, F32),
        compiler_params=pltpu.CompilerParams(vmem_limit_bytes=6 << 20),
        cost_estimate=pl.CostEstimate(
            flops=arrived.size, bytes_accessed=8 * arrived.size, transcendentals=0
        ),
        name="sum_gram",
    )(arrived)


def project_kernel(side, parts, left, out):
    block = jnp.sum(parts[...], axis=0)
    half = left.shape[1] // 2
    mine = jnp.where(side[0] == 0, left[:, :half], left[:, half:])
    turned = product3(block[:, :half], mine, ((1,), (1,)))
    whole = jnp.concatenate([turned, block[:, half:]], axis=1)
    out[...] = jnp.broadcast_to(whole[None], out.shape)


def projected_copies(arrived, left):
    side = lax.axis_index("sub") & 1
    vmem = pl.BlockSpec(memory_space=pltpu.VMEM)
    return pl.pallas_call(
        project_kernel,
        in_specs=[pl.BlockSpec(memory_space=pltpu.SMEM), vmem, vmem],
        out_specs=vmem,
        out_shape=jax.ShapeDtypeStruct((arrived.shape[0], 8, 256), F32),
        compiler_params=pltpu.CompilerParams(vmem_limit_bytes=8 << 20),
        cost_estimate=pl.CostEstimate(
            flops=arrived.size, bytes_accessed=8 * arrived.size, transcendentals=0
        ),
        name="project",
    )(side.reshape(1).astype(jnp.int32), arrived, left)


def gathered(copies):
    tiles = lax.all_to_all(copies, ALL, 0, 0, tiled=True)
    return tiles.reshape(64, 2, *tiles.shape[1:])


def inverse_factor(work):
    size = work.shape[0]
    for first in range(0, size, PANEL):
        last = first + PANEL
        panel = [work[first + 8 * g : first + 8 * g + 8, :] for g in range(PANEL // 8)]
        groups = PANEL // 8
        columns = {}
        for k in range(PANEL):
            for g in range(k // 8, groups):
                columns[k, g] = jnp.broadcast_to(
                    panel[g][:, first + k : first + k + 1], (8, 128)
                )
        place = lax.broadcasted_iota(jnp.int32, (8, 128), 0)
        for j in range(PANEL):
            gj, sj = divmod(j, 8)
            pivot = jnp.broadcast_to(columns[j, gj][sj : sj + 1], (8, 128))
            scale = lax.rsqrt(pivot)
            lower = {}
            for g in range(gj, groups):
                lower[g] = columns[j, g] * scale
            row = jnp.broadcast_to(panel[gj][sj : sj + 1], (8, 256))
            row = row * jnp.concatenate([scale, scale], axis=1)
            for k in range(j + 1, PANEL):
                gk, sk = divmod(k, 8)
                across = jnp.broadcast_to(lower[gk][sk : sk + 1], (8, 128))
                for g in range(gk, groups):
                    columns[k, g] = columns[k, g] - lower[g] * across
            for g in range(gj, groups):
                weight = lower[g]
                if g == gj:
                    weight = jnp.where(place > sj, weight, 0.0)
                wide = jnp.concatenate([weight, weight], axis=1)
                panel[g] = panel[g] - wide * row
            wide_place = lax.broadcasted_iota(jnp.int32, (8, 256), 0)
            panel[gj] = jnp.where(wide_place == sj, row, panel[gj])
        for g in range(groups):
            work[first + 8 * g : first + 8 * g + 8, :] = panel[g]
        if last < size:
            done = jnp.concatenate(panel, axis=0)
            u0, u1, u2 = split3(done)
            left = jnp.concatenate([u0, u0, u1, u1, u0, u2], axis=0)[:, :size]
            right = jnp.concatenate([u0, u1, u0, u1, u2, u0], axis=0)
            change = product(left, right, ((0,), (0,)))
            work[last:, :] -= change[last:, :]


def bases_kernel(gram, start, right_out, left_out, image_out, cross, basis, work):
    rank = cross.shape[0]
    half = rank // 2
    for side in range(2):
        cross[:, side * half : (side + 1) * half] = gram[:, side].reshape(rank, half)
    basis[...] = start[...].T
    size = basis.shape[0]
    eye = (
        lax.broadcasted_iota(jnp.int32, (size, size), 0)
        == lax.broadcasted_iota(jnp.int32, (size, size), 1)
    ).astype(F32)

    @pl.loop(0, 4)
    def _(turn):
        @pl.when(turn % 2 == 0)
        def _():
            image_out[...] = product3(basis[...], cross[...])

        @pl.when(turn % 2 == 1)
        def _():
            image_out[...] = product3(basis[...], cross[...], ((1,), (1,)))

        held = image_out[...]
        work[:, :size] = product6(held, held, ((1,), (1,)))
        work[:, size:] = eye
        inverse_factor(work)
        basis[...] = product6(work[:, size:], held)

        @pl.when(turn == 2)
        def _():
            right_out[...] = basis[...]

    left_out[...] = basis[...]


def bases(gram, start):
    rank, size = start.shape
    shape = jax.ShapeDtypeStruct((size, rank), F32)
    return pl.pallas_call(
        bases_kernel,
        out_shape=[shape, shape, shape],
        scratch_shapes=[
            pltpu.VMEM((rank, rank), F32),
            pltpu.VMEM((size, rank), F32),
            pltpu.VMEM((size, 2 * size), F32),
        ],
        compiler_params=pltpu.CompilerParams(vmem_limit_bytes=16 << 20),
        cost_estimate=pl.CostEstimate(
            flops=20_000_000_000, bytes_accessed=4 << 20, transcendentals=0
        ),
        name="bases",
    )(gram, start)


def finish_kernel(order, right, left, image, blocks, mass, state, inputs, outputs):
    size, rank = right.shape
    turned = (blocks[:, 0, :, :size] + blocks[:, 1, :, :size]).reshape(rank, size)
    few = blocks[:, 0, :, size:].reshape(rank, 128)
    kept_col = lax.broadcasted_iota(jnp.int32, (size, size), 0) < order[0]
    kept_row = lax.broadcasted_iota(jnp.int32, (size, size), 1) < order[0]
    kept = jnp.logical_and(kept_col, kept_row).astype(F32)
    mass[...] = kept * product6(left[...], image[...], ((1,), (1,)))
    state[...] = kept * product3(right[...], turned).T
    inputs[...] = (kept_row.astype(F32) * product3(left[...], few).T)[:4]
    outputs[...] = (kept_row.astype(F32) * product3(right[...], few).T)[4:8]


def finish(order, right, left, image, blocks):
    size, _ = right.shape
    vmem = pl.BlockSpec(memory_space=pltpu.VMEM)
    return pl.pallas_call(
        finish_kernel,
        in_specs=[pl.BlockSpec(memory_space=pltpu.SMEM)] + [vmem] * 4,
        out_specs=[vmem] * 4,
        out_shape=[
            jax.ShapeDtypeStruct((size, size), F32),
            jax.ShapeDtypeStruct((size, size), F32),
            jax.ShapeDtypeStruct((4, size), F32),
            jax.ShapeDtypeStruct((4, size), F32),
        ],
        compiler_params=pltpu.CompilerParams(vmem_limit_bytes=16 << 20),
        cost_estimate=pl.CostEstimate(
            flops=1_000_000_000, bytes_accessed=4 << 20, transcendentals=0
        ),
        name="finish",
    )(order, right, left, image, blocks)


def from_neighbours(low_face, high_face, axis):
    count = lax.axis_size(axis)
    up = [(i, i + 1) for i in range(count - 1)]
    down = [(b, a) for a, b in up]
    return lax.ppermute(high_face, axis, up), lax.ppermute(low_face, axis, down)


def reduced(factor_obs, factor_ctrl, diffusivity, input_map, output_map, start_block, order):
    planes, lines, points, rank = factor_ctrl.shape
    cells = planes * lines * points
    drive = input_map.reshape(input_map.shape[0], cells)
    sense = output_map.reshape(output_map.shape[0], cells)
    zlow, zhigh = from_neighbours(factor_ctrl[:1], factor_ctrl[-1:], "slab")
    ylow, yhigh = from_neighbours(factor_ctrl[:, :1], factor_ctrl[:, -1:], "sub")
    gram, few_ctrl = local_gram(
        factor_obs.reshape(planes, lines * points, rank),
        factor_ctrl.reshape(planes, lines * points, rank),
        sense,
    )
    gram = summed_copies(scattered(gram))
    gram = gathered(gram)
    oper = local_operator(
        factor_obs, factor_ctrl, diffusivity, drive, few_ctrl, zlow, zhigh, ylow, yhigh
    )
    oper = scattered(oper)
    right, left, image = bases(gram, start_block)
    blocks = gathered(projected_copies(oper, left))
    mass, state, inputs, outputs = finish(order, right, left, image, blocks)
    return mass, state, inputs.T, outputs


def solution(mesh):
    placed = (
        P("slab", "sub", None, None),
        P("slab", "sub", None, None),
        P("slab", "sub"),
        P(None, "slab", "sub"),
        P(None, "slab", "sub"),
        P(),
        P(),
    )
    return jax.shard_map(
        reduced, mesh=mesh, in_specs=placed, out_specs=(P(), P(), P(), P()), check_vma=False
    )
```

time: 167 us -> 139 us (0.83)
  waiting for transfers between devices: 62.8 us -> 43 us
  Pallas kernels: 56.6 us -> 49.4 us
  starting transfers between devices: 44 us -> 37.2 us
  local copies, waits for them, and re-layouts: 1.63 us -> 7.75 us
    ppermute x2, waiting for transfers between devices: 12.2 us -> 0.01 us  [from_neighbours(): lax.ppermute(high_face, axis, up)]
    all_to_all x4, starting transfers between devices: 33 us -> 26 us  [the longest x2 16.1 us: scattered(): return lax.all_to_all(tiles, ALL, 0, 0, tiled=True)]
    pallas_call x6 -> x5, Pallas kernels: 54.9 us -> 48.1 us  [the longest x1 18.6 us: bases(): pl.pallas_call(bases_kernel, out_shape=[shape, shape, shape], scratch_sha...]
    ppermute x2, waiting for transfers between devices: 5.93 us -> 0.01 us  [from_neighbours(): lax.ppermute(low_face, axis, down)]
    slice x0 -> x1, local copies, waits for them, and re-layouts: none -> 4.97 us  [reduced(): zlow, zhigh = from_neighbours(factor_ctrl[:1], factor_ctrl[-1:], 'slab')]
    unnamed x10 -> x17, local copies, waits for them, and re-layouts: 0.95 us -> 2.75 us
    all_to_all x4, waiting for transfers between devices: 44.6 us -> 42.9 us  [the longest x2 23.1 us: gathered(): tiles = lax.all_to_all(copies, ALL, 0, 0, tiled=True)]
  transfers between devices with their start and end apart: 8 -> 8, of which waited for: 6 -> 4; matrix products, arithmetic and copies ran while one was open for 0% -> 1% of each run, Pallas kernels for 25% -> 34%
where the time goes in v1:
time: 139 us
  Pallas kernels  49.4 us (36%)
  waiting for transfers between devices  43 us (31%)
  starting transfers between devices  37.2 us (27%)
  local copies, waits for them, and re-layouts  7.75 us (6%)
  between operations  1.51 us (1%)
    all_to_all x2, waiting for transfers between devices, gathered(): tiles = lax.all_to_all(copies, ALL, 0, 0, tiled=True)  23.1 us
    all_to_all x2, waiting for transfers between devices, scattered(): return lax.all_to_all(tiles, ALL, 0, 0, tiled=True)  19.9 us
    pallas_call x1, Pallas kernels, bases(): pl.pallas_call(bases_kernel, out_shape=[shape, shape, shape], scratch_sha...  18.6 us
    all_to_all x2, starting transfers between devices, scattered(): return lax.all_to_all(tiles, ALL, 0, 0, tiled=True)  16.1 us
    pallas_call x1, Pallas kernels, local_operator(): pl.pallas_call(functools.partial(stencil_kernel, lines, points), in_specs...  15.1 us
    pallas_call x1, Pallas kernels, local_gram(): pl.pallas_call(gram_kernel, in_specs=[anywhere, anywhere, vmem], out_spec...  11.8 us
    all_to_all x2, starting transfers between devices, gathered(): tiles = lax.all_to_all(copies, ALL, 0, 0, tiled=True)  9.86 us
    ppermute x2, starting transfers between devices, from_neighbours(): lax.ppermute(high_face, axis, up)  7.86 us
  transfers between devices with their start and end apart: 8, of which 4 were waited for; matrix products, arithmetic and copies ran while one was open for 1% of the time, Pallas kernels for 34%

profile of v1, /device:TPU:1, one launch (start us, length us, event | category | flops | bytes accessed | tf_op | source)
XLA Modules:
  0.0 138.8 jit_solution(11563666925925883791)
XLA Ops:
  0.6 5.0 %fusion = (f32[1,16,64,512]{3,2,1,0:T(8,128)}, f32[1,16,64,512]{3,2,1,0:T(8,128)}) fusion(f32[4,16,64,512]{3,2,1,0:T(8,128)} %ctrl.1), kind=kLoop, calls=%fused_computation.2 | loop fusion | bytes 8388608 | tf_op jit(solution)/shard_map/slice | solution.py:435
  5.6 4.6 %collective-permute-start = (f32[1,16,64,512]{3,2,1,0:T(8,128)}, f32[1,16,64,512]{3,2,1,0:T(8,128)}, u32[]{:S(2)}, u32[]{:S(2)}) collective-permute-start(f32[1,16,64,512]{3,2,1,0:T(8,128)} %get-tuple-element.25), channel_id=1, source_target_pairs={{0,4},{4,8},{8,12},{12,16},{16,20},{20,24},{24,28},{28,32},{32,36}... | collective-permute-start | bytes 6291464 | tf_op jit(solution)/shard_map/ppermute | solution.py:427
  10.2 1.9 %collective-permute-start.1 = (f32[1,16,64,512]{3,2,1,0:T(8,128)}, f32[1,16,64,512]{3,2,1,0:T(8,128)}, u32[]{:S(2)}, u32[]{:S(2)}) collective-permute-start(f32[1,16,64,512]{3,2,1,0:T(8,128)} %get-tuple-element.24), channel_id=1, source_target_pairs={{4,0},{8,4},{12,8},{16,12},{20,16},{24,20},{28,24},{32,28},{36,32}... | collective-permute-start | bytes 6291464 | tf_op jit(solution)/shard_map/ppermute | solution.py:427
  12.1 0.7 copy.15
  12.8 11.8 %local_gram.1 = (f32[64,2,8,256]{3,2,1,0:T(8,128)}, f32[8,512]{1,0:T(8,128)}) custom-call(f32[4,1024,512]{2,1,0:T(8,128)} %bitcast.31, f32[4,1024,512]{2,1,0:T(8,128)} %bitcast.26, f32[4,4096]{1,0:T(4,128)} %bitcast.30), custom_call_target="tpu_custom_call" | custom-call | flops 6442450944 | bytes 18874368 | tf_op jit(solution)/shard_map/local_gram/pallas_call | solution.py:105
  24.6 10.5 %all-to-all-start = ((f32[128,8,256]{2,1,0:T(8,128)}), f32[128,8,256]{2,1,0:T(8,128)S(1)}, u32[]{:S(2)}, u32[]{:S(2)}) async-start(f32[128,8,256]{2,1,0:T(8,128)} %bitcast.27), calls=%async_computation | async-start | bytes 2097152 | tf_op jit(solution)/shard_map/all_to_all | solution.py:244
  35.2 1.3 slice_bitcast_fusion
  36.5 3.3 %collective-permute-start.2 = (f32[4,1,64,512]{3,2,0,1:T(8,128)S(1)}, f32[4,1,64,512]{3,2,0,1:T(8,128)S(1)}, u32[]{:S(2)}, u32[]{:S(2)}) collective-permute-start(f32[4,1,64,512]{3,2,0,1:T(8,128)S(1)} %get-tuple-element.23), channel_id=1, source_target_pairs={{0,1},{1,2},{2,3},{4,5},{5,6},{6,7},{8,9},{9,10},{10,11},{12,13},{... | collective-permute-start | bytes 1572872 | tf_op jit(solution)/shard_map/ppermute | solution.py:427
  39.8 0.0 copy-start.6
  39.8 0.0 copy-start.5
  39.8 1.4 %collective-permute-start.3 = (f32[4,1,64,512]{3,2,0,1:T(8,128)S(1)}, f32[4,1,64,512]{3,2,0,1:T(8,128)S(1)}, u32[]{:S(2)}, u32[]{:S(2)}) collective-permute-start(f32[4,1,64,512]{3,2,0,1:T(8,128)S(1)} %get-tuple-element.22), channel_id=1, source_target_pairs={{1,0},{2,1},{3,2},{5,4},{6,5},{7,6},{9,8},{10,9},{11,10},{13,12},{... | collective-permute-start | bytes 1572872 | tf_op jit(solution)/shard_map/ppermute | solution.py:427
  41.2 14.0 %all-to-all-done.parts = f32[128,8,256]{2,1,0:T(8,128)S(1)} async-done(((f32[128,8,256]{2,1,0:T(8,128)}), f32[128,8,256]{2,1,0:T(8,128)S(1)}, u32[]{:S(2)}, u32[]{:S(2)}) %all-to-all-start) | async-done | bytes 1048608 | tf_op jit(solution)/shard_map/all_to_all | solution.py:244
  55.3 1.3 sum_gram.1
  56.5 5.9 %all-to-all-start.1 = ((f32[128,8,256]{2,1,0:T(8,128)}), f32[128,8,256]{2,1,0:T(8,128)S(1)}, u32[]{:S(2)}, u32[]{:S(2)}) async-start(f32[128,8,256]{2,1,0:T(8,128)} %sum_gram.1), calls=%async_computation.1 | async-start | bytes 2097152 | tf_op jit(solution)/shard_map/all_to_all | solution.py:285
  62.6 15.1 %local_operator.1 = f32[64,2,8,384]{3,2,1,0:T(8,128)} custom-call(f32[8,512,512]{2,1,0:T(8,128)} %bitcast.32, f32[8,1,512]{2,1,0:T(1,128)S(1)} %reshape.60.conduct, f32[4,4096]{1,0:T(4,128)S(1)} %bitcast.23, f32[8,512]{1,0:T(8,128)S(1)} %copy-done.1, f32[4,16,64,512]{3,2,1,0:T(8,128)} %ctrl.1, f32[16,64,512]{2,1,0:T(8,128)} %bitcast.6.zlow, ...), custom_call_target="tpu_custom_call" | custom-call | flops 6442450944 | bytes 25165824 | tf_op jit(solution)/shard_map/local_operator/pallas_call | solution.py:206
  77.8 4.2 %all-to-all-done.1 = f32[128,8,256]{2,1,0:T(8,128)S(1)} async-done(((f32[128,8,256]{2,1,0:T(8,128)}), f32[128,8,256]{2,1,0:T(8,128)S(1)}, u32[]{:S(2)}, u32[]{:S(2)}) %all-to-all-start.1) | async-done | bytes 1048608 | tf_op jit(solution)/shard_map/all_to_all | solution.py:285
  82.0 5.6 %all-to-all-start.2 = ((f32[128,8,384]{2,1,0:T(8,128)}), f32[128,8,384]{2,1,0:T(8,128)S(1)}, u32[]{:S(2)}, u32[]{:S(2)}) async-start(f32[128,8,384]{2,1,0:T(8,128)} %bitcast.10), calls=%async_computation.2 | async-start | bytes 3145728 | tf_op jit(solution)/shard_map/all_to_all | solution.py:244
  87.6 18.6 %bases.1 = (f32[128,512]{1,0:T(8,128)S(1)}, f32[128,512]{1,0:T(8,128)S(1)}, f32[128,512]{1,0:T(8,128)S(1)}) custom-call(f32[64,2,8,256]{3,2,1,0:T(8,128)S(1)} %bitcast.21, f32[512,128]{1,0:T(8,128)S(1)} %copy-done), custom_call_target="tpu_custom_call" | custom-call | flops 20000000000 | bytes 4194304 | tf_op jit(solution)/shard_map/bases/pallas_call | solution.py:373
  106.2 0.7 copy-done.2
  106.9 5.8 %all-to-all-done.2.parts = f32[128,8,384]{2,1,0:T(8,128)S(1)} async-done(((f32[128,8,384]{2,1,0:T(8,128)}), f32[128,8,384]{2,1,0:T(8,128)S(1)}, u32[]{:S(2)}, u32[]{:S(2)}) %all-to-all-start.2) | async-done | bytes 1572896 | tf_op jit(solution)/shard_map/all_to_all | solution.py:244
  112.7 1.3 project.1
  114.1 3.9 %all-to-all-start.3 = ((f32[128,8,256]{2,1,0:T(8,128)}), f32[128,8,256]{2,1,0:T(8,128)S(1)}, u32[]{:S(2)}, u32[]{:S(2)}) async-start(f32[128,8,256]{2,1,0:T(8,128)} %project.1), calls=%async_computation.3 | async-start | bytes 2097152 | tf_op jit(solution)/shard_map/all_to_all | solution.py:285
  118.6 18.9 %all-to-all-done.3 = f32[128,8,256]{2,1,0:T(8,128)S(1)} async-done(((f32[128,8,256]{2,1,0:T(8,128)}), f32[128,8,256]{2,1,0:T(8,128)S(1)}, u32[]{:S(2)}, u32[]{:S(2)}) %all-to-all-start.3) | async-done | bytes 1048608 | tf_op jit(solution)/shard_map/all_to_all | solution.py:285
  137.5 1.3 finish.1
  (17 shorter events, 0.1 us)
Async XLA Ops:
  0.6 11.5 %copy-start.4 = (f32[4,4,1024]{2,1,0:T(4,128)S(1)}, f32[4,4,1024]{2,1,0:T(4,128)}, u32[]{:S(2)}) copy-start(f32[4,4,1024]{2,1,0:T(4,128)} %param.11) | copy-start | bytes 196612
  5.6 57.0 %collective-permute-start = (f32[1,16,64,512]{3,2,1,0:T(8,128)}, f32[1,16,64,512]{3,2,1,0:T(8,128)}, u32[]{:S(2)}, u32[]{:S(2)}) collective-permute-start(f32[1,16,64,512]{3,2,1,0:T(8,128)} %get-tuple-element.25), channel_id=1, source_target_pairs={{0,4},{4,8},{8,12},{12,16},{16,20},{20,24},{24,28},{28,32},{32,36}... | collective-permute-start | bytes 6291464 | tf_op jit(solution)/shard_map/ppermute | solution.py:427
  10.2 52.4 %collective-permute-start.1 = (f32[1,16,64,512]{3,2,1,0:T(8,128)}, f32[1,16,64,512]{3,2,1,0:T(8,128)}, u32[]{:S(2)}, u32[]{:S(2)}) collective-permute-start(f32[1,16,64,512]{3,2,1,0:T(8,128)} %get-tuple-element.24), channel_id=1, source_target_pairs={{4,0},{8,4},{12,8},{16,12},{20,16},{24,20},{28,24},{32,28},{36,32}... | collective-permute-start | bytes 6291464 | tf_op jit(solution)/shard_map/ppermute | solution.py:427
  24.6 30.6 %all-to-all-start = ((f32[128,8,256]{2,1,0:T(8,128)}), f32[128,8,256]{2,1,0:T(8,128)S(1)}, u32[]{:S(2)}, u32[]{:S(2)}) async-start(f32[128,8,256]{2,1,0:T(8,128)} %bitcast.27), calls=%async_computation | async-start | bytes 2097152 | tf_op jit(solution)/shard_map/all_to_all | solution.py:244
  36.5 26.1 %collective-permute-start.2 = (f32[4,1,64,512]{3,2,0,1:T(8,128)S(1)}, f32[4,1,64,512]{3,2,0,1:T(8,128)S(1)}, u32[]{:S(2)}, u32[]{:S(2)}) collective-permute-start(f32[4,1,64,512]{3,2,0,1:T(8,128)S(1)} %get-tuple-element.23), channel_id=1, source_target_pairs={{0,1},{1,2},{2,3},{4,5},{5,6},{6,7},{8,9},{9,10},{10,11},{12,13},{... | collective-permute-start | bytes 1572872 | tf_op jit(solution)/shard_map/ppermute | solution.py:427
  39.8 22.7 %copy-start.6 = (f32[4,1024]{1,0:T(4,128)S(1)}, f32[4,1024]{1,0:T(4,128)}, u32[]{:S(2)}) copy-start(f32[4,1024]{1,0:T(4,128)} %param.9) | copy-start | bytes 49156
  39.8 22.7 %copy-start.5 = (f32[4,4,1024]{2,1,0:T(4,128)S(1)}, f32[4,4,1024]{2,1,0:T(4,128)}, u32[]{:S(2)}) copy-start(f32[4,4,1024]{2,1,0:T(4,128)} %param.10) | copy-start | bytes 196612
  39.8 22.8 %copy-start.1 = (f32[8,512]{1,0:T(8,128)S(1)}, f32[8,512]{1,0:T(8,128)}, u32[]{:S(2)}) copy-start(f32[8,512]{1,0:T(8,128)} %get-tuple-element.17.few_ctrl) | copy-start | bytes 49156
  39.8 22.8 %collective-permute-start.3 = (f32[4,1,64,512]{3,2,0,1:T(8,128)S(1)}, f32[4,1,64,512]{3,2,0,1:T(8,128)S(1)}, u32[]{:S(2)}, u32[]{:S(2)}) collective-permute-start(f32[4,1,64,512]{3,2,0,1:T(8,128)S(1)} %get-tuple-element.22), channel_id=1, source_target_pairs={{1,0},{2,1},{3,2},{5,4},{6,5},{7,6},{9,8},{10,9},{11,10},{13,12},{... | collective-permute-start | bytes 1572872 | tf_op jit(solution)/shard_map/ppermute | solution.py:427
  56.5 25.5 %all-to-all-start.1 = ((f32[128,8,256]{2,1,0:T(8,128)}), f32[128,8,256]{2,1,0:T(8,128)S(1)}, u32[]{:S(2)}, u32[]{:S(2)}) async-start(f32[128,8,256]{2,1,0:T(8,128)} %sum_gram.1), calls=%async_computation.1 | async-start | bytes 2097152 | tf_op jit(solution)/shard_map/all_to_all | solution.py:285
  77.8 9.8 %copy-start = (f32[512,128]{1,0:T(8,128)S(1)}, f32[512,128]{1,0:T(8,128)}, u32[]{:S(2)}) copy-start(f32[512,128]{1,0:T(8,128)} %start.1) | copy-start | bytes 786436
  82.0 30.7 %all-to-all-start.2 = ((f32[128,8,384]{2,1,0:T(8,128)}), f32[128,8,384]{2,1,0:T(8,128)S(1)}, u32[]{:S(2)}, u32[]{:S(2)}) async-start(f32[128,8,384]{2,1,0:T(8,128)} %bitcast.10), calls=%async_computation.2 | async-start | bytes 3145728 | tf_op jit(solution)/shard_map/all_to_all | solution.py:244
  106.2 0.7 copy-start.2
  112.7 24.8 %copy-start.3 = (f32[128,512]{1,0:T(8,128)S(1)}, f32[128,512]{1,0:T(8,128)}, u32[]{:S(2)}) copy-start(f32[128,512]{1,0:T(8,128)} %copy-done.2) | copy-start | bytes 786436
  114.1 23.5 %all-to-all-start.3 = ((f32[128,8,256]{2,1,0:T(8,128)}), f32[128,8,256]{2,1,0:T(8,128)S(1)}, u32[]{:S(2)}, u32[]{:S(2)}) async-start(f32[128,8,256]{2,1,0:T(8,128)} %project.1), calls=%async_computation.3 | async-start | bytes 2097152 | tf_op jit(solution)/shard_map/all_to_all | solution.py:285

commit v2 on v1

--- a/solution.py
+++ b/solution.py
@@ -12,6 +12,7 @@
 F32 = jnp.float32
 BF16 = jnp.bfloat16
 PANEL = 32
+AHEAD = 3
 
 
 def split2(x):
@@ -52,185 +53,309 @@
     return jnp.concatenate([halves, jnp.zeros_like(halves)], axis=0).astype(BF16)
 
 
-def add_products(total, extra, turned, few, right):
+def add_products(total, turned, right, extra=None, few=None):
     count = turned.shape[0]
     th, tl = split2(turned)
     rh, rl = split2(right)
-    top = jnp.concatenate([th, tl, th], axis=1)
-    bottom = jnp.concatenate([few, jnp.zeros_like(few), few], axis=1)
-    result = product(
-        jnp.concatenate([top, bottom], axis=0), jnp.concatenate([rh, rh, rl], axis=0)
-    )
+    left = jnp.concatenate([th, tl, th], axis=1)
+    if few is not None:
+        bottom = jnp.concatenate([few, jnp.zeros_like(few), few], axis=1)
+        left = jnp.concatenate([left, bottom], axis=0)
+    result = product(left, jnp.concatenate([rh, rh, rl], axis=0))
     total[...] += result[:count]
-    extra[...] += result[count:]
-
-
-def in_chunks(total, out):
+    if few is not None:
+        extra[...] += result[count:]
+
+
+def plane_rows(rows, plane, first, size):
+    chosen = jnp.zeros((rows.shape[0], size), F32)
+    for p in range(rows.shape[1]):
+        chosen = jnp.where(plane == p, rows[:, p, pl.ds(first, size)], chosen)
+    return rows_split(chosen)
+
+
+def gram_kernel(
+    obs, ctrl, sense,
+    gram, few, zlow, zhigh, ylow, yhigh,
+    obs_here, ctrl_here, total, extra, obs_sems, ctrl_sems, z_sems, low_sems, high_sems,
+):
+    steps, rows, _ = obs.shape
+    points = ylow.shape[1]
+
+    def copies(i):
+        return (
+            pltpu.make_async_copy(obs.at[i], obs_here.at[i], obs_sems.at[i]),
+            pltpu.make_async_copy(ctrl.at[i], ctrl_here.at[i], ctrl_sems.at[i]),
+        )
+
+    def z_copy(i):
+        source = ctrl_here.at[i if i < 2 else steps - 4 + i]
+        return pltpu.make_async_copy(source, (zlow if i < 2 else zhigh).at[i % 2], z_sems.at[i])
+
+    def low_copy(p):
+        source = ctrl_here.at[2 * p, pl.ds(0, points)]
+        return pltpu.make_async_copy(source, ylow.at[p], low_sems.at[p])
+
+    def high_copy(p):
+        source = ctrl_here.at[2 * p + 1, pl.ds(rows - points, points)]
+        return pltpu.make_async_copy(source, yhigh.at[p], high_sems.at[p])
+
+    for i in range(AHEAD):
+        for copy in copies(i):
+            copy.start()
+    total[...] = jnp.zeros_like(total)
+    extra[...] = jnp.zeros_like(extra)
+
+    @pl.loop(0, steps)
+    def _(i):
+        for copy in copies(i):
+            copy.wait()
+
+        @pl.when(i + AHEAD < steps)
+        def _():
+            for copy in copies(i + AHEAD):
+                copy.start()
+
+        for j in range(4):
+
+            @pl.when(i == (j if j < 2 else steps - 4 + j))
+            def _():
+                z_copy(j).start()
+
+        @pl.when(i % 2 == 0)
+        def _():
+            low_copy(i // 2).start()
+
+        @pl.when(i % 2 == 1)
+        def _():
+            high_copy(i // 2).start()
+
+        first = pl.multiple_of((i % 2) * rows, 128)
+        some = plane_rows(sense, i // 2, first, rows)
+        add_products(total, obs_here[i].T, ctrl_here[i], extra, some)
+
     width = total.shape[1] // 2
     for side in range(2):
         cols = total[:, side * width : (side + 1) * width]
-        out[:, side, :, :width] = cols.reshape(out.shape[0], out.shape[2], width)
-
-
-def gram_kernel(obs, ctrl, sense, gram, few, obs_here, ctrl_here, total, extra, obs_sems, ctrl_sems):
-    planes = obs.shape[0]
-
-    def copies(p):
-        return (
-            pltpu.make_async_copy(obs.at[p], obs_here.at[p], obs_sems.at[p]),
-            pltpu.make_async_copy(ctrl.at[p], ctrl_here.at[p], ctrl_sems.at[p]),
-        )
-
-    for p in range(planes):
-        for copy in copies(p):
-            copy.start()
-    total[...] = jnp.zeros_like(total)
-    extra[...] = jnp.zeros_like(extra)
-
-    @pl.loop(0, planes)
-    def _(p):
-        for copy in copies(p):
-            copy.wait()
-        rows = rows_split(sense[:, pl.ds(pl.multiple_of(p * obs.shape[1], 128), obs.shape[1])])
-        add_products(total, extra, obs_here[p].T, rows, ctrl_here[p])
-
-    in_chunks(total, gram)
+        gram[:, side] = cols.reshape(gram.shape[0], gram.shape[2], width)
     few[...] = extra[:8]
-
-
-def local_gram(observe, control, sense):
-    blocks, rows, rank = observe.shape
+    for i in range(4):
+        z_copy(i).wait()
+    for p in range(steps // 2):
+        low_copy(p).wait()
+        high_copy(p).wait()
+
+
+def local_gram(observe, control, sense, points):
+    steps, rows, rank = observe.shape
     anywhere = pl.BlockSpec(memory_space=pltpu.HBM)
     vmem = pl.BlockSpec(memory_space=pltpu.VMEM)
+    face = jax.ShapeDtypeStruct((2, rows, rank), F32)
+    edge = jax.ShapeDtypeStruct((steps // 2, points, rank), F32)
     return pl.pallas_call(
         gram_kernel,
         in_specs=[anywhere, anywhere, vmem],
-        out_specs=[vmem, vmem],
+        out_specs=[vmem, vmem] + [anywhere] * 4,
         out_shape=[
             jax.ShapeDtypeStruct((64, 2, 8, rank // 2), F32),
             jax.ShapeDtypeStruct((8, rank), F32),
+            face,
+            face,
+            edge,
+            edge,
         ],
         scratch_shapes=[
-            pltpu.VMEM((blocks, rows, rank), F32),
-            pltpu.VMEM((blocks, rows, rank), F32),
+            pltpu.VMEM((steps, rows, rank), F32),
+            pltpu.VMEM((steps, rows, rank), F32),
             pltpu.VMEM((rank, rank), F32),
             pltpu.VMEM((16, rank), F32),
-            pltpu.SemaphoreType.DMA((blocks,)),
-            pltpu.SemaphoreType.DMA((blocks,)),
-        ],
-        compiler_params=pltpu.CompilerParams(vmem_limit_bytes=60 << 20),
-        cost_estimate=pl.CostEstimate(
-            flops=6 * blocks * rows * rank * rank, bytes_accessed=18 << 20, transcendentals=0
+            pltpu.SemaphoreType.DMA((steps,)),
+            pltpu.SemaphoreType.DMA((steps,)),
+            pltpu.SemaphoreType.DMA((4,)),
+            pltpu.SemaphoreType.DMA((steps // 2,)),
+            pltpu.SemaphoreType.DMA((steps // 2,)),
+        ],
+        compiler_params=pltpu.CompilerParams(vmem_limit_bytes=58 << 20),
+        cost_estimate=pl.CostEstimate(
+            flops=6 * steps * rows * rank * rank, bytes_accessed=24 << 20, transcendentals=0
         ),
         name="local_gram",
     )(observe, control, sense)
 
 
-def stencil_kernel(
+def inner_kernel(
     lines, points,
-    obs, conduct, drive, few_ctrl, ctrl, zlow, zhigh, ylow, yhigh,
-    out, field, obs_here, total, extra, sems, obs_sems,
+    obs, ctrl, conduct, drive, total, extra, field, obs_here, obs_sems, ctrl_sems,
 ):
-    steps = obs.shape[0]
-    planes = steps // 2
+    planes = ctrl.shape[0]
     inner = pl.ds(1, lines)
-    copies = [pltpu.make_async_copy(zlow, field.at[0, inner], sems.at[0])]
-    for p in range(planes):
-        copies.append(pltpu.make_async_copy(ctrl.at[p], field.at[p + 1, inner], sems.at[p + 1]))
-    copies.append(pltpu.make_async_copy(zhigh, field.at[planes + 1, inner], sems.at[planes + 1]))
-    sides = [
-        pltpu.make_async_copy(ylow, field.at[pl.ds(1, planes), 0], sems.at[planes + 2]),
-        pltpu.make_async_copy(yhigh, field.at[pl.ds(1, planes), lines + 1], sems.at[planes + 3]),
-    ]
-
-    def obs_copy(step):
-        return pltpu.make_async_copy(obs.at[step], obs_here.at[step], obs_sems.at[step])
-
-    for copy in copies[:3] + sides:
-        copy.start()
-    obs_copy(0).start()
-    obs_copy(1).start()
-    for p in range(1, planes):
-        copies[p + 2].start()
-        obs_copy(2 * p).start()
-        obs_copy(2 * p + 1).start()
+    rank = total.shape[0]
+
+    def ctrl_copy(p):
+        return pltpu.make_async_copy(ctrl.at[p], field.at[p + 1, inner], ctrl_sems.at[p])
+
+    def obs_copy(p):
+        return pltpu.make_async_copy(obs.at[p], obs_here.at[p], obs_sems.at[p])
+
+    for p in range(2):
+        ctrl_copy(p).start()
+        obs_copy(p).start()
     total[...] = jnp.zeros_like(total)
     extra[...] = jnp.zeros_like(extra)
-    for copy in copies[:3] + sides:
-        copy.wait()
-
-    @pl.loop(0, steps)
-    def _(step):
-        for p in range(1, planes):
-
-            @pl.when(step == 2 * p)
-            def _():
-                copies[p + 2].wait()
-
-        obs_copy(step).wait()
-        p = step // 2
+    empty = jnp.zeros((points, rank), F32)
+    for p in range(planes):
+        field[p + 1, 0] = empty
+        field[p + 1, lines + 1] = empty
+    for line in range(1, lines + 1):
+        field[0, line] = empty
+        field[planes + 1, line] = empty
+    ctrl_copy(0).wait()
+
+    @pl.loop(0, planes)
+    def _(p):
+        @pl.when(p + 1 < planes)
+        def _():
+            ctrl_copy(p + 1).wait()
+
+        @pl.when(p + 2 < planes)
+        def _():
+            ctrl_copy(p + 2).start()
+            obs_copy(p + 2).start()
+
+        obs_copy(p).wait()
         half = lines // 2
-        line = (step % 2) * half
-
-        def part(plane, first):
-            return field[plane, pl.ds(first, half)]
-
-        center = part(p + 1, line + 1)
-        beside = part(p + 2, line + 1) + part(p, line + 1)
-        beside = beside + part(p + 1, line + 2) + part(p + 1, line)
         rows = half * points
-        rank = center.shape[-1]
-        center = center.reshape(rows, rank)
-        beside = beside.reshape(rows, rank)
-        place = lax.broadcasted_iota(jnp.int32, (rows, rank), 0) % points
-        beside = beside + jnp.where(place > 0, pltpu.roll(center, 1, 0), 0.0)
-        beside = beside + jnp.where(place < points - 1, pltpu.roll(center, rows - 1, 0), 0.0)
-        applied = (beside - 6.0 * center).T * (conduct[step] * (1.0 / 6.0))
-        some = rows_split(drive[:, pl.ds(pl.multiple_of(step * rows, 128), rows)])
-        add_products(total, extra, applied, some, obs_here[step])
-
-    in_chunks(total, out)
-    rank = total.shape[1]
+        for line in (0, half):
+
+            def part(plane, first):
+                return field[plane, first : first + half]
+
+            center = part(p + 1, line + 1)
+            beside = part(p + 2, line + 1) + part(p, line + 1)
+            beside = beside + part(p + 1, line + 2) + part(p + 1, line)
+            center = center.reshape(rows, rank)
+            beside = beside.reshape(rows, rank)
+            place = lax.broadcasted_iota(jnp.int32, (rows, rank), 0) % points
+            beside = beside + jnp.where(place > 0, pltpu.roll(center, 1, 0), 0.0)
+            beside = beside + jnp.where(place < points - 1, pltpu.roll(center, rows - 1, 0), 0.0)
+            first = line * points
+            scale = conduct[p][:, first : first + rows] * (1.0 / 6.0)
+            applied = (beside - 6.0 * center).T * scale
+            some = plane_rows(drive, p, first, rows)
+            add_products(total, applied, obs_here[p, first : first + rows], extra, some)
+
+
+def inner_operator(observe, control, conduct, drive):
+    planes, lines, points, rank = control.shape
+    cells = lines * points
+    anywhere = pl.BlockSpec(memory_space=pltpu.HBM)
+    vmem = pl.BlockSpec(memory_space=pltpu.VMEM)
+    return pl.pallas_call(
+        functools.partial(inner_kernel, lines, points),
+        in_specs=[anywhere, anywhere, vmem, vmem],
+        out_specs=[vmem, vmem],
+        out_shape=[
+            jax.ShapeDtypeStruct((rank, rank), F32),
+            jax.ShapeDtypeStruct((16, rank), F32),
+        ],
+        scratch_shapes=[
+            pltpu.VMEM((planes + 2, lines + 2, points, rank), F32),
+            pltpu.VMEM((planes, cells, rank), F32),
+            pltpu.SemaphoreType.DMA((planes,)),
+            pltpu.SemaphoreType.DMA((planes,)),
+        ],
+        compiler_params=pltpu.CompilerParams(vmem_limit_bytes=58 << 20),
+        cost_estimate=pl.CostEstimate(
+            flops=6 * planes * cells * rank * rank, bytes_accessed=18 << 20, transcendentals=0
+        ),
+        name="inner_operator",
+    )(observe.reshape(planes, cells, rank), control, conduct.reshape(planes, 1, cells), drive)
+
+
+def outer_kernel(
+    obs, zlow, zhigh, ylow, yhigh, z_conduct, y_conduct, inner, extra, few_ctrl,
+    out, z_field, z_obs, y_field, y_obs, total, sems,
+):
+    planes, lines, points, rank = obs.shape
+
+    def copies(i):
+        if i < 2:
+            plane = (planes - 1) * i
+            return (
+                pltpu.make_async_copy((zhigh if i else zlow), z_field.at[i], sems.at[2 * i]),
+                pltpu.make_async_copy(obs.at[plane], z_obs.at[i], sems.at[2 * i + 1]),
+            )
+        line = (lines - 1) * (i - 2)
+        place = pl.ds(planes * (i - 2), planes)
+        return (
+            pltpu.make_async_copy((yhigh if i == 3 else ylow), y_field.at[place], sems.at[2 * i]),
+            pltpu.make_async_copy(obs.at[:, line], y_obs.at[place], sems.at[2 * i + 1]),
+        )
+
+    for i in (2, 3, 0, 1):
+        for copy in copies(i):
+            copy.start()
+    total[...] = inner[...]
+    for i in (2, 3):
+        for copy in copies(i):
+            copy.wait()
+    rows = 2 * planes * points
+    applied = y_field[...].reshape(rows, rank).T * (y_conduct[...] * (1.0 / 6.0))
+    add_products(total, applied, y_obs[...].reshape(rows, rank))
+    for i in range(2):
+        for copy in copies(i):
+            copy.wait()
+        rows = lines * points
+        applied = z_field[i].reshape(rows, rank).T * (z_conduct[i] * (1.0 / 6.0))
+        add_products(total, applied, z_obs[i].reshape(rows, rank))
+
+    width = rank // 2
+    for side in range(2):
+        cols = total[:, side * width : (side + 1) * width]
+        out[:, side, :, :width] = cols.reshape(out.shape[0], out.shape[2], width)
     summed = jnp.concatenate([extra[0:4] + extra[4:8], few_ctrl[0:4] + few_ctrl[4:8]], axis=0)
     wide = jnp.concatenate([summed, jnp.zeros((120, rank), F32)], axis=0).T
-    out[:, 0, :, rank // 2 :] = wide.reshape(out.shape[0], out.shape[2], 128)
-    out[:, 1, :, rank // 2 :] = jnp.zeros((out.shape[0], out.shape[2], 128), F32)
-
-
-def local_operator(observe, control, conduct, drive, few_ctrl, zlow, zhigh, ylow, yhigh):
-    planes, lines, points, rank = control.shape
-    steps = 2 * planes
-    rows = lines * points // 2
+    out[:, 0, :, width:] = wide.reshape(out.shape[0], out.shape[2], 128)
+    out[:, 1, :, width:] = jnp.zeros((out.shape[0], out.shape[2], 128), F32)
+
+
+def with_outer(observe, faces, conduct, inner, extra, few_ctrl):
+    planes, lines, points, rank = observe.shape
+    zlow, zhigh, ylow, yhigh = faces
+    cells = lines * points
+    z_conduct = jnp.stack([conduct[0], conduct[-1]]).reshape(2, 1, cells)
+    y_conduct = jnp.stack([conduct[:, :points], conduct[:, cells - points :]])
     anywhere = pl.BlockSpec(memory_space=pltpu.HBM)
     vmem = pl.BlockSpec(memory_space=pltpu.VMEM)
     return pl.pallas_call(
-        functools.partial(stencil_kernel, lines, points),
-        in_specs=[anywhere, vmem, vmem, vmem] + [anywhere] * 5,
+        outer_kernel,
+        in_specs=[anywhere] * 5 + [vmem] * 5,
         out_specs=vmem,
         out_shape=jax.ShapeDtypeStruct((64, 2, 8, rank // 2 + 128), F32),
         scratch_shapes=[
-            pltpu.VMEM((planes + 2, lines + 2, points, rank), F32),
-            pltpu.VMEM((steps, rows, rank), F32),
+            pltpu.VMEM((2, lines, points, rank), F32),
+            pltpu.VMEM((2, lines, points, rank), F32),
+            pltpu.VMEM((2 * planes, points, rank), F32),
+            pltpu.VMEM((2 * planes, points, rank), F32),
             pltpu.VMEM((rank, rank), F32),
-            pltpu.VMEM((16, rank), F32),
-            pltpu.SemaphoreType.DMA((planes + 4,)),
-            pltpu.SemaphoreType.DMA((steps,)),
-        ],
-        compiler_params=pltpu.CompilerParams(vmem_limit_bytes=44 << 20),
-        cost_estimate=pl.CostEstimate(
-            flops=6 * steps * rows * rank * rank, bytes_accessed=24 << 20, transcendentals=0
-        ),
-        name="local_operator",
+            pltpu.SemaphoreType.DMA((8,)),
+        ],
+        compiler_params=pltpu.CompilerParams(vmem_limit_bytes=58 << 20),
+        cost_estimate=pl.CostEstimate(
+            flops=15 * cells * rank * rank, bytes_accessed=14 << 20, transcendentals=0
+        ),
+        name="outer_operator",
     )(
-        observe.reshape(steps, rows, rank),
-        conduct.reshape(steps, 1, rows),
-        drive,
-        few_ctrl,
-        control,
+        observe,
         zlow.reshape(lines, points, rank),
         zhigh.reshape(lines, points, rank),
-        ylow.reshape(planes, points, rank),
-        yhigh.reshape(planes, points, rank),
+        ylow,
+        yhigh,
+        z_conduct,
+        y_conduct.reshape(1, 2 * planes * points),
+        inner,
+        extra,
+        few_ctrl,
     )
 
 
@@ -429,21 +554,16 @@
 
 def reduced(factor_obs, factor_ctrl, diffusivity, input_map, output_map, start_block, order):
     planes, lines, points, rank = factor_ctrl.shape
-    cells = planes * lines * points
-    drive = input_map.reshape(input_map.shape[0], cells)
-    sense = output_map.reshape(output_map.shape[0], cells)
-    zlow, zhigh = from_neighbours(factor_ctrl[:1], factor_ctrl[-1:], "slab")
-    ylow, yhigh = from_neighbours(factor_ctrl[:, :1], factor_ctrl[:, -1:], "sub")
-    gram, few_ctrl = local_gram(
-        factor_obs.reshape(planes, lines * points, rank),
-        factor_ctrl.reshape(planes, lines * points, rank),
-        sense,
+    halves = (2 * planes, lines * points // 2, rank)
+    gram, few_ctrl, zlow, zhigh, ylow, yhigh = local_gram(
+        factor_obs.reshape(halves), factor_ctrl.reshape(halves), output_map, points
     )
-    gram = summed_copies(scattered(gram))
-    gram = gathered(gram)
-    oper = local_operator(
-        factor_obs, factor_ctrl, diffusivity, drive, few_ctrl, zlow, zhigh, ylow, yhigh
-    )
+    arrived = scattered(gram)
+    zlow, zhigh = from_neighbours(zlow, zhigh, "slab")
+    ylow, yhigh = from_neighbours(ylow, yhigh, "sub")
+    inner, extra = inner_operator(factor_obs, factor_ctrl, diffusivity, input_map)
+    gram = gathered(summed_copies(arrived))
+    oper = with_outer(factor_obs, (zlow, zhigh, ylow, yhigh), diffusivity, inner, extra, few_ctrl)
     oper = scattered(oper)
     right, left, image = bases(gram, start_block)
     blocks = gathered(projected_copies(oper, left))

time: 139 us -> 157 us (1.13)
  Pallas kernels: 49.4 us -> 58.1 us
  starting transfers between devices: 37.2 us -> 45 us
  waiting for transfers between devices: 43 us -> 47.5 us
  local copies, waits for them, and re-layouts: 7.75 us -> 3.99 us
    all_to_all x2, waiting for transfers between devices: 19.9 us -> 28.6 us  [scattered(): return lax.all_to_all(tiles, ALL, 0, 0, tiled=True)]
    pallas_call x1 -> x2, Pallas kernels: 15.1 us -> 23.3 us  [the longest x1 14.4 us: inner_operator(): pl.pallas_call(functools.partial(inner_kernel, lines, points), in_specs=[...]
    slice x1, local copies, waits for them, and re-layouts: 4.97 us -> 0.01 us  [with_outer(): z_conduct = jnp.stack([conduct[0], conduct[-1]]).reshape(2, 1, cells)]
    all_to_all x2, starting transfers between devices: 16.1 us -> 20.3 us  [scattered(): return lax.all_to_all(tiles, ALL, 0, 0, tiled=True)]
    all_to_all x2, waiting for transfers between devices: 23.1 us -> 18.9 us  [gathered(): tiles = lax.all_to_all(copies, ALL, 0, 0, tiled=True)]
    all_to_all x2, starting transfers between devices: 9.86 us -> 12.8 us  [gathered(): tiles = lax.all_to_all(copies, ALL, 0, 0, tiled=True)]
    reshape x1 -> x3, local copies, waits for them, and re-layouts: 0.03 us -> 1.87 us  [the longest x1 0.66 us: with_outer(): y_conduct.reshape(1, 2 * planes * points)]
  transfers between devices with their start and end apart: 8 -> 8, of which waited for: 4 -> 3; matrix products, arithmetic and copies ran while one was open for 1% -> 1% of each run, Pallas kernels for 34% -> 28%
where the time goes in v2:
time: 157 us; the launch traced here: 156 us
  Pallas kernels  58.1 us (37%)
  waiting for transfers between devices  47.5 us (30%)
  starting transfers between devices  45 us (29%)
  local copies, waits for them, and re-layouts  3.99 us (3%)
    all_to_all x2, waiting for transfers between devices, scattered(): return lax.all_to_all(tiles, ALL, 0, 0, tiled=True)  28.6 us
    all_to_all x2, starting transfers between devices, scattered(): return lax.all_to_all(tiles, ALL, 0, 0, tiled=True)  20.3 us
    all_to_all x2, waiting for transfers between devices, gathered(): tiles = lax.all_to_all(copies, ALL, 0, 0, tiled=True)  18.9 us
    pallas_call x1, Pallas kernels, bases(): pl.pallas_call(bases_kernel, out_shape=[shape, shape, shape], scratch_sha...  18.6 us
    pallas_call x1, Pallas kernels, inner_operator(): pl.pallas_call(functools.partial(inner_kernel, lines, points), in_specs=[...  14.4 us
    all_to_all x2, starting transfers between devices, gathered(): tiles = lax.all_to_all(copies, ALL, 0, 0, tiled=True)  12.8 us
    pallas_call x1, Pallas kernels, local_gram(): pl.pallas_call(gram_kernel, in_specs=[anywhere, anywhere, vmem], out_spec...  12.3 us
    pallas_call x1, Pallas kernels, with_outer(): pl.pallas_call(outer_kernel, in_specs=[anywhere] * 5 + [vmem] * 5, out_sp...  8.92 us
  transfers between devices with their start and end apart: 8, of which 3 were waited for; matrix products, arithmetic and copies ran while one was open for 1% of the time, Pallas kernels for 28%

profile of v2, /device:TPU:1, one launch (start us, length us, event | category | flops | bytes accessed | tf_op | source)
XLA Modules:
  0.0 156.2 jit_solution(3174120456524683001)
XLA Ops:
  0.6 12.3 %local_gram.1 = (f32[64,2,8,256]{3,2,1,0:T(8,128)}, f32[8,512]{1,0:T(8,128)}, f32[2,512,512]{2,1,0:T(8,128)}, f32[2,512,512]{2,1,0:T(8,128)}, f32[4,64,512]{2,1,0:T(8,128)}, /*index=5*/f32[4,64,512]{2,1,0:T(8,128)}) custom-call(f32[8,512,512]{2,1,0:T(8,128)} %bitcast.17, f32[8,512,512]{2,1,0:T(8,128)} %bitcast.22, f32[4,4,1024]{2,1,0:T(4,128)} %sense.1), custom_call_target="tpu_custom_call" | custom-call | flops 6442450944 | bytes 25165824 | tf_op jit(solution)/shard_map/local_gram/pallas_call | solution.py:155
  13.0 4.6 %collective-permute-start = (f32[2,512,512]{2,1,0:T(8,128)}, f32[2,512,512]{2,1,0:T(8,128)S(1)}, u32[]{:S(2)}, u32[]{:S(2)}) collective-permute-start(f32[2,512,512]{2,1,0:T(8,128)} %get-tuple-element.23), channel_id=1, source_target_pairs={{0,4},{4,8},{8,12},{12,16},{16,20},{20,24},{24,28},{28,32},{32,36}... | collective-permute-start | bytes 6291464 | tf_op jit(solution)/shard_map/ppermute | solution.py:552
  17.6 1.9 %collective-permute-start.1 = (f32[2,512,512]{2,1,0:T(8,128)}, f32[2,512,512]{2,1,0:T(8,128)}, u32[]{:S(2)}, u32[]{:S(2)}) collective-permute-start(f32[2,512,512]{2,1,0:T(8,128)} %get-tuple-element.24), channel_id=1, source_target_pairs={{4,0},{8,4},{12,8},{16,12},{20,16},{24,20},{28,24},{32,28},{36,32}... | collective-permute-start | bytes 6291464 | tf_op jit(solution)/shard_map/ppermute | solution.py:552
  19.5 10.6 %all-to-all-start = ((f32[128,8,256]{2,1,0:T(8,128)}), f32[128,8,256]{2,1,0:T(8,128)S(1)}, u32[]{:S(2)}, u32[]{:S(2)}) async-start(f32[128,8,256]{2,1,0:T(8,128)} %bitcast.21), calls=%async_computation | async-start | bytes 2097152 | tf_op jit(solution)/shard_map/all_to_all | solution.py:369
  30.1 4.1 %collective-permute-start.2 = (f32[4,64,512]{2,1,0:T(8,128)}, f32[4,64,512]{2,1,0:T(8,128)}, u32[]{:S(2)}, u32[]{:S(2)}) collective-permute-start(f32[4,64,512]{2,1,0:T(8,128)} %get-tuple-element.25), channel_id=1, source_target_pairs={{0,1},{1,2},{2,3},{4,5},{5,6},{6,7},{8,9},{9,10},{10,11},{12,13},{... | collective-permute-start | bytes 1572872 | tf_op jit(solution)/shard_map/ppermute | solution.py:552
  34.2 1.3 collective-permute-start.3
  35.5 0.6 reshape.57.conduct
  36.1 0.6 reshape.54.z_conduct
  36.7 0.1 slice_bitcast_fusion.1
  36.8 22.8 %all-to-all-done.parts = f32[128,8,256]{2,1,0:T(8,128)S(1)} async-done(((f32[128,8,256]{2,1,0:T(8,128)}), f32[128,8,256]{2,1,0:T(8,128)S(1)}, u32[]{:S(2)}, u32[]{:S(2)}) %all-to-all-start) | async-done | bytes 1048608 | tf_op jit(solution)/shard_map/all_to_all | solution.py:369
  59.6 1.2 sum_gram.1
  60.8 8.9 %all-to-all-start.1 = ((f32[128,8,256]{2,1,0:T(8,128)}), f32[128,8,256]{2,1,0:T(8,128)S(1)}, u32[]{:S(2)}, u32[]{:S(2)}) async-start(f32[128,8,256]{2,1,0:T(8,128)} %sum_gram.1), calls=%async_computation.1 | async-start | bytes 2097152 | tf_op jit(solution)/shard_map/all_to_all | solution.py:410
  69.7 0.7 reshape.55.y_conduct
  70.4 14.4 %inner_operator.1 = (f32[512,512]{1,0:T(8,128)}, f32[16,512]{1,0:T(8,128)}) custom-call(f32[4,1024,512]{2,1,0:T(8,128)} %bitcast.18, f32[4,16,64,512]{3,2,1,0:T(8,128)} %ctrl.1, f32[4,1,1024]{2,1,0:T(1,128)} %reshape.57.conduct, f32[4,4,1024]{2,1,0:T(4,128)} %drive.1), custom_call_target="tpu_custom_call" | custom-call | flops 6442450944 | bytes 18874368 | tf_op jit(solution)/shard_map/inner_operator/pallas_call | solution.py:253
  84.8 1.3 copy-done.3
  86.2 8.9 %outer_operator.1 = f32[64,2,8,384]{3,2,1,0:T(8,128)} custom-call(f32[4,16,64,512]{3,2,1,0:T(8,128)} %obs.1, f32[16,64,512]{2,1,0:T(8,128)} %bitcast.20, f32[16,64,512]{2,1,0:T(8,128)} %bitcast.6.zhigh, f32[4,64,512]{2,1,0:T(8,128)} %collective-permute-done.2.ylow, f32[4,64,512]{2,1,0:T(8,128)} %collective-permute-done.3.yhigh, ...), custom_call_target="tpu_custom_call" | custom-call | flops 4026531840 | bytes 14680064 | tf_op jit(solution)/shard_map/outer_operator/pallas_call | solution.py:330
  95.1 9.8 %all-to-all-start.2 = ((f32[128,8,384]{2,1,0:T(8,128)}), f32[128,8,384]{2,1,0:T(8,128)S(1)}, u32[]{:S(2)}, u32[]{:S(2)}) async-start(f32[128,8,384]{2,1,0:T(8,128)} %bitcast.19), calls=%async_computation.2 | async-start | bytes 3145728 | tf_op jit(solution)/shard_map/all_to_all | solution.py:369
  104.9 18.6 %bases.1 = (f32[128,512]{1,0:T(8,128)S(1)}, f32[128,512]{1,0:T(8,128)S(1)}, f32[128,512]{1,0:T(8,128)S(1)}) custom-call(f32[64,2,8,256]{3,2,1,0:T(8,128)S(1)} %bitcast.15, f32[512,128]{1,0:T(8,128)S(1)} %copy-done), custom_call_target="tpu_custom_call" | custom-call | flops 20000000000 | bytes 4194304 | tf_op jit(solution)/shard_map/bases/pallas_call | solution.py:498
  123.5 0.7 copy-done.1
  124.2 5.8 %all-to-all-done.2.parts = f32[128,8,384]{2,1,0:T(8,128)S(1)} async-done(((f32[128,8,384]{2,1,0:T(8,128)}), f32[128,8,384]{2,1,0:T(8,128)S(1)}, u32[]{:S(2)}, u32[]{:S(2)}) %all-to-all-start.2) | async-done | bytes 1572896 | tf_op jit(solution)/shard_map/all_to_all | solution.py:369
  130.0 1.3 project.1
  131.4 3.9 %all-to-all-start.3 = ((f32[128,8,256]{2,1,0:T(8,128)}), f32[128,8,256]{2,1,0:T(8,128)S(1)}, u32[]{:S(2)}, u32[]{:S(2)}) async-start(f32[128,8,256]{2,1,0:T(8,128)} %project.1), calls=%async_computation.3 | async-start | bytes 2097152 | tf_op jit(solution)/shard_map/all_to_all | solution.py:410
  136.0 18.9 %all-to-all-done.3 = f32[128,8,256]{2,1,0:T(8,128)S(1)} async-done(((f32[128,8,256]{2,1,0:T(8,128)}), f32[128,8,256]{2,1,0:T(8,128)S(1)}, u32[]{:S(2)}, u32[]{:S(2)}) %all-to-all-start.3) | async-done | bytes 1048608 | tf_op jit(solution)/shard_map/all_to_all | solution.py:410
  154.8 1.3 finish.1
  (16 shorter events, 0.1 us)
Async XLA Ops:
  13.0 22.5 %copy-start.4 = (f32[4,1024]{1,0:T(4,128)S(1)}, f32[4,1024]{1,0:T(4,128)}, u32[]{:S(2)}) copy-start(f32[4,1024]{1,0:T(4,128)} %param.9) | copy-start | bytes 49156
  13.0 71.8 %collective-permute-start = (f32[2,512,512]{2,1,0:T(8,128)}, f32[2,512,512]{2,1,0:T(8,128)S(1)}, u32[]{:S(2)}, u32[]{:S(2)}) collective-permute-start(f32[2,512,512]{2,1,0:T(8,128)} %get-tuple-element.23), channel_id=1, source_target_pairs={{0,4},{4,8},{8,12},{12,16},{16,20},{20,24},{24,28},{28,32},{32,36}... | collective-permute-start | bytes 6291464 | tf_op jit(solution)/shard_map/ppermute | solution.py:552
  17.6 67.3 %collective-permute-start.1 = (f32[2,512,512]{2,1,0:T(8,128)}, f32[2,512,512]{2,1,0:T(8,128)}, u32[]{:S(2)}, u32[]{:S(2)}) collective-permute-start(f32[2,512,512]{2,1,0:T(8,128)} %get-tuple-element.24), channel_id=1, source_target_pairs={{4,0},{8,4},{12,8},{16,12},{20,16},{24,20},{28,24},{32,28},{36,32}... | collective-permute-start | bytes 6291464 | tf_op jit(solution)/shard_map/ppermute | solution.py:552
  19.5 40.1 %all-to-all-start = ((f32[128,8,256]{2,1,0:T(8,128)}), f32[128,8,256]{2,1,0:T(8,128)S(1)}, u32[]{:S(2)}, u32[]{:S(2)}) async-start(f32[128,8,256]{2,1,0:T(8,128)} %bitcast.21), calls=%async_computation | async-start | bytes 2097152 | tf_op jit(solution)/shard_map/all_to_all | solution.py:369
  30.1 54.7 %collective-permute-start.2 = (f32[4,64,512]{2,1,0:T(8,128)}, f32[4,64,512]{2,1,0:T(8,128)}, u32[]{:S(2)}, u32[]{:S(2)}) collective-permute-start(f32[4,64,512]{2,1,0:T(8,128)} %get-tuple-element.25), channel_id=1, source_target_pairs={{0,1},{1,2},{2,3},{4,5},{5,6},{6,7},{8,9},{9,10},{10,11},{12,13},{... | collective-permute-start | bytes 1572872 | tf_op jit(solution)/shard_map/ppermute | solution.py:552
  34.2 50.6 %collective-permute-start.3 = (f32[4,64,512]{2,1,0:T(8,128)}, f32[4,64,512]{2,1,0:T(8,128)}, u32[]{:S(2)}, u32[]{:S(2)}) collective-permute-start(f32[4,64,512]{2,1,0:T(8,128)} %get-tuple-element.26), channel_id=1, source_target_pairs={{1,0},{2,1},{3,2},{5,4},{6,5},{7,6},{9,8},{10,9},{11,10},{13,12},{... | collective-permute-start | bytes 1572872 | tf_op jit(solution)/shard_map/ppermute | solution.py:552
  60.8 34.3 %all-to-all-start.1 = ((f32[128,8,256]{2,1,0:T(8,128)}), f32[128,8,256]{2,1,0:T(8,128)S(1)}, u32[]{:S(2)}, u32[]{:S(2)}) async-start(f32[128,8,256]{2,1,0:T(8,128)} %sum_gram.1), calls=%async_computation.1 | async-start | bytes 2097152 | tf_op jit(solution)/shard_map/all_to_all | solution.py:410
  84.8 1.3 copy-start.3
  95.1 9.8 %copy-start = (f32[512,128]{1,0:T(8,128)S(1)}, f32[512,128]{1,0:T(8,128)}, u32[]{:S(2)}) copy-start(f32[512,128]{1,0:T(8,128)} %start.1) | copy-start | bytes 786436
  95.1 34.9 %all-to-all-start.2 = ((f32[128,8,384]{2,1,0:T(8,128)}), f32[128,8,384]{2,1,0:T(8,128)S(1)}, u32[]{:S(2)}, u32[]{:S(2)}) async-start(f32[128,8,384]{2,1,0:T(8,128)} %bitcast.19), calls=%async_computation.2 | async-start | bytes 3145728 | tf_op jit(solution)/shard_map/all_to_all | solution.py:369
  123.5 0.7 copy-start.1
  130.0 24.8 %copy-start.2 = (f32[128,512]{1,0:T(8,128)S(1)}, f32[128,512]{1,0:T(8,128)}, u32[]{:S(2)}) copy-start(f32[128,512]{1,0:T(8,128)} %copy-done.1) | copy-start | bytes 786436
  131.4 23.5 %all-to-all-start.3 = ((f32[128,8,256]{2,1,0:T(8,128)}), f32[128,8,256]{2,1,0:T(8,128)S(1)}, u32[]{:S(2)}, u32[]{:S(2)}) async-start(f32[128,8,256]{2,1,0:T(8,128)} %project.1), calls=%async_computation.3 | async-start | bytes 2097152 | tf_op jit(solution)/shard_map/all_to_all | solution.py:410

commit v3 on v2

--- a/solution.py
+++ b/solution.py
@@ -12,7 +12,7 @@
 F32 = jnp.float32
 BF16 = jnp.bfloat16
 PANEL = 32
-AHEAD = 3
+AHEAD = 2
 
 
 def split2(x):
@@ -74,10 +74,14 @@
     return rows_split(chosen)
 
 
+def in_hbm(value):
+    return pltpu.with_memory_space_constraint(value, pltpu.HBM)
+
+
 def gram_kernel(
     obs, ctrl, sense,
-    gram, few, zlow, zhigh, ylow, yhigh,
-    obs_here, ctrl_here, total, extra, obs_sems, ctrl_sems, z_sems, low_sems, high_sems,
+    gram, few_far, zlow, zhigh, ylow, yhigh,
+    obs_here, ctrl_here, total, extra, sense_here, obs_sems, ctrl_sems, z_sems, low_sems, high_sems, other_sems,
 ):
     steps, rows, _ = obs.shape
     points = ylow.shape[1]
@@ -100,11 +104,15 @@
         source = ctrl_here.at[2 * p + 1, pl.ds(rows - points, points)]
         return pltpu.make_async_copy(source, yhigh.at[p], high_sems.at[p])
 
+    sense_copy = pltpu.make_async_copy(sense, sense_here, other_sems.at[0])
     for i in range(AHEAD):
         for copy in copies(i):
             copy.start()
+        if i == 0:
+            sense_copy.start()
     total[...] = jnp.zeros_like(total)
     extra[...] = jnp.zeros_like(extra)
+    sense_copy.wait()
 
     @pl.loop(0, steps)
     def _(i):
@@ -131,14 +139,16 @@
             high_copy(i // 2).start()
 
         first = pl.multiple_of((i % 2) * rows, 128)
-        some = plane_rows(sense, i // 2, first, rows)
+        some = plane_rows(sense_here, i // 2, first, rows)
         add_products(total, obs_here[i].T, ctrl_here[i], extra, some)
 
+    few_copy = pltpu.make_async_copy(extra, few_far, other_sems.at[0])
+    few_copy.start()
     width = total.shape[1] // 2
     for side in range(2):
         cols = total[:, side * width : (side + 1) * width]
         gram[:, side] = cols.reshape(gram.shape[0], gram.shape[2], width)
-    few[...] = extra[:8]
+    few_copy.wait()
     for i in range(4):
         z_copy(i).wait()
     for p in range(steps // 2):
@@ -150,15 +160,15 @@
     steps, rows, rank = observe.shape
     anywhere = pl.BlockSpec(memory_space=pltpu.HBM)
     vmem = pl.BlockSpec(memory_space=pltpu.VMEM)
-    face = jax.ShapeDtypeStruct((2, rows, rank), F32)
-    edge = jax.ShapeDtypeStruct((steps // 2, points, rank), F32)
+    face = pltpu.HBM((2, rows, rank), F32)
+    edge = pltpu.HBM((steps // 2, points, rank), F32)
     return pl.pallas_call(
         gram_kernel,
-        in_specs=[anywhere, anywhere, vmem],
-        out_specs=[vmem, vmem] + [anywhere] * 4,
+        in_specs=[anywhere] * 3,
+        out_specs=[vmem] + [anywhere] * 5,
         out_shape=[
             jax.ShapeDtypeStruct((64, 2, 8, rank // 2), F32),
-            jax.ShapeDtypeStruct((8, rank), F32),
+            pltpu.HBM((16, rank), F32),
             face,
             face,
             edge,
@@ -169,146 +179,200 @@
             pltpu.VMEM((steps, rows, rank), F32),
             pltpu.VMEM((rank, rank), F32),
             pltpu.VMEM((16, rank), F32),
+            pltpu.VMEM(sense.shape, F32),
             pltpu.SemaphoreType.DMA((steps,)),
             pltpu.SemaphoreType.DMA((steps,)),
             pltpu.SemaphoreType.DMA((4,)),
             pltpu.SemaphoreType.DMA((steps // 2,)),
             pltpu.SemaphoreType.DMA((steps // 2,)),
+            pltpu.SemaphoreType.DMA((1,)),
         ],
-        compiler_params=pltpu.CompilerParams(vmem_limit_bytes=58 << 20),
+        compiler_params=pltpu.CompilerParams(vmem_limit_bytes=36 << 20),
         cost_estimate=pl.CostEstimate(
             flops=6 * steps * rows * rank * rank, bytes_accessed=24 << 20, transcendentals=0
         ),
         name="local_gram",
-    )(observe, control, sense)
+    )(in_hbm(observe), in_hbm(control), in_hbm(sense))
 
 
 def inner_kernel(
-    lines, points,
-    obs, ctrl, conduct, drive, total, extra, field, obs_here, obs_sems, ctrl_sems,
+    points, obs_far, ctrl_far, conduct, drive,
+    total_far, extra_far, total, extra, obs, ctrl, conduct_here, drive_here, sems, obs_sems, ctrl_sems,
 ):
-    planes = ctrl.shape[0]
-    inner = pl.ds(1, lines)
-    rank = total.shape[0]
-
-    def ctrl_copy(p):
-        return pltpu.make_async_copy(ctrl.at[p], field.at[p + 1, inner], ctrl_sems.at[p])
-
-    def obs_copy(p):
-        return pltpu.make_async_copy(obs.at[p], obs_here.at[p], obs_sems.at[p])
-
-    for p in range(2):
-        ctrl_copy(p).start()
-        obs_copy(p).start()
+    steps, rows, rank = ctrl.shape
+    planes = steps // 2
+    small = [
+        pltpu.make_async_copy(conduct, conduct_here, sems.at[0]),
+        pltpu.make_async_copy(drive, drive_here, sems.at[1]),
+    ]
+
+    def ctrl_copy(i):
+        return pltpu.make_async_copy(ctrl_far.at[i], ctrl.at[i], ctrl_sems.at[i])
+
+    def obs_copy(i):
+        return pltpu.make_async_copy(obs_far.at[i], obs.at[i], obs_sems.at[i])
+
+    for i in (0, 1, 2):
+        ctrl_copy(i).start()
+    obs_copy(0).start()
+    for copy in small:
+        copy.start()
+    ctrl_copy(3).start()
+    obs_copy(1).start()
     total[...] = jnp.zeros_like(total)
     extra[...] = jnp.zeros_like(extra)
+    for copy in small:
+        copy.wait()
+    ctrl_copy(0).wait()
+    ctrl_copy(1).wait()
     empty = jnp.zeros((points, rank), F32)
-    for p in range(planes):
-        field[p + 1, 0] = empty
-        field[p + 1, lines + 1] = empty
-    for line in range(1, lines + 1):
-        field[0, line] = empty
-        field[planes + 1, line] = empty
-    ctrl_copy(0).wait()
 
     @pl.loop(0, planes)
     def _(p):
-        @pl.when(p + 1 < planes)
-        def _():
-            ctrl_copy(p + 1).wait()
-
-        @pl.when(p + 2 < planes)
-        def _():
-            ctrl_copy(p + 2).start()
-            obs_copy(p + 2).start()
-
-        obs_copy(p).wait()
-        half = lines // 2
-        rows = half * points
-        for line in (0, half):
-
-            def part(plane, first):
-                return field[plane, first : first + half]
-
-            center = part(p + 1, line + 1)
-            beside = part(p + 2, line + 1) + part(p, line + 1)
-            beside = beside + part(p + 1, line + 2) + part(p + 1, line)
-            center = center.reshape(rows, rank)
-            beside = beside.reshape(rows, rank)
+        up = jnp.minimum(p + 1, planes - 1)
+        down = jnp.maximum(p - 1, 0)
+        has_up = (p + 1 < planes).astype(F32)
+        has_down = (p > 0).astype(F32)
+        for half in range(2):
+
+            @pl.when(p + 1 < planes)
+            def _():
+                ctrl_copy(2 * p + 2 + half).wait()
+
+            @pl.when(p + 2 < planes)
+            def _():
+                ctrl_copy(2 * p + 4 + half).start()
+
+            @pl.when(p + 1 < planes)
+            def _():
+                obs_copy(2 * p + 2 + half).start()
+
+            obs_copy(2 * p + half).wait()
+            center = ctrl[2 * p + half]
+            beside = has_up * ctrl[2 * up + half] + has_down * ctrl[2 * down + half]
+            if half == 0:
+                before = empty
+                after = ctrl[2 * p + 1, :points]
+            else:
+                before = ctrl[2 * p, rows - points :]
+                after = empty
+            beside = beside + jnp.concatenate([before, center[: rows - points]], axis=0)
+            beside = beside + jnp.concatenate([center[points:], after], axis=0)
             place = lax.broadcasted_iota(jnp.int32, (rows, rank), 0) % points
             beside = beside + jnp.where(place > 0, pltpu.roll(center, 1, 0), 0.0)
             beside = beside + jnp.where(place < points - 1, pltpu.roll(center, rows - 1, 0), 0.0)
-            first = line * points
-            scale = conduct[p][:, first : first + rows] * (1.0 / 6.0)
+            first = half * rows
+            scale = conduct_here[pl.ds(p, 1), first : first + rows] * (1.0 / 6.0)
             applied = (beside - 6.0 * center).T * scale
-            some = plane_rows(drive, p, first, rows)
-            add_products(total, applied, obs_here[p, first : first + rows], extra, some)
-
-
-def inner_operator(observe, control, conduct, drive):
-    planes, lines, points, rank = control.shape
-    cells = lines * points
+            some = plane_rows(drive_here, p, first, rows)
+            add_products(total, applied, obs[2 * p + half], extra, some)
+
+    results = [
+        pltpu.make_async_copy(total, total_far, sems.at[0]),
+        pltpu.make_async_copy(extra, extra_far, sems.at[1]),
+    ]
+    for copy in results:
+        copy.start()
+    for copy in results:
+        copy.wait()
+
+
+def inner_operator(observe, control, conduct, drive, points):
+    steps, rows, rank = control.shape
     anywhere = pl.BlockSpec(memory_space=pltpu.HBM)
-    vmem = pl.BlockSpec(memory_space=pltpu.VMEM)
     return pl.pallas_call(
-        functools.partial(inner_kernel, lines, points),
-        in_specs=[anywhere, anywhere, vmem, vmem],
-        out_specs=[vmem, vmem],
+        functools.partial(inner_kernel, points),
+        in_specs=[anywhere] * 4,
+        out_specs=[anywhere] * 2,
         out_shape=[
-            jax.ShapeDtypeStruct((rank, rank), F32),
-            jax.ShapeDtypeStruct((16, rank), F32),
+            pltpu.HBM((rank, rank), F32),
+            pltpu.HBM((16, rank), F32),
         ],
         scratch_shapes=[
-            pltpu.VMEM((planes + 2, lines + 2, points, rank), F32),
-            pltpu.VMEM((planes, cells, rank), F32),
-            pltpu.SemaphoreType.DMA((planes,)),
-            pltpu.SemaphoreType.DMA((planes,)),
+            pltpu.VMEM((rank, rank), F32),
+            pltpu.VMEM((16, rank), F32),
+            pltpu.VMEM((steps, rows, rank), F32),
+            pltpu.VMEM((steps, rows, rank), F32),
+            pltpu.VMEM(conduct.shape, F32),
+            pltpu.VMEM(drive.shape, F32),
+            pltpu.SemaphoreType.DMA((2,)),
+            pltpu.SemaphoreType.DMA((steps,)),
+            pltpu.SemaphoreType.DMA((steps,)),
         ],
-        compiler_params=pltpu.CompilerParams(vmem_limit_bytes=58 << 20),
+        compiler_params=pltpu.CompilerParams(vmem_limit_bytes=36 << 20),
         cost_estimate=pl.CostEstimate(
-            flops=6 * planes * cells * rank * rank, bytes_accessed=18 << 20, transcendentals=0
+            flops=6 * steps * rows * rank * rank, bytes_accessed=18 << 20, transcendentals=0
         ),
         name="inner_operator",
-    )(observe.reshape(planes, cells, rank), control, conduct.reshape(planes, 1, cells), drive)
+    )(in_hbm(observe), in_hbm(control), in_hbm(conduct), in_hbm(drive))
 
 
 def outer_kernel(
-    obs, zlow, zhigh, ylow, yhigh, z_conduct, y_conduct, inner, extra, few_ctrl,
-    out, z_field, z_obs, y_field, y_obs, total, sems,
+    points, obs, zlow, zhigh, ylow, yhigh, conduct, inner, extra_far, few_far,
+    out, z_field, y_field, z_obs, y_obs, conduct_here, total, extra, few_ctrl, sems, obs_sems,
 ):
-    planes, lines, points, rank = obs.shape
-
-    def copies(i):
-        if i < 2:
-            plane = (planes - 1) * i
-            return (
-                pltpu.make_async_copy((zhigh if i else zlow), z_field.at[i], sems.at[2 * i]),
-                pltpu.make_async_copy(obs.at[plane], z_obs.at[i], sems.at[2 * i + 1]),
-            )
-        line = (lines - 1) * (i - 2)
-        place = pl.ds(planes * (i - 2), planes)
-        return (
-            pltpu.make_async_copy((yhigh if i == 3 else ylow), y_field.at[place], sems.at[2 * i]),
-            pltpu.make_async_copy(obs.at[:, line], y_obs.at[place], sems.at[2 * i + 1]),
+    steps, rows, rank = obs.shape
+    planes = steps // 2
+    conduct_copy = pltpu.make_async_copy(conduct, conduct_here, sems.at[0])
+    inner_copy = pltpu.make_async_copy(inner, total, sems.at[7])
+    few_copies = [
+        pltpu.make_async_copy(extra_far, extra, sems.at[8]),
+        pltpu.make_async_copy(few_far, few_ctrl, sems.at[9]),
+    ]
+    y_near = [
+        pltpu.make_async_copy(
+            obs.at[2 * p + i, pl.ds(i * (rows - points), points)],
+            y_obs.at[i, pl.ds(p * points, points)],
+            obs_sems.at[4 + planes * i + p],
         )
-
-    for i in (2, 3, 0, 1):
-        for copy in copies(i):
-            copy.start()
-    total[...] = inner[...]
-    for i in (2, 3):
-        for copy in copies(i):
-            copy.wait()
-    rows = 2 * planes * points
-    applied = y_field[...].reshape(rows, rank).T * (y_conduct[...] * (1.0 / 6.0))
-    add_products(total, applied, y_obs[...].reshape(rows, rank))
+        for i in range(2)
+        for p in range(planes)
+    ]
+    z_near = [
+        pltpu.make_async_copy(
+            obs.at[i if i < 2 else steps - 4 + i], z_obs.at[i], obs_sems.at[i]
+        )
+        for i in range(4)
+    ]
+    y_copies = [
+        pltpu.make_async_copy(ylow, y_field.at[0], sems.at[1]),
+        pltpu.make_async_copy(yhigh, y_field.at[1], sems.at[2]),
+    ]
+    z_copies = [
+        pltpu.make_async_copy(face.at[half], z_field.at[2 * i + half], sems.at[3 + 2 * i + half])
+        for i, face in enumerate((zlow, zhigh))
+        for half in range(2)
+    ]
+    conduct_copy.start()
+    for copy in y_copies + y_near + [inner_copy]:
+        copy.start()
+    for far, near in zip(z_copies, z_near):
+        far.start()
+        near.start()
+    for copy in few_copies:
+        copy.start()
+    conduct_copy.wait()
+    scale = conduct_here[...] * (1.0 / 6.0)
+    for copy in y_copies + y_near + [inner_copy]:
+        copy.wait()
     for i in range(2):
-        for copy in copies(i):
-            copy.wait()
-        rows = lines * points
-        applied = z_field[i].reshape(rows, rank).T * (z_conduct[i] * (1.0 / 6.0))
-        add_products(total, applied, z_obs[i].reshape(rows, rank))
-
+        cells = i * (2 * rows - points)
+        near = y_obs[i]
+        turned = [
+            y_field[i, p].T * scale[p : p + 1, cells : cells + points] for p in range(planes)
+        ]
+        add_products(total, jnp.concatenate(turned, axis=1), near)
+    for i in range(2):
+        plane = (planes - 1) * i
+        for half in range(2):
+            z_copies[2 * i + half].wait()
+            z_near[2 * i + half].wait()
+            turned = z_field[2 * i + half].T
+            turned = turned * scale[plane : plane + 1, half * rows : (half + 1) * rows]
+            add_products(total, turned, z_obs[2 * i + half])
+
+    for copy in few_copies:
+        copy.wait()
     width = rank // 2
     for side in range(2):
         cols = total[:, side * width : (side + 1) * width]
@@ -319,44 +383,33 @@
     out[:, 1, :, width:] = jnp.zeros((out.shape[0], out.shape[2], 128), F32)
 
 
-def with_outer(observe, faces, conduct, inner, extra, few_ctrl):
-    planes, lines, points, rank = observe.shape
-    zlow, zhigh, ylow, yhigh = faces
-    cells = lines * points
-    z_conduct = jnp.stack([conduct[0], conduct[-1]]).reshape(2, 1, cells)
-    y_conduct = jnp.stack([conduct[:, :points], conduct[:, cells - points :]])
+def with_outer(observe, faces, conduct, inner, extra, few_ctrl, points):
+    steps, rows, rank = observe.shape
     anywhere = pl.BlockSpec(memory_space=pltpu.HBM)
     vmem = pl.BlockSpec(memory_space=pltpu.VMEM)
     return pl.pallas_call(
-        outer_kernel,
-        in_specs=[anywhere] * 5 + [vmem] * 5,
+        functools.partial(outer_kernel, points),
+        in_specs=[anywhere] * 9,
         out_specs=vmem,
         out_shape=jax.ShapeDtypeStruct((64, 2, 8, rank // 2 + 128), F32),
         scratch_shapes=[
-            pltpu.VMEM((2, lines, points, rank), F32),
-            pltpu.VMEM((2, lines, points, rank), F32),
-            pltpu.VMEM((2 * planes, points, rank), F32),
-            pltpu.VMEM((2 * planes, points, rank), F32),
+            pltpu.VMEM((4, rows, rank), F32),
+            pltpu.VMEM((2, steps // 2, points, rank), F32),
+            pltpu.VMEM((4, rows, rank), F32),
+            pltpu.VMEM((2, steps // 2 * points, rank), F32),
+            pltpu.VMEM(conduct.shape, F32),
             pltpu.VMEM((rank, rank), F32),
-            pltpu.SemaphoreType.DMA((8,)),
+            pltpu.VMEM(extra.shape, F32),
+            pltpu.VMEM(few_ctrl.shape, F32),
+            pltpu.SemaphoreType.DMA((10,)),
+            pltpu.SemaphoreType.DMA((4 + steps,)),
         ],
-        compiler_params=pltpu.CompilerParams(vmem_limit_bytes=58 << 20),
+        compiler_params=pltpu.CompilerParams(vmem_limit_bytes=36 << 20),
         cost_estimate=pl.CostEstimate(
-            flops=15 * cells * rank * rank, bytes_accessed=14 << 20, transcendentals=0
+            flops=30 * rows * rank * rank, bytes_accessed=7 << 20, transcendentals=0
         ),
         name="outer_operator",
-    )(
-        observe,
-        zlow.reshape(lines, points, rank),
-        zhigh.reshape(lines, points, rank),
-        ylow,
-        yhigh,
-        z_conduct,
-        y_conduct.reshape(1, 2 * planes * points),
-        inner,
-        extra,
-        few_ctrl,
-    )
+    )(*map(in_hbm, (observe, *faces, conduct, inner, extra, few_ctrl)))
 
 
 def sum_kernel(parts, out):
@@ -457,11 +510,13 @@
             work[last:, :] -= change[last:, :]
 
 
-def bases_kernel(gram, start, right_out, left_out, image_out, cross, basis, work):
-    rank = cross.shape[0]
+def bases_kernel(gram, start, right_out, left_out, image_out, high, low, basis, work):
+    rank = high.shape[0]
     half = rank // 2
     for side in range(2):
-        cross[:, side * half : (side + 1) * half] = gram[:, side].reshape(rank, half)
+        cols = gram[:, side].reshape(rank, half)
+        place = slice(side * half, (side + 1) * half)
+        high[:, place], low[:, place] = split2(cols)
     basis[...] = start[...].T
     size = basis.shape[0]
     eye = (
@@ -471,13 +526,13 @@
 
     @pl.loop(0, 4)
     def _(turn):
-        @pl.when(turn % 2 == 0)
-        def _():
-            image_out[...] = product3(basis[...], cross[...])
-
-        @pl.when(turn % 2 == 1)
-        def _():
-            image_out[...] = product3(basis[...], cross[...], ((1,), (1,)))
+        for parity, contract in enumerate((((1,), (0,)), ((1,), (1,)))):
+
+            @pl.when(turn % 2 == parity)
+            def _():
+                bh, bl = split2(basis[...])
+                small = product(bh, low[...], contract) + product(bl, high[...], contract)
+                image_out[...] = product(bh, high[...], contract) + small
 
         held = image_out[...]
         work[:, :size] = product6(held, held, ((1,), (1,)))
@@ -499,7 +554,8 @@
         bases_kernel,
         out_shape=[shape, shape, shape],
         scratch_shapes=[
-            pltpu.VMEM((rank, rank), F32),
+            pltpu.VMEM((rank, rank), BF16),
+            pltpu.VMEM((rank, rank), BF16),
             pltpu.VMEM((size, rank), F32),
             pltpu.VMEM((size, 2 * size), F32),
         ],
@@ -555,15 +611,18 @@
 def reduced(factor_obs, factor_ctrl, diffusivity, input_map, output_map, start_block, order):
     planes, lines, points, rank = factor_ctrl.shape
     halves = (2 * planes, lines * points // 2, rank)
+    observe = factor_obs.reshape(halves)
+    control = factor_ctrl.reshape(halves)
     gram, few_ctrl, zlow, zhigh, ylow, yhigh = local_gram(
-        factor_obs.reshape(halves), factor_ctrl.reshape(halves), output_map, points
+        observe, control, output_map, points
     )
     arrived = scattered(gram)
     zlow, zhigh = from_neighbours(zlow, zhigh, "slab")
     ylow, yhigh = from_neighbours(ylow, yhigh, "sub")
-    inner, extra = inner_operator(factor_obs, factor_ctrl, diffusivity, input_map)
+    inner, extra = inner_operator(observe, control, diffusivity, input_map, points)
     gram = gathered(summed_copies(arrived))
-    oper = with_outer(factor_obs, (zlow, zhigh, ylow, yhigh), diffusivity, inner, extra, few_ctrl)
+    faces = (zlow, zhigh, ylow, yhigh)
+    oper = with_outer(observe, faces, diffusivity, inner, extra, few_ctrl, points)
     oper = scattered(oper)
     right, left, image = bases(gram, start_block)
     blocks = gathered(projected_copies(oper, left))

time: 157 us -> 164 us (1.045)
  blocking collectives: 0 us -> 40.1 us
  waiting for transfers between devices: 47.5 us -> 30.1 us
  starting transfers between devices: 45 us -> 34 us
  local copies, waits for them, and re-layouts: 3.99 us -> 1.51 us
    all_to_all x0 -> x1, blocking collectives: none -> 40.1 us  [scattered(): return lax.all_to_all(tiles, ALL, 0, 0, tiled=True)]
    all_to_all x2 -> x1, waiting for transfers between devices: 28.6 us -> 5.72 us  [scattered(): return lax.all_to_all(tiles, ALL, 0, 0, tiled=True)]
    all_to_all x2 -> x1, starting transfers between devices: 20.3 us -> 9.91 us  [scattered(): return lax.all_to_all(tiles, ALL, 0, 0, tiled=True)]
    ppermute x2, waiting for transfers between devices: 0.01 us -> 2.86 us  [from_neighbours(): lax.ppermute(high_face, axis, up)]
    ppermute x2, waiting for transfers between devices: 0.01 us -> 2.63 us  [from_neighbours(): lax.ppermute(low_face, axis, down)]
    reshape x3 -> x0, local copies, waits for them, and re-layouts: 1.87 us -> none  [the longest x1 0.66 us: with_outer(): y_conduct.reshape(1, 2 * planes * points)]
    pallas_call x3, Pallas kernels: 35.7 us -> 33.9 us  [the longest x1 13.7 us: inner_operator(): pl.pallas_call(functools.partial(inner_kernel, points), in_specs=[anywher...]
  transfers between devices with their start and end apart: 8 -> 7, of which waited for: 3 -> 4; matrix products, arithmetic and copies ran while one was open for 1% -> 0% of each run, Pallas kernels for 28% -> 26%
where the time goes in v3:
time: 164 us
  Pallas kernels  56.5 us (34%)
  blocking collectives  40.1 us (24%)
  starting transfers between devices  34 us (21%)
  waiting for transfers between devices  30.1 us (18%)
    all_to_all x1, blocking collectives, scattered(): return lax.all_to_all(tiles, ALL, 0, 0, tiled=True)  40.1 us
    all_to_all x2, waiting for transfers between devices, gathered(): tiles = lax.all_to_all(copies, ALL, 0, 0, tiled=True)  18.9 us
    pallas_call x1, Pallas kernels, bases(): pl.pallas_call(bases_kernel, out_shape=[shape, shape, shape], scratch_sha...  18.7 us
    pallas_call x1, Pallas kernels, inner_operator(): pl.pallas_call(functools.partial(inner_kernel, points), in_specs=[anywher...  13.7 us
    all_to_all x2, starting transfers between devices, gathered(): tiles = lax.all_to_all(copies, ALL, 0, 0, tiled=True)  13 us
    pallas_call x1, Pallas kernels, local_gram(): pl.pallas_call(gram_kernel, in_specs=[anywhere] * 3, out_specs=[vmem] + [...  10.9 us
    all_to_all x1, starting transfers between devices, scattered(): return lax.all_to_all(tiles, ALL, 0, 0, tiled=True)  9.91 us
    pallas_call x1, Pallas kernels, with_outer(): pl.pallas_call(functools.partial(outer_kernel, points), in_specs=[anywher...  9.33 us
  transfers between devices with their start and end apart: 7, of which 4 were waited for; matrix products, arithmetic and copies ran while one was open for 0% of the time, Pallas kernels for 26%

profile of v3, /device:TPU:1, one launch (start us, length us, event | category | flops | bytes accessed | tf_op | source)
XLA Modules:
  0.0 163.6 jit_solution(18137232254927135554)
XLA Ops:
  0.6 10.9 %local_gram.1 = (f32[64,2,8,256]{3,2,1,0:T(8,128)S(1)}, f32[16,512]{1,0:T(8,128)}, f32[2,512,512]{2,1,0:T(8,128)}, f32[2,512,512]{2,1,0:T(8,128)}, f32[4,64,512]{2,1,0:T(8,128)}, /*index=5*/f32[4,64,512]{2,1,0:T(8,128)}) custom-call(f32[8,512,512]{2,1,0:T(8,128)} %bitcast.11, f32[8,512,512]{2,1,0:T(8,128)} %bitcast.14, f32[4,4,1024]{2,1,0:T(4,128)} %sense.1), custom_call_target="tpu_custom_call" | custom-call | flops 6442450944 | bytes 25165824 | tf_op jit(solution)/shard_map/local_gram/pallas_call | solution.py:165
  11.5 4.6 %collective-permute-start = (f32[2,512,512]{2,1,0:T(8,128)}, f32[2,512,512]{2,1,0:T(8,128)}, u32[]{:S(2)}, u32[]{:S(2)}) collective-permute-start(f32[2,512,512]{2,1,0:T(8,128)} %get-tuple-element.23), channel_id=1, source_target_pairs={{0,4},{4,8},{8,12},{12,16},{16,20},{20,24},{24,28},{28,32},{32,36}... | collective-permute-start | bytes 6291464 | tf_op jit(solution)/shard_map/ppermute | solution.py:608
  16.1 1.9 %collective-permute-start.1 = (f32[2,512,512]{2,1,0:T(8,128)}, f32[2,512,512]{2,1,0:T(8,128)}, u32[]{:S(2)}, u32[]{:S(2)}) collective-permute-start(f32[2,512,512]{2,1,0:T(8,128)} %get-tuple-element.24), channel_id=1, source_target_pairs={{4,0},{8,4},{12,8},{16,12},{20,16},{24,20},{28,24},{32,28},{36,32}... | collective-permute-start | bytes 6291464 | tf_op jit(solution)/shard_map/ppermute | solution.py:608
  18.0 40.1 %all_to_all.20.parts = f32[128,8,256]{2,1,0:T(8,128)S(1)} all-to-all(f32[128,8,256]{2,1,0:T(8,128)S(1)} %bitcast.10), channel_id=1, replica_groups=mesh['slab'=32,'sub'=4] {'slab','sub'}, dimensions={0} | all-to-all | bytes 2097152 | tf_op jit(solution)/shard_map/all_to_all | solution.py:422
  58.1 1.3 sum_gram.1
  59.4 8.9 %all-to-all-start.1 = ((f32[128,8,256]{2,1,0:T(8,128)}), f32[128,8,256]{2,1,0:T(8,128)S(1)}, u32[]{:S(2)}, u32[]{:S(2)}) async-start(f32[128,8,256]{2,1,0:T(8,128)} %sum_gram.1), calls=%async_computation.1 | async-start | bytes 2097152 | tf_op jit(solution)/shard_map/all_to_all | solution.py:463
  68.3 3.3 %collective-permute-start.2 = (f32[4,64,512]{2,1,0:T(8,128)S(1)}, f32[4,64,512]{2,1,0:T(8,128)S(1)}, u32[]{:S(2)}, u32[]{:S(2)}) collective-permute-start(f32[4,64,512]{2,1,0:T(8,128)S(1)} %copy-done.6), channel_id=1, source_target_pairs={{0,1},{1,2},{2,3},{4,5},{5,6},{6,7},{8,9},{9,10},{10,11},{12,13},{... | collective-permute-start | bytes 1572872 | tf_op jit(solution)/shard_map/ppermute | solution.py:608
  71.6 1.3 collective-permute-start.3
  73.0 13.7 %inner_operator.1 = (f32[512,512]{1,0:T(8,128)}, f32[16,512]{1,0:T(8,128)}) custom-call(f32[8,512,512]{2,1,0:T(8,128)} %bitcast.12, f32[8,512,512]{2,1,0:T(8,128)} %bitcast.15, f32[4,1024]{1,0:T(4,128)} %conduct.3, f32[4,4,1024]{2,1,0:T(4,128)} %drive.1), custom_call_target="tpu_custom_call" | custom-call | flops 6442450944 | bytes 18874368 | tf_op jit(solution)/shard_map/inner_operator/pallas_call | solution.py:283
  86.7 2.9 %collective-permute-done.2.ylow = f32[4,64,512]{2,1,0:T(8,128)S(1)} collective-permute-done((f32[4,64,512]{2,1,0:T(8,128)S(1)}, f32[4,64,512]{2,1,0:T(8,128)S(1)}, u32[]{:S(2)}, u32[]{:S(2)}) %collective-permute-start.2) | collective-permute-done | bytes 524320 | tf_op jit(solution)/shard_map/ppermute | solution.py:608
  89.5 2.6 %collective-permute-done.3.yhigh = f32[4,64,512]{2,1,0:T(8,128)S(1)} collective-permute-done((f32[4,64,512]{2,1,0:T(8,128)S(1)}, f32[4,64,512]{2,1,0:T(8,128)S(1)}, u32[]{:S(2)}, u32[]{:S(2)}) %collective-permute-start.3) | collective-permute-done | bytes 524320 | tf_op jit(solution)/shard_map/ppermute | solution.py:608
  92.2 0.0 collective-permute-done.1.zhigh
  92.2 0.8 copy-done.4
  93.0 9.3 %outer_operator.1 = f32[64,2,8,384]{3,2,1,0:T(8,128)} custom-call(f32[8,512,512]{2,1,0:T(8,128)} %bitcast.13, f32[2,512,512]{2,1,0:T(8,128)} %collective-permute-done.zlow, f32[2,512,512]{2,1,0:T(8,128)} %collective-permute-done.1.zhigh, f32[4,64,512]{2,1,0:T(8,128)} %copy-done.3, f32[4,64,512]{2,1,0:T(8,128)} %copy-done.4, f32[4,1024]{1,0:T(4,128)} %conduct.3, ...), custom_call_target="tpu_custom_call" | custom-call | flops 4026531840 | bytes 7340032 | tf_op jit(solution)/shard_map/outer_operator/pallas_call | solution.py:390
  102.3 0.0 copy-start
  102.3 0.0 all-to-all-done.1
  102.3 9.9 %all-to-all-start.2 = ((f32[128,8,384]{2,1,0:T(8,128)}), f32[128,8,384]{2,1,0:T(8,128)S(1)}, u32[]{:S(2)}, u32[]{:S(2)}) async-start(f32[128,8,384]{2,1,0:T(8,128)} %bitcast.5), calls=%async_computation.2 | async-start | bytes 3145728 | tf_op jit(solution)/shard_map/all_to_all | solution.py:422
  112.2 18.7 %bases.1 = (f32[128,512]{1,0:T(8,128)S(1)}, f32[128,512]{1,0:T(8,128)S(1)}, f32[128,512]{1,0:T(8,128)S(1)}) custom-call(f32[64,2,8,256]{3,2,1,0:T(8,128)S(1)} %bitcast.8, f32[512,128]{1,0:T(8,128)S(1)} %copy-done), custom_call_target="tpu_custom_call" | custom-call | flops 20000000000 | bytes 4194304 | tf_op jit(solution)/shard_map/bases/pallas_call | solution.py:553
  130.9 0.7 copy-done.1
  131.7 5.7 %all-to-all-done.2.parts = f32[128,8,384]{2,1,0:T(8,128)S(1)} async-done(((f32[128,8,384]{2,1,0:T(8,128)}), f32[128,8,384]{2,1,0:T(8,128)S(1)}, u32[]{:S(2)}, u32[]{:S(2)}) %all-to-all-start.2) | async-done | bytes 1572896 | tf_op jit(solution)/shard_map/all_to_all | solution.py:422
  137.4 1.3 project.1
  138.7 4.0 %all-to-all-start.3 = ((f32[128,8,256]{2,1,0:T(8,128)}), f32[128,8,256]{2,1,0:T(8,128)S(1)}, u32[]{:S(2)}, u32[]{:S(2)}) async-start(f32[128,8,256]{2,1,0:T(8,128)} %project.1), calls=%async_computation.3 | async-start | bytes 2097152 | tf_op jit(solution)/shard_map/all_to_all | solution.py:463
  143.4 18.9 %all-to-all-done.3 = f32[128,8,256]{2,1,0:T(8,128)S(1)} async-done(((f32[128,8,256]{2,1,0:T(8,128)}), f32[128,8,256]{2,1,0:T(8,128)S(1)}, u32[]{:S(2)}, u32[]{:S(2)}) %all-to-all-start.3) | async-done | bytes 1048608 | tf_op jit(solution)/shard_map/all_to_all | solution.py:463
  162.3 1.3 finish.1
  (12 shorter events, 0.0 us)
Async XLA Ops:
  11.5 80.7 %collective-permute-start = (f32[2,512,512]{2,1,0:T(8,128)}, f32[2,512,512]{2,1,0:T(8,128)}, u32[]{:S(2)}, u32[]{:S(2)}) collective-permute-start(f32[2,512,512]{2,1,0:T(8,128)} %get-tuple-element.23), channel_id=1, source_target_pairs={{0,4},{4,8},{8,12},{12,16},{16,20},{20,24},{24,28},{28,32},{32,36}... | collective-permute-start | bytes 6291464 | tf_op jit(solution)/shard_map/ppermute | solution.py:608
  16.1 76.1 %collective-permute-start.1 = (f32[2,512,512]{2,1,0:T(8,128)}, f32[2,512,512]{2,1,0:T(8,128)}, u32[]{:S(2)}, u32[]{:S(2)}) collective-permute-start(f32[2,512,512]{2,1,0:T(8,128)} %get-tuple-element.24), channel_id=1, source_target_pairs={{4,0},{8,4},{12,8},{16,12},{20,16},{24,20},{28,24},{32,28},{36,32}... | collective-permute-start | bytes 6291464 | tf_op jit(solution)/shard_map/ppermute | solution.py:608
  58.1 10.2 %copy-start.6 = (f32[4,64,512]{2,1,0:T(8,128)S(1)}, f32[4,64,512]{2,1,0:T(8,128)}, u32[]{:S(2)}) copy-start(f32[4,64,512]{2,1,0:T(8,128)} %get-tuple-element.25) | copy-start | bytes 1572868
  58.1 13.5 %copy-start.5 = (f32[4,64,512]{2,1,0:T(8,128)S(1)}, f32[4,64,512]{2,1,0:T(8,128)}, u32[]{:S(2)}) copy-start(f32[4,64,512]{2,1,0:T(8,128)} %get-tuple-element.26) | copy-start | bytes 1572868
  59.4 42.9 %all-to-all-start.1 = ((f32[128,8,256]{2,1,0:T(8,128)}), f32[128,8,256]{2,1,0:T(8,128)S(1)}, u32[]{:S(2)}, u32[]{:S(2)}) async-start(f32[128,8,256]{2,1,0:T(8,128)} %sum_gram.1), calls=%async_computation.1 | async-start | bytes 2097152 | tf_op jit(solution)/shard_map/all_to_all | solution.py:463
  68.3 21.2 %collective-permute-start.2 = (f32[4,64,512]{2,1,0:T(8,128)S(1)}, f32[4,64,512]{2,1,0:T(8,128)S(1)}, u32[]{:S(2)}, u32[]{:S(2)}) collective-permute-start(f32[4,64,512]{2,1,0:T(8,128)S(1)} %copy-done.6), channel_id=1, source_target_pairs={{0,1},{1,2},{2,3},{4,5},{5,6},{6,7},{8,9},{9,10},{10,11},{12,13},{... | collective-permute-start | bytes 1572872 | tf_op jit(solution)/shard_map/ppermute | solution.py:608
  71.6 20.5 %collective-permute-start.3 = (f32[4,64,512]{2,1,0:T(8,128)S(1)}, f32[4,64,512]{2,1,0:T(8,128)S(1)}, u32[]{:S(2)}, u32[]{:S(2)}) collective-permute-start(f32[4,64,512]{2,1,0:T(8,128)S(1)} %copy-done.5), channel_id=1, source_target_pairs={{1,0},{2,1},{3,2},{5,4},{6,5},{7,6},{9,8},{10,9},{11,10},{13,12},{... | collective-permute-start | bytes 1572872 | tf_op jit(solution)/shard_map/ppermute | solution.py:608
  89.5 2.6 %copy-start.3 = (f32[4,64,512]{2,1,0:T(8,128)}, f32[4,64,512]{2,1,0:T(8,128)S(1)}, u32[]{:S(2)}) copy-start(f32[4,64,512]{2,1,0:T(8,128)S(1)} %collective-permute-done.2.ylow) | copy-start | bytes 1572868
  92.2 0.8 copy-start.4
  102.3 9.9 %copy-start = (f32[512,128]{1,0:T(8,128)S(1)}, f32[512,128]{1,0:T(8,128)}, u32[]{:S(2)}) copy-start(f32[512,128]{1,0:T(8,128)} %start.1) | copy-start | bytes 786436
  102.3 35.1 %all-to-all-start.2 = ((f32[128,8,384]{2,1,0:T(8,128)}), f32[128,8,384]{2,1,0:T(8,128)S(1)}, u32[]{:S(2)}, u32[]{:S(2)}) async-start(f32[128,8,384]{2,1,0:T(8,128)} %bitcast.5), calls=%async_computation.2 | async-start | bytes 3145728 | tf_op jit(solution)/shard_map/all_to_all | solution.py:422
  130.9 0.7 copy-start.1
  137.4 24.9 %copy-start.2 = (f32[128,512]{1,0:T(8,128)S(1)}, f32[128,512]{1,0:T(8,128)}, u32[]{:S(2)}) copy-start(f32[128,512]{1,0:T(8,128)} %copy-done.1) | copy-start | bytes 786436
  138.7 23.6 %all-to-all-start.3 = ((f32[128,8,256]{2,1,0:T(8,128)}), f32[128,8,256]{2,1,0:T(8,128)S(1)}, u32[]{:S(2)}, u32[]{:S(2)}) async-start(f32[128,8,256]{2,1,0:T(8,128)} %project.1), calls=%async_computation.3 | async-start | bytes 2097152 | tf_op jit(solution)/shard_map/all_to_all | solution.py:463

commit v4 on v3

--- a/solution.py
+++ b/solution.py
@@ -5,10 +5,11 @@
 from jax import lax
 from jax.experimental import pallas as pl
 from jax.experimental.pallas import tpu as pltpu
+from jax.sharding import Mesh
 from jax.sharding import PartitionSpec as P
 
 
-ALL = ("slab", "sub")
+CHIPS = ("chip", "sub")
 F32 = jnp.float32
 BF16 = jnp.bfloat16
 PANEL = 32
@@ -74,13 +75,22 @@
     return rows_split(chosen)
 
 
+def half_of(total, side):
+    width = total.shape[1] // 2
+    return total[:, pl.ds(pl.multiple_of(side * width, 128), width)]
+
+
+def core_index():
+    return lax.axis_index("core").reshape(1).astype(jnp.int32)
+
+
 def in_hbm(value):
     return pltpu.with_memory_space_constraint(value, pltpu.HBM)
 
 
 def gram_kernel(
-    obs, ctrl, sense,
-    gram, few_far, zlow, zhigh, ylow, yhigh,
+    core, obs, ctrl, sense,
+    own, other, few_far, zlow, zhigh, ylow, yhigh,
     obs_here, ctrl_here, total, extra, sense_here, obs_sems, ctrl_sems, z_sems, low_sems, high_sems, other_sems,
 ):
     steps, rows, _ = obs.shape
@@ -144,10 +154,8 @@
 
     few_copy = pltpu.make_async_copy(extra, few_far, other_sems.at[0])
     few_copy.start()
-    width = total.shape[1] // 2
-    for side in range(2):
-        cols = total[:, side * width : (side + 1) * width]
-        gram[:, side] = cols.reshape(gram.shape[0], gram.shape[2], width)
+    for slot, out in enumerate((own, other)):
+        out[...] = half_of(total, core[0] ^ slot).reshape(out.shape)
     few_copy.wait()
     for i in range(4):
         z_copy(i).wait()
@@ -164,10 +172,11 @@
     edge = pltpu.HBM((steps // 2, points, rank), F32)
     return pl.pallas_call(
         gram_kernel,
-        in_specs=[anywhere] * 3,
-        out_specs=[vmem] + [anywhere] * 5,
+        in_specs=[pl.BlockSpec(memory_space=pltpu.SMEM)] + [anywhere] * 3,
+        out_specs=[vmem] * 2 + [anywhere] * 5,
         out_shape=[
-            jax.ShapeDtypeStruct((64, 2, 8, rank // 2), F32),
+            jax.ShapeDtypeStruct((rank // 8, 8, rank // 2), F32),
+            jax.ShapeDtypeStruct((rank // 8, 8, rank // 2), F32),
             pltpu.HBM((16, rank), F32),
             face,
             face,
@@ -192,7 +201,7 @@
             flops=6 * steps * rows * rank * rank, bytes_accessed=24 << 20, transcendentals=0
         ),
         name="local_gram",
-    )(in_hbm(observe), in_hbm(control), in_hbm(sense))
+    )(core_index(), in_hbm(observe), in_hbm(control), in_hbm(sense))
 
 
 def inner_kernel(
@@ -308,8 +317,8 @@
 
 
 def outer_kernel(
-    points, obs, zlow, zhigh, ylow, yhigh, conduct, inner, extra_far, few_far,
-    out, z_field, y_field, z_obs, y_obs, conduct_here, total, extra, few_ctrl, sems, obs_sems,
+    points, core, obs, zlow, zhigh, ylow, yhigh, conduct, inner, extra_far, few_far,
+    own, other, z_field, y_field, z_obs, y_obs, conduct_here, total, extra, few_ctrl, sems, obs_sems,
 ):
     steps, rows, rank = obs.shape
     planes = steps // 2
@@ -373,14 +382,14 @@
 
     for copy in few_copies:
         copy.wait()
-    width = rank // 2
-    for side in range(2):
-        cols = total[:, side * width : (side + 1) * width]
-        out[:, side, :, :width] = cols.reshape(out.shape[0], out.shape[2], width)
     summed = jnp.concatenate([extra[0:4] + extra[4:8], few_ctrl[0:4] + few_ctrl[4:8]], axis=0)
     wide = jnp.concatenate([summed, jnp.zeros((120, rank), F32)], axis=0).T
-    out[:, 0, :, width:] = wide.reshape(out.shape[0], out.shape[2], 128)
-    out[:, 1, :, width:] = jnp.zeros((out.shape[0], out.shape[2], 128), F32)
+    width = rank // 2
+    for slot, out in enumerate((own, other)):
+        side = core[0] ^ slot
+        out[:, :, :width] = half_of(total, side).reshape(out.shape[0], out.shape[1], width)
+        part = wide * (side == 0).astype(F32)
+        out[:, :, width:] = part.reshape(out.shape[0], out.shape[1], 128)
 
 
 def with_outer(observe, faces, conduct, inner, extra, few_ctrl, points):
@@ -389,9 +398,9 @@
     vmem = pl.BlockSpec(memory_space=pltpu.VMEM)
     return pl.pallas_call(
         functools.partial(outer_kernel, points),
-        in_specs=[anywhere] * 9,
-        out_specs=vmem,
-        out_shape=jax.ShapeDtypeStruct((64, 2, 8, rank // 2 + 128), F32),
+        in_specs=[pl.BlockSpec(memory_space=pltpu.SMEM)] + [anywhere] * 9,
+        out_specs=[vmem] * 2,
+        out_shape=[jax.ShapeDtypeStruct((rank // 8, 8, rank // 2 + 128), F32)] * 2,
         scratch_shapes=[
             pltpu.VMEM((4, rows, rank), F32),
             pltpu.VMEM((2, steps // 2, points, rank), F32),
@@ -409,7 +418,7 @@
             flops=30 * rows * rank * rank, bytes_accessed=7 << 20, transcendentals=0
         ),
         name="outer_operator",
-    )(*map(in_hbm, (observe, *faces, conduct, inner, extra, few_ctrl)))
+    )(core_index(), *map(in_hbm, (observe, *faces, conduct, inner, extra, few_ctrl)))
 
 
 def sum_kernel(parts, out):
@@ -417,9 +426,25 @@
     out[...] = jnp.broadcast_to(whole, out.shape)
 
 
-def scattered(parts):
-    tiles = parts.reshape(parts.shape[0] * parts.shape[1], *parts.shape[2:])
-    return lax.all_to_all(tiles, ALL, 0, 0, tiled=True)
+def swapped(value):
+    return lax.ppermute(value, "core", [(0, 1), (1, 0)])
+
+
+def add_kernel(first, second, out):
+    out[...] = first[...] + second[...]
+
+
+def scattered(own, other):
+    other = swapped(other)
+    both = pl.pallas_call(
+        add_kernel,
+        out_shape=jax.ShapeDtypeStruct(own.shape, F32),
+        compiler_params=pltpu.CompilerParams(vmem_limit_bytes=6 << 20),
+        cost_estimate=pl.CostEstimate(
+            flops=own.size, bytes_accessed=12 * own.size, transcendentals=0
+        ),
+    )(own, other)
+    return lax.all_to_all(both, CHIPS, 0, 0, tiled=True)
 
 
 def summed_copies(arrived):
@@ -444,7 +469,6 @@
 
 
 def projected_copies(arrived, left):
-    side = lax.axis_index("sub") & 1
     vmem = pl.BlockSpec(memory_space=pltpu.VMEM)
     return pl.pallas_call(
         project_kernel,
@@ -456,12 +480,12 @@
             flops=arrived.size, bytes_accessed=8 * arrived.size, transcendentals=0
         ),
         name="project",
-    )(side.reshape(1).astype(jnp.int32), arrived, left)
+    )(core_index(), arrived, left)
 
 
 def gathered(copies):
-    tiles = lax.all_to_all(copies, ALL, 0, 0, tiled=True)
-    return tiles.reshape(64, 2, *tiles.shape[1:])
+    mine = lax.all_to_all(copies, CHIPS, 0, 0, tiled=True)
+    return mine, swapped(mine)
 
 
 def inverse_factor(work):
@@ -510,13 +534,12 @@
             work[last:, :] -= change[last:, :]
 
 
-def bases_kernel(gram, start, right_out, left_out, image_out, high, low, basis, work):
+def bases_kernel(core, mine, theirs, start, right_out, left_out, image_out, high, low, basis, work):
     rank = high.shape[0]
     half = rank // 2
-    for side in range(2):
-        cols = gram[:, side].reshape(rank, half)
-        place = slice(side * half, (side + 1) * half)
-        high[:, place], low[:, place] = split2(cols)
+    for slot, part in enumerate((mine, theirs)):
+        place = pl.ds(pl.multiple_of((core[0] ^ slot) * half, 128), half)
+        high[:, place], low[:, place] = split2(part[...].reshape(rank, half))
     basis[...] = start[...].T
     size = basis.shape[0]
     eye = (
@@ -547,11 +570,13 @@
     left_out[...] = basis[...]
 
 
-def bases(gram, start):
+def bases(mine, theirs, start):
     rank, size = start.shape
     shape = jax.ShapeDtypeStruct((size, rank), F32)
+    vmem = pl.BlockSpec(memory_space=pltpu.VMEM)
     return pl.pallas_call(
         bases_kernel,
+        in_specs=[pl.BlockSpec(memory_space=pltpu.SMEM)] + [vmem] * 3,
         out_shape=[shape, shape, shape],
         scratch_shapes=[
             pltpu.VMEM((rank, rank), BF16),
@@ -564,13 +589,13 @@
             flops=20_000_000_000, bytes_accessed=4 << 20, transcendentals=0
         ),
         name="bases",
-    )(gram, start)
-
-
-def finish_kernel(order, right, left, image, blocks, mass, state, inputs, outputs):
+    )(core_index(), mine, theirs, start)
+
+
+def finish_kernel(order, right, left, image, mine, theirs, mass, state, inputs, outputs):
     size, rank = right.shape
-    turned = (blocks[:, 0, :, :size] + blocks[:, 1, :, :size]).reshape(rank, size)
-    few = blocks[:, 0, :, size:].reshape(rank, 128)
+    blocks = (mine[...] + theirs[...]).reshape(rank, size + 128)
+    turned, few = blocks[:, :size], blocks[:, size:]
     kept_col = lax.broadcasted_iota(jnp.int32, (size, size), 0) < order[0]
     kept_row = lax.broadcasted_iota(jnp.int32, (size, size), 1) < order[0]
     kept = jnp.logical_and(kept_col, kept_row).astype(F32)
@@ -580,12 +605,12 @@
     outputs[...] = (kept_row.astype(F32) * product3(right[...], few).T)[4:8]
 
 
-def finish(order, right, left, image, blocks):
+def finish(order, right, left, image, mine, theirs):
     size, _ = right.shape
     vmem = pl.BlockSpec(memory_space=pltpu.VMEM)
     return pl.pallas_call(
         finish_kernel,
-        in_specs=[pl.BlockSpec(memory_space=pltpu.SMEM)] + [vmem] * 4,
+        in_specs=[pl.BlockSpec(memory_space=pltpu.SMEM)] + [vmem] * 5,
         out_specs=[vmem] * 4,
         out_shape=[
             jax.ShapeDtypeStruct((size, size), F32),
@@ -598,7 +623,7 @@
             flops=1_000_000_000, bytes_accessed=4 << 20, transcendentals=0
         ),
         name="finish",
-    )(order, right, left, image, blocks)
+    )(order, right, left, image, mine, theirs)
 
 
 def from_neighbours(low_face, high_face, axis):
@@ -613,33 +638,38 @@
     halves = (2 * planes, lines * points // 2, rank)
     observe = factor_obs.reshape(halves)
     control = factor_ctrl.reshape(halves)
-    gram, few_ctrl, zlow, zhigh, ylow, yhigh = local_gram(
+    own, other, few_ctrl, zlow, zhigh, ylow, yhigh = local_gram(
         observe, control, output_map, points
     )
-    arrived = scattered(gram)
-    zlow, zhigh = from_neighbours(zlow, zhigh, "slab")
+    arrived = scattered(own, other)
+    zlow, zhigh = from_neighbours(zlow, zhigh, ("chip", "core"))
     ylow, yhigh = from_neighbours(ylow, yhigh, "sub")
     inner, extra = inner_operator(observe, control, diffusivity, input_map, points)
     gram = gathered(summed_copies(arrived))
     faces = (zlow, zhigh, ylow, yhigh)
-    oper = with_outer(observe, faces, diffusivity, inner, extra, few_ctrl, points)
-    oper = scattered(oper)
-    right, left, image = bases(gram, start_block)
+    own, other = with_outer(observe, faces, diffusivity, inner, extra, few_ctrl, points)
+    oper = scattered(own, other)
+    right, left, image = bases(*gram, start_block)
     blocks = gathered(projected_copies(oper, left))
-    mass, state, inputs, outputs = finish(order, right, left, image, blocks)
+    mass, state, inputs, outputs = finish(order, right, left, image, *blocks)
     return mass, state, inputs.T, outputs
 
 
 def solution(mesh):
+    slab = mesh.shape["slab"]
+    torus = Mesh(
+        mesh.devices.reshape(slab // 2, 2, mesh.shape["sub"]), ("chip", "core", "sub")
+    )
+    slabs = ("chip", "core")
     placed = (
-        P("slab", "sub", None, None),
-        P("slab", "sub", None, None),
-        P("slab", "sub"),
-        P(None, "slab", "sub"),
-        P(None, "slab", "sub"),
+        P(slabs, "sub", None, None),
+        P(slabs, "sub", None, None),
+        P(slabs, "sub"),
+        P(None, slabs, "sub"),
+        P(None, slabs, "sub"),
         P(),
         P(),
     )
     return jax.shard_map(
-        reduced, mesh=mesh, in_specs=placed, out_specs=(P(), P(), P(), P()), check_vma=False
+        reduced, mesh=torus, in_specs=placed, out_specs=(P(), P(), P(), P()), check_vma=False
     )

time: 164 us -> 133 us (0.81)
  waiting for transfers between devices: 30.1 us -> 2.34 us
  blocking collectives: 40.1 us -> 21.4 us
  starting transfers between devices: 34 us -> 49.6 us
    all_to_all x3, waiting for transfers between devices: 24.6 us -> 1.26 us  [the longest x2 1.26 us: scattered(): return lax.all_to_all(both, CHIPS, 0, 0, tiled=True)]
    all_to_all x1, blocking collectives: 40.1 us -> 21.4 us  [gathered(): mine = lax.all_to_all(copies, CHIPS, 0, 0, tiled=True)]
    all_to_all x3, starting transfers between devices: 22.9 us -> 31.1 us  [the longest x2 22 us: scattered(): return lax.all_to_all(both, CHIPS, 0, 0, tiled=True)]
    ppermute x0 -> x4, starting transfers between devices: none -> 7.61 us  [swapped(): return lax.ppermute(value, 'core', [(0, 1), (1, 0)])]
    ppermute x2, waiting for transfers between devices: 2.86 us -> 0.01 us  [from_neighbours(): lax.ppermute(high_face, axis, up)]
    ppermute x2, waiting for transfers between devices: 2.63 us -> 0.01 us  [from_neighbours(): lax.ppermute(low_face, axis, down)]
    pallas_call x3 -> x5, Pallas kernels: 38.9 us -> 39.8 us  [the longest x1 18.7 us: bases(): pl.pallas_call(bases_kernel, in_specs=[pl.BlockSpec(memory_space=pltpu.SM...]
  transfers between devices with their start and end apart: 7 -> 11, of which waited for: 4 -> 3; matrix products, arithmetic and copies ran while one was open for 0% -> 0% of each run, Pallas kernels for 26% -> 33%
where the time goes in v4:
time: 133 us
  Pallas kernels  56.1 us (42%)
  starting transfers between devices  49.6 us (37%)
  blocking collectives  21.4 us (16%)
  waiting for transfers between devices  2.34 us (2%)
  local copies, waits for them, and re-layouts  1.87 us (1%)
  between operations  1.47 us (1%)
    all_to_all x2, starting transfers between devices, scattered(): return lax.all_to_all(both, CHIPS, 0, 0, tiled=True)  22 us
    all_to_all x1, blocking collectives, gathered(): mine = lax.all_to_all(copies, CHIPS, 0, 0, tiled=True)  21.4 us
    pallas_call x1, Pallas kernels, bases(): pl.pallas_call(bases_kernel, in_specs=[pl.BlockSpec(memory_space=pltpu.SM...  18.7 us
    pallas_call x1, Pallas kernels, inner_operator(): pl.pallas_call(functools.partial(inner_kernel, points), in_specs=[anywher...  13.8 us
    pallas_call x1, Pallas kernels, local_gram(): pl.pallas_call(gram_kernel, in_specs=[pl.BlockSpec(memory_space=pltpu.SME...  10.9 us
    all_to_all x1, starting transfers between devices, gathered(): mine = lax.all_to_all(copies, CHIPS, 0, 0, tiled=True)  9.03 us
    pallas_call x1, Pallas kernels, with_outer(): pl.pallas_call(functools.partial(outer_kernel, points), in_specs=[pl.Bloc...  8.47 us
    ppermute x2, starting transfers between devices, from_neighbours(): lax.ppermute(high_face, axis, up)  7.74 us
  transfers between devices with their start and end apart: 11, of which 3 were waited for; matrix products, arithmetic and copies ran while one was open for 0% of the time, Pallas kernels for 33%

profile of v4, /device:TPU:1, one launch (start us, length us, event | category | flops | bytes accessed | tf_op | source)
XLA Modules:
  0.0 132.8 jit_solution(5100504020442320536)
XLA Ops:
  0.6 10.9 %local_gram.1 = (f32[64,8,256]{2,1,0:T(8,128)S(1)}, f32[64,8,256]{2,1,0:T(8,128)S(1)}, f32[16,512]{1,0:T(8,128)}, f32[2,512,512]{2,1,0:T(8,128)}, f32[2,512,512]...) custom-call(s32[1]{0:T(128)} %bitcast.core.side, f32[8,512,512]{2,1,0:T(8,128)} %bitcast.6, ...), custom_call_target="tpu_custom_call" | custom-call | flops 6442450944 | bytes 25165824 | tf_op jit(solution)/shard_map/local_gram/pallas_call | solution.py:173
  11.5 4.6 %collective-permute-start.2 = (f32[2,512,512]{2,1,0:T(8,128)}, f32[2,512,512]{2,1,0:T(8,128)}, u32[]{:S(2)}, u32[]{:S(2)}) collective-permute-start(f32[2,512,512]{2,1,0:T(8,128)} %get-tuple-element.27), channel_id=1, source_target_pairs={{0,4},{4,8},{8,12},{12,16},{16,20},{20,24},{24,28},{28,32},{32,36}... | collective-permute-start | bytes 6291464 | tf_op jit(solution)/shard_map/ppermute | solution.py:633
  16.1 1.9 %collective-permute-start.3 = (f32[2,512,512]{2,1,0:T(8,128)}, f32[2,512,512]{2,1,0:T(8,128)}, u32[]{:S(2)}, u32[]{:S(2)}) collective-permute-start(f32[2,512,512]{2,1,0:T(8,128)} %get-tuple-element.28), channel_id=1, source_target_pairs={{4,0},{8,4},{12,8},{16,12},{20,16},{24,20},{28,24},{32,28},{36,32}... | collective-permute-start | bytes 6291464 | tf_op jit(solution)/shard_map/ppermute | solution.py:633
  18.1 3.1 %collective-permute-start.4 = (f32[4,64,512]{2,1,0:T(8,128)}, f32[4,64,512]{2,1,0:T(8,128)S(1)}, u32[]{:S(2)}, u32[]{:S(2)}) collective-permute-start(f32[4,64,512]{2,1,0:T(8,128)} %get-tuple-element.29), channel_id=1, source_target_pairs={{0,1},{1,2},{2,3},{4,5},{5,6},{6,7},{8,9},{9,10},{10,11},{12,13},{... | collective-permute-start | bytes 1572872 | tf_op jit(solution)/shard_map/ppermute | solution.py:633
  21.3 1.3 collective-permute-start.5
  22.8 0.8 shard_map.102
  23.6 12.3 %all-to-all-start = ((f32[64,8,256]{2,1,0:T(8,128)}), f32[64,8,256]{2,1,0:T(8,128)S(1)}, u32[]{:S(2)}, u32[]{:S(2)}) async-start(f32[64,8,256]{2,1,0:T(8,128)} %shard_map.102), calls=%async_computation | async-start | bytes 1048576 | tf_op jit(solution)/shard_map/all_to_all | solution.py:447
  36.0 13.8 %inner_operator.1 = (f32[512,512]{1,0:T(8,128)}, f32[16,512]{1,0:T(8,128)}) custom-call(f32[8,512,512]{2,1,0:T(8,128)} %bitcast.7, f32[8,512,512]{2,1,0:T(8,128)} %bitcast.5, f32[4,1024]{1,0:T(4,128)} %conduct.3, f32[4,4,1024]{2,1,0:T(4,128)} %drive.1), custom_call_target="tpu_custom_call" | custom-call | flops 6442450944 | bytes 18874368 | tf_op jit(solution)/shard_map/inner_operator/pallas_call | solution.py:292
  49.7 1.3 all-to-all-done.parts
  51.0 0.9 sum_gram.1
  51.9 9.0 %all-to-all-start.1 = ((f32[64,8,256]{2,1,0:T(8,128)}), f32[64,8,256]{2,1,0:T(8,128)S(1)}, u32[]{:S(2)}, u32[]{:S(2)}) async-start(f32[64,8,256]{2,1,0:T(8,128)} %sum_gram.1), calls=%async_computation.1 | async-start | bytes 1048576 | tf_op jit(solution)/shard_map/all_to_all | solution.py:487
  61.0 0.7 copy-done.1
  61.9 8.5 %outer_operator.1 = (f32[64,8,384]{2,1,0:T(8,128)S(1)}, f32[64,8,384]{2,1,0:T(8,128)S(1)}) custom-call(s32[1]{0:T(128)} %bitcast.core.side, f32[8,512,512]{2,1,0:T(8,128)} %bitcast.8, f32[2,512,512]{2,1,0:T(8,128)} %collective-permute-done.2.zlow, f32[2,512,512]{2,1,0:T(8,128)} %collective-permute-done.3.zhigh, f32[4,64,512]{2,1,0:T(8,128)} %copy-done.1, ...), custom_call_target="tpu_custom_call" | custom-call | flops 4026531840 | bytes 7340032 | tf_op jit(solution)/shard_map/outer_operator/pallas_call | solution.py:399
  70.4 2.8 %collective-permute-start.6 = (f32[64,8,384]{2,1,0:T(8,128)S(1)}, f32[64,8,384]{2,1,0:T(8,128)S(1)}, u32[]{:S(2)}, u32[]{:S(2)}) collective-permute-start(f32[64,8,384]{2,1,0:T(8,128)S(1)} %get-tuple-element.35), channel_id=1, source_target_pairs={{0,4},{4,0},{1,5},{5,1},{2,6},{6,2},{3,7},{7,3},{8,12},{12,8},{9,1... | collective-permute-start | bytes 2359304 | tf_op jit(solution)/shard_map/ppermute | solution.py:430
  73.2 2.4 %collective-permute-start.1 = (f32[64,8,256]{2,1,0:T(8,128)S(1)}, f32[64,8,256]{2,1,0:T(8,128)S(1)}, u32[]{:S(2)}, u32[]{:S(2)}) collective-permute-start(f32[64,8,256]{2,1,0:T(8,128)S(1)} %all-to-all-done.1.mine), channel_id=1, source_target_pairs={{0,4},{4,0},{1,5},{5,1},{2,6},{6,2},{3,7},{7,3},{8,12},{12,8},{9,1... | collective-permute-start | bytes 1572872 | tf_op jit(solution)/shard_map/ppermute | solution.py:430
  75.6 1.0 shard_map.103
  76.6 9.7 %all-to-all-start.2 = ((f32[64,8,384]{2,1,0:T(8,128)}), f32[64,8,384]{2,1,0:T(8,128)S(1)}, u32[]{:S(2)}, u32[]{:S(2)}) async-start(f32[64,8,384]{2,1,0:T(8,128)} %shard_map.103), calls=%async_computation.2 | async-start | bytes 1572864 | tf_op jit(solution)/shard_map/all_to_all | solution.py:447
  86.3 0.9 copy-done
  87.2 18.7 %bases.1 = (f32[128,512]{1,0:T(8,128)S(1)}, f32[128,512]{1,0:T(8,128)S(1)}, f32[128,512]{1,0:T(8,128)S(1)}) custom-call(s32[1]{0:T(128)} %bitcast.core.side, f32[64,8,256]{2,1,0:T(8,128)S(1)} %all-to-all-done.1.mine, f32[64,8,256]{2,1,0:T(8,128)S(1)} %collective-permute-done.1.theirs, f32[512,128]{1,0:T(8,128)S(1)} %copy-done), custom_call_target="tpu_custom_call" | custom-call | flops 20000000000 | bytes 4194304 | tf_op jit(solution)/shard_map/bases/pallas_call | solution.py:577
  105.9 0.3 project.1
  106.2 21.4 %all_to_all.20.mine = f32[64,8,256]{2,1,0:T(8,128)S(1)} all-to-all(f32[64,8,256]{2,1,0:T(8,128)S(1)} %project.1), channel_id=1, replica_groups=mesh['chip'=16,'core'=2,'sub'=4] {'chip','sub'}, dimensions={0} | all-to-all | bytes 1048576 | tf_op jit(solution)/shard_map/all_to_all | solution.py:487
  127.6 2.3 %collective-permute-start.7 = (f32[64,8,256]{2,1,0:T(8,128)S(1)}, f32[64,8,256]{2,1,0:T(8,128)S(1)}, u32[]{:S(2)}, u32[]{:S(2)}) collective-permute-start(f32[64,8,256]{2,1,0:T(8,128)S(1)} %all_to_all.20.mine), channel_id=1, source_target_pairs={{0,4},{4,0},{1,5},{5,1},{2,6},{6,2},{3,7},{7,3},{8,12},{12,8},{9,1... | collective-permute-start | bytes 1572872 | tf_op jit(solution)/shard_map/ppermute | solution.py:430
  130.6 0.9 collective-permute-done.7.theirs
  131.5 1.3 %finish.1 = (f32[128,128]{1,0:T(8,128)}, f32[128,128]{1,0:T(8,128)}, f32[4,128]{1,0:T(4,128)}, f32[4,128]{1,0:T(4,128)}) custom-call(s32[1]{0:T(128)S(6)} %copy.11.order, f32[128,512]{1,0:T(8,128)S(1)} %get-tuple-element.24.right, f32[128,512]{1,0:T(8,128)S(1)} %get-tuple-element.25.left, f32[128,512]{1,0:T(8,128)S(1)} %get-tuple-element.26.image, ...), custom_call_target="tpu_custom_call" | custom-call | flops 1000000000 | bytes 4194304 | tf_op jit(solution)/shard_map/finish/pallas_call | solution.py:611
  (14 shorter events, 0.5 us)
Async XLA Ops:
  11.5 49.5 %collective-permute-start.2 = (f32[2,512,512]{2,1,0:T(8,128)}, f32[2,512,512]{2,1,0:T(8,128)}, u32[]{:S(2)}, u32[]{:S(2)}) collective-permute-start(f32[2,512,512]{2,1,0:T(8,128)} %get-tuple-element.27), channel_id=1, source_target_pairs={{0,4},{4,8},{8,12},{12,16},{16,20},{20,24},{24,28},{28,32},{32,36}... | collective-permute-start | bytes 6291464 | tf_op jit(solution)/shard_map/ppermute | solution.py:633
  16.1 44.9 %collective-permute-start.3 = (f32[2,512,512]{2,1,0:T(8,128)}, f32[2,512,512]{2,1,0:T(8,128)}, u32[]{:S(2)}, u32[]{:S(2)}) collective-permute-start(f32[2,512,512]{2,1,0:T(8,128)} %get-tuple-element.28), channel_id=1, source_target_pairs={{4,0},{8,4},{12,8},{16,12},{20,16},{24,20},{28,24},{32,28},{36,32}... | collective-permute-start | bytes 6291464 | tf_op jit(solution)/shard_map/ppermute | solution.py:633
  18.0 4.7 %collective-permute-start = (f32[64,8,256]{2,1,0:T(8,128)S(1)}, f32[64,8,256]{2,1,0:T(8,128)S(1)}, u32[]{:S(2)}, u32[]{:S(2)}) collective-permute-start(f32[64,8,256]{2,1,0:T(8,128)S(1)} %get-tuple-element.23), channel_id=1, source_target_pairs={{0,4},{4,0},{1,5},{5,1},{2,6},{6,2},{3,7},{7,3},{8,12},{12,8},{9,1... | collective-permute-start | bytes 1572872 | tf_op jit(solution)/shard_map/ppermute | solution.py:430
  18.1 42.8 %collective-permute-start.4 = (f32[4,64,512]{2,1,0:T(8,128)}, f32[4,64,512]{2,1,0:T(8,128)S(1)}, u32[]{:S(2)}, u32[]{:S(2)}) collective-permute-start(f32[4,64,512]{2,1,0:T(8,128)} %get-tuple-element.29), channel_id=1, source_target_pairs={{0,1},{1,2},{2,3},{4,5},{5,6},{6,7},{8,9},{9,10},{10,11},{12,13},{... | collective-permute-start | bytes 1572872 | tf_op jit(solution)/shard_map/ppermute | solution.py:633
  21.3 39.7 %collective-permute-start.5 = (f32[4,64,512]{2,1,0:T(8,128)}, f32[4,64,512]{2,1,0:T(8,128)S(1)}, u32[]{:S(2)}, u32[]{:S(2)}) collective-permute-start(f32[4,64,512]{2,1,0:T(8,128)} %get-tuple-element.30), channel_id=1, source_target_pairs={{1,0},{2,1},{3,2},{5,4},{6,5},{7,6},{9,8},{10,9},{11,10},{13,12},{... | collective-permute-start | bytes 1572872 | tf_op jit(solution)/shard_map/ppermute | solution.py:633
  23.6 27.4 %all-to-all-start = ((f32[64,8,256]{2,1,0:T(8,128)}), f32[64,8,256]{2,1,0:T(8,128)S(1)}, u32[]{:S(2)}, u32[]{:S(2)}) async-start(f32[64,8,256]{2,1,0:T(8,128)} %shard_map.102), calls=%async_computation | async-start | bytes 1048576 | tf_op jit(solution)/shard_map/all_to_all | solution.py:447
  51.9 21.3 %all-to-all-start.1 = ((f32[64,8,256]{2,1,0:T(8,128)}), f32[64,8,256]{2,1,0:T(8,128)S(1)}, u32[]{:S(2)}, u32[]{:S(2)}) async-start(f32[64,8,256]{2,1,0:T(8,128)} %sum_gram.1), calls=%async_computation.1 | async-start | bytes 1048576 | tf_op jit(solution)/shard_map/all_to_all | solution.py:487
  60.9 0.8 copy-start.1
  61.0 1.0 copy-start.2
  70.4 5.2 %collective-permute-start.6 = (f32[64,8,384]{2,1,0:T(8,128)S(1)}, f32[64,8,384]{2,1,0:T(8,128)S(1)}, u32[]{:S(2)}, u32[]{:S(2)}) collective-permute-start(f32[64,8,384]{2,1,0:T(8,128)S(1)} %get-tuple-element.35), channel_id=1, source_target_pairs={{0,4},{4,0},{1,5},{5,1},{2,6},{6,2},{3,7},{7,3},{8,12},{12,8},{9,1... | collective-permute-start | bytes 2359304 | tf_op jit(solution)/shard_map/ppermute | solution.py:430
  73.2 13.1 %collective-permute-start.1 = (f32[64,8,256]{2,1,0:T(8,128)S(1)}, f32[64,8,256]{2,1,0:T(8,128)S(1)}, u32[]{:S(2)}, u32[]{:S(2)}) collective-permute-start(f32[64,8,256]{2,1,0:T(8,128)S(1)} %all-to-all-done.1.mine), channel_id=1, source_target_pairs={{0,4},{4,0},{1,5},{5,1},{2,6},{6,2},{3,7},{7,3},{8,12},{12,8},{9,1... | collective-permute-start | bytes 1572872 | tf_op jit(solution)/shard_map/ppermute | solution.py:430
  76.6 29.4 %all-to-all-start.2 = ((f32[64,8,384]{2,1,0:T(8,128)}), f32[64,8,384]{2,1,0:T(8,128)S(1)}, u32[]{:S(2)}, u32[]{:S(2)}) async-start(f32[64,8,384]{2,1,0:T(8,128)} %shard_map.103), calls=%async_computation.2 | async-start | bytes 1572864 | tf_op jit(solution)/shard_map/all_to_all | solution.py:447
  86.3 1.0 copy-start
  127.6 3.9 %collective-permute-start.7 = (f32[64,8,256]{2,1,0:T(8,128)S(1)}, f32[64,8,256]{2,1,0:T(8,128)S(1)}, u32[]{:S(2)}, u32[]{:S(2)}) collective-permute-start(f32[64,8,256]{2,1,0:T(8,128)S(1)} %all_to_all.20.mine), channel_id=1, source_target_pairs={{0,4},{4,0},{1,5},{5,1},{2,6},{6,2},{3,7},{7,3},{8,12},{12,8},{9,1... | collective-permute-start | bytes 1572872 | tf_op jit(solution)/shard_map/ppermute | solution.py:430

commit v5 on v4

--- a/solution.py
+++ b/solution.py
@@ -13,7 +13,6 @@
 F32 = jnp.float32
 BF16 = jnp.bfloat16
 PANEL = 32
-AHEAD = 2
 
 
 def split2(x):
@@ -88,132 +87,14 @@
     return pltpu.with_memory_space_constraint(value, pltpu.HBM)
 
 
-def gram_kernel(
-    core, obs, ctrl, sense,
-    own, other, few_far, zlow, zhigh, ylow, yhigh,
-    obs_here, ctrl_here, total, extra, sense_here, obs_sems, ctrl_sems, z_sems, low_sems, high_sems, other_sems,
-):
-    steps, rows, _ = obs.shape
-    points = ylow.shape[1]
-
-    def copies(i):
-        return (
-            pltpu.make_async_copy(obs.at[i], obs_here.at[i], obs_sems.at[i]),
-            pltpu.make_async_copy(ctrl.at[i], ctrl_here.at[i], ctrl_sems.at[i]),
-        )
-
-    def z_copy(i):
-        source = ctrl_here.at[i if i < 2 else steps - 4 + i]
-        return pltpu.make_async_copy(source, (zlow if i < 2 else zhigh).at[i % 2], z_sems.at[i])
-
-    def low_copy(p):
-        source = ctrl_here.at[2 * p, pl.ds(0, points)]
-        return pltpu.make_async_copy(source, ylow.at[p], low_sems.at[p])
-
-    def high_copy(p):
-        source = ctrl_here.at[2 * p + 1, pl.ds(rows - points, points)]
-        return pltpu.make_async_copy(source, yhigh.at[p], high_sems.at[p])
-
-    sense_copy = pltpu.make_async_copy(sense, sense_here, other_sems.at[0])
-    for i in range(AHEAD):
-        for copy in copies(i):
-            copy.start()
-        if i == 0:
-            sense_copy.start()
-    total[...] = jnp.zeros_like(total)
-    extra[...] = jnp.zeros_like(extra)
-    sense_copy.wait()
-
-    @pl.loop(0, steps)
-    def _(i):
-        for copy in copies(i):
-            copy.wait()
-
-        @pl.when(i + AHEAD < steps)
-        def _():
-            for copy in copies(i + AHEAD):
-                copy.start()
-
-        for j in range(4):
-
-            @pl.when(i == (j if j < 2 else steps - 4 + j))
-            def _():
-                z_copy(j).start()
-
-        @pl.when(i % 2 == 0)
-        def _():
-            low_copy(i // 2).start()
-
-        @pl.when(i % 2 == 1)
-        def _():
-            high_copy(i // 2).start()
-
-        first = pl.multiple_of((i % 2) * rows, 128)
-        some = plane_rows(sense_here, i // 2, first, rows)
-        add_products(total, obs_here[i].T, ctrl_here[i], extra, some)
-
-    few_copy = pltpu.make_async_copy(extra, few_far, other_sems.at[0])
-    few_copy.start()
-    for slot, out in enumerate((own, other)):
-        out[...] = half_of(total, core[0] ^ slot).reshape(out.shape)
-    few_copy.wait()
-    for i in range(4):
-        z_copy(i).wait()
-    for p in range(steps // 2):
-        low_copy(p).wait()
-        high_copy(p).wait()
-
-
-def local_gram(observe, control, sense, points):
-    steps, rows, rank = observe.shape
-    anywhere = pl.BlockSpec(memory_space=pltpu.HBM)
-    vmem = pl.BlockSpec(memory_space=pltpu.VMEM)
-    face = pltpu.HBM((2, rows, rank), F32)
-    edge = pltpu.HBM((steps // 2, points, rank), F32)
-    return pl.pallas_call(
-        gram_kernel,
-        in_specs=[pl.BlockSpec(memory_space=pltpu.SMEM)] + [anywhere] * 3,
-        out_specs=[vmem] * 2 + [anywhere] * 5,
-        out_shape=[
-            jax.ShapeDtypeStruct((rank // 8, 8, rank // 2), F32),
-            jax.ShapeDtypeStruct((rank // 8, 8, rank // 2), F32),
-            pltpu.HBM((16, rank), F32),
-            face,
-            face,
-            edge,
-            edge,
-        ],
-        scratch_shapes=[
-            pltpu.VMEM((steps, rows, rank), F32),
-            pltpu.VMEM((steps, rows, rank), F32),
-            pltpu.VMEM((rank, rank), F32),
-            pltpu.VMEM((16, rank), F32),
-            pltpu.VMEM(sense.shape, F32),
-            pltpu.SemaphoreType.DMA((steps,)),
-            pltpu.SemaphoreType.DMA((steps,)),
-            pltpu.SemaphoreType.DMA((4,)),
-            pltpu.SemaphoreType.DMA((steps // 2,)),
-            pltpu.SemaphoreType.DMA((steps // 2,)),
-            pltpu.SemaphoreType.DMA((1,)),
-        ],
-        compiler_params=pltpu.CompilerParams(vmem_limit_bytes=36 << 20),
-        cost_estimate=pl.CostEstimate(
-            flops=6 * steps * rows * rank * rank, bytes_accessed=24 << 20, transcendentals=0
-        ),
-        name="local_gram",
-    )(core_index(), in_hbm(observe), in_hbm(control), in_hbm(sense))
-
-
-def inner_kernel(
-    points, obs_far, ctrl_far, conduct, drive,
-    total_far, extra_far, total, extra, obs, ctrl, conduct_here, drive_here, sems, obs_sems, ctrl_sems,
+def local_kernel(
+    points, core, obs_far, ctrl_far, sense, conduct, drive,
+    own, other, few_far, zlow, zhigh, ylow, yhigh, total_far, extra_far,
+    obs, ctrl, gram, few, total, extra, sense_here, conduct_here, drive_here,
+    obs_sems, ctrl_sems, z_sems, low_sems, high_sems, small_sems,
 ):
     steps, rows, rank = ctrl.shape
     planes = steps // 2
-    small = [
-        pltpu.make_async_copy(conduct, conduct_here, sems.at[0]),
-        pltpu.make_async_copy(drive, drive_here, sems.at[1]),
-    ]
 
     def ctrl_copy(i):
         return pltpu.make_async_copy(ctrl_far.at[i], ctrl.at[i], ctrl_sems.at[i])
@@ -221,6 +102,24 @@
     def obs_copy(i):
         return pltpu.make_async_copy(obs_far.at[i], obs.at[i], obs_sems.at[i])
 
+    def z_copy(i):
+        source = ctrl.at[i if i < 2 else steps - 4 + i]
+        return pltpu.make_async_copy(source, (zlow if i < 2 else zhigh).at[i % 2], z_sems.at[i])
+
+    def low_copy(p):
+        source = ctrl.at[2 * p, pl.ds(0, points)]
+        return pltpu.make_async_copy(source, ylow.at[p], low_sems.at[p])
+
+    def high_copy(p):
+        source = ctrl.at[2 * p + 1, pl.ds(rows - points, points)]
+        return pltpu.make_async_copy(source, yhigh.at[p], high_sems.at[p])
+
+    small = [
+        pltpu.make_async_copy(far, here, small_sems.at[i])
+        for i, (far, here) in enumerate(
+            ((sense, sense_here), (conduct, conduct_here), (drive, drive_here))
+        )
+    ]
     for i in (0, 1, 2):
         ctrl_copy(i).start()
     obs_copy(0).start()
@@ -228,12 +127,13 @@
         copy.start()
     ctrl_copy(3).start()
     obs_copy(1).start()
-    total[...] = jnp.zeros_like(total)
-    extra[...] = jnp.zeros_like(extra)
+    for ref in (gram, few, total, extra):
+        ref[...] = jnp.zeros_like(ref)
     for copy in small:
         copy.wait()
-    ctrl_copy(0).wait()
-    ctrl_copy(1).wait()
+    for i in range(2):
+        ctrl_copy(i).wait()
+        z_copy(i).start()
     empty = jnp.zeros((points, rank), F32)
 
     @pl.loop(0, planes)
@@ -242,6 +142,8 @@
         down = jnp.maximum(p - 1, 0)
         has_up = (p + 1 < planes).astype(F32)
         has_down = (p > 0).astype(F32)
+        low_copy(p).start()
+        high_copy(p).start()
         for half in range(2):
 
             @pl.when(p + 1 < planes)
@@ -256,8 +158,15 @@
             def _():
                 obs_copy(2 * p + 2 + half).start()
 
+            @pl.when(p + 2 == planes)
+            def _():
+                z_copy(2 + half).start()
+
             obs_copy(2 * p + half).wait()
+            near = obs[2 * p + half]
             center = ctrl[2 * p + half]
+            first = half * rows
+            add_products(gram, near.T, center, few, plane_rows(sense_here, p, first, rows))
             beside = has_up * ctrl[2 * up + half] + has_down * ctrl[2 * down + half]
             if half == 0:
                 before = empty
@@ -270,55 +179,68 @@
             place = lax.broadcasted_iota(jnp.int32, (rows, rank), 0) % points
             beside = beside + jnp.where(place > 0, pltpu.roll(center, 1, 0), 0.0)
             beside = beside + jnp.where(place < points - 1, pltpu.roll(center, rows - 1, 0), 0.0)
-            first = half * rows
             scale = conduct_here[pl.ds(p, 1), first : first + rows] * (1.0 / 6.0)
             applied = (beside - 6.0 * center).T * scale
-            some = plane_rows(drive_here, p, first, rows)
-            add_products(total, applied, obs[2 * p + half], extra, some)
+            add_products(total, applied, near, extra, plane_rows(drive_here, p, first, rows))
 
     results = [
-        pltpu.make_async_copy(total, total_far, sems.at[0]),
-        pltpu.make_async_copy(extra, extra_far, sems.at[1]),
+        pltpu.make_async_copy(here, far, small_sems.at[i])
+        for i, (here, far) in enumerate(((few, few_far), (total, total_far), (extra, extra_far)))
     ]
     for copy in results:
         copy.start()
+    for slot, out in enumerate((own, other)):
+        out[...] = half_of(gram, core[0] ^ slot).reshape(out.shape)
     for copy in results:
         copy.wait()
-
-
-def inner_operator(observe, control, conduct, drive, points):
-    steps, rows, rank = control.shape
+    for i in range(4):
+        z_copy(i).wait()
+    for p in range(planes):
+        low_copy(p).wait()
+        high_copy(p).wait()
+
+
+def local_products(observe, control, sense, conduct, drive, points):
+    steps, rows, rank = observe.shape
     anywhere = pl.BlockSpec(memory_space=pltpu.HBM)
+    vmem = pl.BlockSpec(memory_space=pltpu.VMEM)
+    chunks = jax.ShapeDtypeStruct((rank // 8, 8, rank // 2), F32)
+    few = pltpu.HBM((16, rank), F32)
+    face = pltpu.HBM((2, rows, rank), F32)
+    edge = pltpu.HBM((steps // 2, points, rank), F32)
     return pl.pallas_call(
-        functools.partial(inner_kernel, points),
-        in_specs=[anywhere] * 4,
-        out_specs=[anywhere] * 2,
-        out_shape=[
-            pltpu.HBM((rank, rank), F32),
-            pltpu.HBM((16, rank), F32),
-        ],
+        functools.partial(local_kernel, points),
+        in_specs=[pl.BlockSpec(memory_space=pltpu.SMEM)] + [anywhere] * 5,
+        out_specs=[vmem] * 2 + [anywhere] * 7,
+        out_shape=[chunks, chunks, few, face, face, edge, edge, pltpu.HBM((rank, rank), F32), few],
         scratch_shapes=[
+            pltpu.VMEM((steps, rows, rank), F32),
+            pltpu.VMEM((steps, rows, rank), F32),
             pltpu.VMEM((rank, rank), F32),
             pltpu.VMEM((16, rank), F32),
-            pltpu.VMEM((steps, rows, rank), F32),
-            pltpu.VMEM((steps, rows, rank), F32),
+            pltpu.VMEM((rank, rank), F32),
+            pltpu.VMEM((16, rank), F32),
+            pltpu.VMEM(sense.shape, F32),
             pltpu.VMEM(conduct.shape, F32),
             pltpu.VMEM(drive.shape, F32),
-            pltpu.SemaphoreType.DMA((2,)),
             pltpu.SemaphoreType.DMA((steps,)),
             pltpu.SemaphoreType.DMA((steps,)),
+            pltpu.SemaphoreType.DMA((4,)),
+            pltpu.SemaphoreType.DMA((steps // 2,)),
+            pltpu.SemaphoreType.DMA((steps // 2,)),
+            pltpu.SemaphoreType.DMA((3,)),
         ],
-        compiler_params=pltpu.CompilerParams(vmem_limit_bytes=36 << 20),
+        compiler_params=pltpu.CompilerParams(vmem_limit_bytes=44 << 20),
         cost_estimate=pl.CostEstimate(
-            flops=6 * steps * rows * rank * rank, bytes_accessed=18 << 20, transcendentals=0
+            flops=12 * steps * rows * rank * rank, bytes_accessed=26 << 20, transcendentals=0
         ),
-        name="inner_operator",
-    )(in_hbm(observe), in_hbm(control), in_hbm(conduct), in_hbm(drive))
+        name="local_products",
+    )(core_index(), *map(in_hbm, (observe, control, sense, conduct, drive)))
 
 
 def outer_kernel(
-    points, core, obs, zlow, zhigh, ylow, yhigh, conduct, inner, extra_far, few_far,
-    own, other, z_field, y_field, z_obs, y_obs, conduct_here, total, extra, few_ctrl, sems, obs_sems,
+    points, obs, zlow, zhigh, ylow, yhigh, conduct, inner, extra_far, few_far,
+    out, z_field, y_field, z_obs, y_obs, conduct_here, total, extra, few_ctrl, sems, obs_sems,
 ):
     steps, rows, rank = obs.shape
     planes = steps // 2
@@ -385,11 +307,11 @@
     summed = jnp.concatenate([extra[0:4] + extra[4:8], few_ctrl[0:4] + few_ctrl[4:8]], axis=0)
     wide = jnp.concatenate([summed, jnp.zeros((120, rank), F32)], axis=0).T
     width = rank // 2
-    for slot, out in enumerate((own, other)):
-        side = core[0] ^ slot
-        out[:, :, :width] = half_of(total, side).reshape(out.shape[0], out.shape[1], width)
-        part = wide * (side == 0).astype(F32)
-        out[:, :, width:] = part.reshape(out.shape[0], out.shape[1], 128)
+    for side in range(2):
+        cols = total[:, side * width : (side + 1) * width]
+        out[:, side, :, :width] = cols.reshape(out.shape[0], out.shape[2], width)
+    out[:, 0, :, width:] = wide.reshape(out.shape[0], out.shape[2], 128)
+    out[:, 1, :, width:] = jnp.zeros((out.shape[0], out.shape[2], 128), F32)
 
 
 def with_outer(observe, faces, conduct, inner, extra, few_ctrl, points):
@@ -398,9 +320,9 @@
     vmem = pl.BlockSpec(memory_space=pltpu.VMEM)
     return pl.pallas_call(
         functools.partial(outer_kernel, points),
-        in_specs=[pl.BlockSpec(memory_space=pltpu.SMEM)] + [anywhere] * 9,
-        out_specs=[vmem] * 2,
-        out_shape=[jax.ShapeDtypeStruct((rank // 8, 8, rank // 2 + 128), F32)] * 2,
+        in_specs=[anywhere] * 9,
+        out_specs=vmem,
+        out_shape=jax.ShapeDtypeStruct((rank // 8, 2, 8, rank // 2 + 128), F32),
         scratch_shapes=[
             pltpu.VMEM((4, rows, rank), F32),
             pltpu.VMEM((2, steps // 2, points, rank), F32),
@@ -418,7 +340,7 @@
             flops=30 * rows * rank * rank, bytes_accessed=7 << 20, transcendentals=0
         ),
         name="outer_operator",
-    )(core_index(), *map(in_hbm, (observe, *faces, conduct, inner, extra, few_ctrl)))
+    )(*map(in_hbm, (observe, *faces, conduct, inner, extra, few_ctrl)))
 
 
 def sum_kernel(parts, out):
@@ -474,7 +396,7 @@
         project_kernel,
         in_specs=[pl.BlockSpec(memory_space=pltpu.SMEM), vmem, vmem],
         out_specs=vmem,
-        out_shape=jax.ShapeDtypeStruct((arrived.shape[0], 8, 256), F32),
+        out_shape=jax.ShapeDtypeStruct((arrived.shape[0] // 2, 8, 256), F32),
         compiler_params=pltpu.CompilerParams(vmem_limit_bytes=8 << 20),
         cost_estimate=pl.CostEstimate(
             flops=arrived.size, bytes_accessed=8 * arrived.size, transcendentals=0
@@ -534,13 +456,19 @@
             work[last:, :] -= change[last:, :]
 
 
-def bases_kernel(core, mine, theirs, start, right_out, left_out, image_out, high, low, basis, work):
+def bases_kernel(
+    core, mine, theirs, start, right_out, left_out, image_out,
+    high, low, basis, work, first, sem,
+):
+    copy = pltpu.make_async_copy(start, first, sem.at[0])
+    copy.start()
     rank = high.shape[0]
     half = rank // 2
     for slot, part in enumerate((mine, theirs)):
         place = pl.ds(pl.multiple_of((core[0] ^ slot) * half, 128), half)
         high[:, place], low[:, place] = split2(part[...].reshape(rank, half))
-    basis[...] = start[...].T
+    copy.wait()
+    basis[...] = first[...].T
     size = basis.shape[0]
     eye = (
         lax.broadcasted_iota(jnp.int32, (size, size), 0)
@@ -576,20 +504,27 @@
     vmem = pl.BlockSpec(memory_space=pltpu.VMEM)
     return pl.pallas_call(
         bases_kernel,
-        in_specs=[pl.BlockSpec(memory_space=pltpu.SMEM)] + [vmem] * 3,
+        in_specs=[
+            pl.BlockSpec(memory_space=pltpu.SMEM),
+            vmem,
+            vmem,
+            pl.BlockSpec(memory_space=pltpu.HBM),
+        ],
         out_shape=[shape, shape, shape],
         scratch_shapes=[
             pltpu.VMEM((rank, rank), BF16),
             pltpu.VMEM((rank, rank), BF16),
             pltpu.VMEM((size, rank), F32),
             pltpu.VMEM((size, 2 * size), F32),
+            pltpu.VMEM((rank, size), F32),
+            pltpu.SemaphoreType.DMA((1,)),
         ],
         compiler_params=pltpu.CompilerParams(vmem_limit_bytes=16 << 20),
         cost_estimate=pl.CostEstimate(
             flops=20_000_000_000, bytes_accessed=4 << 20, transcendentals=0
         ),
         name="bases",
-    )(core_index(), mine, theirs, start)
+    )(core_index(), mine, theirs, in_hbm(start))
 
 
 def finish_kernel(order, right, left, image, mine, theirs, mass, state, inputs, outputs):
@@ -637,18 +572,17 @@
     planes, lines, points, rank = factor_ctrl.shape
     halves = (2 * planes, lines * points // 2, rank)
     observe = factor_obs.reshape(halves)
-    control = factor_ctrl.reshape(halves)
-    own, other, few_ctrl, zlow, zhigh, ylow, yhigh = local_gram(
-        observe, control, output_map, points
+    own, other, few_ctrl, zlow, zhigh, ylow, yhigh, inner, extra = local_products(
+        observe, factor_ctrl.reshape(halves), output_map, diffusivity, input_map, points
     )
     arrived = scattered(own, other)
     zlow, zhigh = from_neighbours(zlow, zhigh, ("chip", "core"))
     ylow, yhigh = from_neighbours(ylow, yhigh, "sub")
-    inner, extra = inner_operator(observe, control, diffusivity, input_map, points)
     gram = gathered(summed_copies(arrived))
     faces = (zlow, zhigh, ylow, yhigh)
-    own, other = with_outer(observe, faces, diffusivity, inner, extra, few_ctrl, points)
-    oper = scattered(own, other)
+    oper = with_outer(observe, faces, diffusivity, inner, extra, few_ctrl, points)
+    tiles = oper.reshape(-1, *oper.shape[2:])
+    oper = lax.all_to_all(tiles, CHIPS + ("core",), 0, 0, tiled=True)
     right, left, image = bases(*gram, start_block)
     blocks = gathered(projected_copies(oper, left))
     mass, state, inputs, outputs = finish(order, right, left, image, *blocks)

time: 133 us -> 158 us (1.19)
  blocking collectives: 21.4 us -> 45.5 us
  waiting for transfers between devices: 2.34 us -> 17.7 us
  starting transfers between devices: 49.6 us -> 38.9 us
  Pallas kernels: 56.1 us -> 52.7 us
    all_to_all x0 -> x1, blocking collectives: none -> 28.2 us  [scattered(): return lax.all_to_all(both, CHIPS, 0, 0, tiled=True)]
    all_to_all x2 -> x1, starting transfers between devices: 22 us -> 10.7 us  [reduced(): oper = lax.all_to_all(tiles, CHIPS + ('core',), 0, 0, tiled=True)]
    all_to_all x1, waiting for transfers between devices: 0.01 us -> 6.75 us  [gathered(): mine = lax.all_to_all(copies, CHIPS, 0, 0, tiled=True)]
    ppermute x4 -> x3, waiting for transfers between devices: 1.07 us -> 5.52 us  [swapped(): return lax.ppermute(value, 'core', [(0, 1), (1, 0)])]
    all_to_all x2 -> x1, waiting for transfers between devices: 1.26 us -> 5.39 us  [reduced(): oper = lax.all_to_all(tiles, CHIPS + ('core',), 0, 0, tiled=True)]
    all_to_all x1, blocking collectives: 21.4 us -> 17.4 us  [gathered(): mine = lax.all_to_all(copies, CHIPS, 0, 0, tiled=True)]
    pallas_call x3 -> x2, Pallas kernels: 33.1 us -> 30.6 us  [the longest x1 21.3 us: local_products(): pl.pallas_call(functools.partial(local_kernel, points), in_specs=[pl.Bloc...]
    pallas_call x2 -> x1, Pallas kernels: 1.8 us -> 0.05 us  [scattered(): pl.pallas_call(add_kernel, out_shape=jax.ShapeDtypeStruct(own.shape, F32)...]
  transfers between devices with their start and end apart: 11 -> 9, of which waited for: 3 -> 4; matrix products, arithmetic and copies ran while one was open for 0% -> 0% of each run, Pallas kernels for 33% -> 19%
where the time goes in v5:
time: 158 us; the launch traced here: 157 us
  Pallas kernels  52.7 us (33%)
  blocking collectives  45.5 us (29%)
  starting transfers between devices  38.9 us (25%)
  waiting for transfers between devices  17.7 us (11%)
    all_to_all x1, blocking collectives, scattered(): return lax.all_to_all(both, CHIPS, 0, 0, tiled=True)  28.2 us
    pallas_call x1, Pallas kernels, local_products(): pl.pallas_call(functools.partial(local_kernel, points), in_specs=[pl.Bloc...  21.3 us
    pallas_call x1, Pallas kernels, bases(): pl.pallas_call(bases_kernel, in_specs=[pl.BlockSpec(memory_space=pltpu.SM...  19.4 us
    all_to_all x1, blocking collectives, gathered(): mine = lax.all_to_all(copies, CHIPS, 0, 0, tiled=True)  17.4 us
    all_to_all x1, starting transfers between devices, reduced(): oper = lax.all_to_all(tiles, CHIPS + ('core',), 0, 0, tiled=True)  10.7 us
    pallas_call x1, Pallas kernels, with_outer(): pl.pallas_call(functools.partial(outer_kernel, points), in_specs=[anywher...  9.34 us
    ppermute x3, starting transfers between devices, swapped(): return lax.ppermute(value, 'core', [(0, 1), (1, 0)])  8.75 us
    all_to_all x1, starting transfers between devices, gathered(): mine = lax.all_to_all(copies, CHIPS, 0, 0, tiled=True)  8.73 us
  transfers between devices with their start and end apart: 9, of which 4 were waited for; matrix products, arithmetic and copies ran while one was open for 0% of the time, Pallas kernels for 19%

profile of v5, /device:TPU:1, one launch (start us, length us, event | category | flops | bytes accessed | tf_op | source)
XLA Modules:
  0.0 157.1 jit_solution(215322051650481123)
XLA Ops:
  0.6 21.3 %local_products.1 = (f32[64,8,256]{2,1,0:T(8,128)S(1)}, f32[64,8,256]{2,1,0:T(8,128)S(1)}, f32[16,512]{1,0:T(8,128)}, f32[2,512,512]{2,1,0:T(8,128)}, f32[2,512,...) custom-call(s32[1]{0:T(128)} %bitcast.core.side, ...), custom_call_target="tpu_custom_call" | custom-call | flops 12884901888 | bytes 27262976 | tf_op jit(solution)/shard_map/local_products/pallas_call | solution.py:211
  21.9 4.6 %collective-permute-start.2 = (f32[2,512,512]{2,1,0:T(8,128)}, f32[2,512,512]{2,1,0:T(8,128)}, u32[]{:S(2)}, u32[]{:S(2)}) collective-permute-start(f32[2,512,512]{2,1,0:T(8,128)} %get-tuple-element.25), channel_id=1, source_target_pairs={{0,4},{4,8},{8,12},{12,16},{16,20},{20,24},{24,28},{28,32},{32,36}... | collective-permute-start | bytes 6291464 | tf_op jit(solution)/shard_map/ppermute | solution.py:568
  26.5 1.9 %collective-permute-start.3 = (f32[2,512,512]{2,1,0:T(8,128)}, f32[2,512,512]{2,1,0:T(8,128)}, u32[]{:S(2)}, u32[]{:S(2)}) collective-permute-start(f32[2,512,512]{2,1,0:T(8,128)} %get-tuple-element.26), channel_id=1, source_target_pairs={{4,0},{8,4},{12,8},{16,12},{20,16},{24,20},{28,24},{32,28},{36,32}... | collective-permute-start | bytes 6291464 | tf_op jit(solution)/shard_map/ppermute | solution.py:568
  28.4 0.1 collective-permute-start
  28.5 4.6 %collective-permute-done.second = f32[64,8,256]{2,1,0:T(8,128)S(1)} collective-permute-done((f32[64,8,256]{2,1,0:T(8,128)S(1)}, f32[64,8,256]{2,1,0:T(8,128)S(1)}, u32[]{:S(2)}, u32[]{:S(2)}) %collective-permute-start) | collective-permute-done | bytes 524320 | tf_op jit(solution)/shard_map/ppermute | solution.py:352
  33.2 0.1 shard_map.102
  33.2 28.2 %all_to_all.20.parts = f32[64,8,256]{2,1,0:T(8,128)S(1)} all-to-all(f32[64,8,256]{2,1,0:T(8,128)S(1)} %shard_map.102), channel_id=1, replica_groups=mesh['chip'=16,'core'=2,'sub'=4] {'chip','sub'}, dimensions={0} | all-to-all | bytes 1048576 | tf_op jit(solution)/shard_map/all_to_all | solution.py:369
  61.4 0.9 sum_gram.1
  62.3 8.7 %all-to-all-start.1 = ((f32[64,8,256]{2,1,0:T(8,128)}), f32[64,8,256]{2,1,0:T(8,128)S(1)}, u32[]{:S(2)}, u32[]{:S(2)}) async-start(f32[64,8,256]{2,1,0:T(8,128)} %sum_gram.1), calls=%async_computation.1 | async-start | bytes 1048576 | tf_op jit(solution)/shard_map/all_to_all | solution.py:409
  71.0 2.9 %collective-permute-start.4 = (f32[4,64,512]{2,1,0:T(8,128)S(1)}, f32[4,64,512]{2,1,0:T(8,128)S(1)}, u32[]{:S(2)}, u32[]{:S(2)}) collective-permute-start(f32[4,64,512]{2,1,0:T(8,128)S(1)} %copy-done.3), channel_id=1, source_target_pairs={{0,1},{1,2},{2,3},{4,5},{5,6},{6,7},{8,9},{9,10},{10,11},{12,13},{... | collective-permute-start | bytes 1572872 | tf_op jit(solution)/shard_map/ppermute | solution.py:568
  74.0 1.3 collective-permute-start.5
  75.3 6.7 %all-to-all-done.1.mine = f32[64,8,256]{2,1,0:T(8,128)S(1)} async-done(((f32[64,8,256]{2,1,0:T(8,128)}), f32[64,8,256]{2,1,0:T(8,128)S(1)}, u32[]{:S(2)}, u32[]{:S(2)}) %all-to-all-start.1) | async-done | bytes 524320 | tf_op jit(solution)/shard_map/all_to_all | solution.py:409
  82.0 6.8 %collective-permute-start.1 = (f32[64,8,256]{2,1,0:T(8,128)S(1)}, f32[64,8,256]{2,1,0:T(8,128)S(1)}, u32[]{:S(2)}, u32[]{:S(2)}) collective-permute-start(f32[64,8,256]{2,1,0:T(8,128)S(1)} %all-to-all-done.1.mine), channel_id=1, source_target_pairs={{0,4},{4,0},{1,5},{5,1},{2,6},{6,2},{3,7},{7,3},{8,12},{12,8},{9,1... | collective-permute-start | bytes 1572872 | tf_op jit(solution)/shard_map/ppermute | solution.py:352
  88.9 0.8 copy-done
  89.6 0.2 copy-done.1
  89.8 9.3 %outer_operator.1 = f32[64,2,8,384]{3,2,1,0:T(8,128)} custom-call(f32[8,512,512]{2,1,0:T(8,128)} %bitcast.6, f32[2,512,512]{2,1,0:T(8,128)} %collective-permute-done.2.zlow, f32[2,512,512]{2,1,0:T(8,128)} %collective-permute-done.3.zhigh, f32[4,64,512]{2,1,0:T(8,128)} %copy-done, f32[4,64,512]{2,1,0:T(8,128)} %copy-done.1, f32[4,1024]{1,0:T(4,128)} %conduct.3, ...), custom_call_target="tpu_custom_call" | custom-call | flops 4026531840 | bytes 7340032 | tf_op jit(solution)/shard_map/outer_operator/pallas_call | solution.py:321
  99.1 10.7 %all-to-all-start.2 = ((f32[128,8,384]{2,1,0:T(8,128)}), f32[128,8,384]{2,1,0:T(8,128)S(1)}, u32[]{:S(2)}, u32[]{:S(2)}) async-start(f32[128,8,384]{2,1,0:T(8,128)} %bitcast.3), calls=%async_computation.2 | async-start | bytes 3145728 | tf_op jit(solution)/shard_map/all_to_all | solution.py:585
  109.8 19.4 %bases.1 = (f32[128,512]{1,0:T(8,128)S(1)}, f32[128,512]{1,0:T(8,128)S(1)}, f32[128,512]{1,0:T(8,128)S(1)}) custom-call(s32[1]{0:T(128)} %bitcast.core.side, f32[64,8,256]{2,1,0:T(8,128)S(1)} %all-to-all-done.1.mine, f32[64,8,256]{2,1,0:T(8,128)S(1)} %collective-permute-done.1.theirs, f32[512,128]{1,0:T(8,128)} %start.1), custom_call_target="tpu_custom_call" | custom-call | flops 20000000000 | bytes 4194304 | tf_op jit(solution)/shard_map/bases/pallas_call | solution.py:505
  129.3 5.4 %all-to-all-done.2.parts = f32[128,8,384]{2,1,0:T(8,128)S(1)} async-done(((f32[128,8,384]{2,1,0:T(8,128)}), f32[128,8,384]{2,1,0:T(8,128)S(1)}, u32[]{:S(2)}, u32[]{:S(2)}) %all-to-all-start.2) | async-done | bytes 1572896 | tf_op jit(solution)/shard_map/all_to_all | solution.py:585
  134.7 0.3 project.1
  135.0 17.4 %all_to_all.21.mine = f32[64,8,256]{2,1,0:T(8,128)S(1)} all-to-all(f32[64,8,256]{2,1,0:T(8,128)S(1)} %project.1), channel_id=1, replica_groups=mesh['chip'=16,'core'=2,'sub'=4] {'chip','sub'}, dimensions={0} | all-to-all | bytes 1048576 | tf_op jit(solution)/shard_map/all_to_all | solution.py:409
  152.4 1.9 %collective-permute-start.6 = (f32[64,8,256]{2,1,0:T(8,128)S(1)}, f32[64,8,256]{2,1,0:T(8,128)S(1)}, u32[]{:S(2)}, u32[]{:S(2)}) collective-permute-start(f32[64,8,256]{2,1,0:T(8,128)S(1)} %all_to_all.21.mine), channel_id=1, source_target_pairs={{0,4},{4,0},{1,5},{5,1},{2,6},{6,2},{3,7},{7,3},{8,12},{12,8},{9,1... | collective-permute-start | bytes 1572872 | tf_op jit(solution)/shard_map/ppermute | solution.py:352
  154.9 0.9 collective-permute-done.6.theirs
  155.8 1.3 finish.1
  (11 shorter events, 0.0 us)
Async XLA Ops:
  21.9 66.9 %collective-permute-start.2 = (f32[2,512,512]{2,1,0:T(8,128)}, f32[2,512,512]{2,1,0:T(8,128)}, u32[]{:S(2)}, u32[]{:S(2)}) collective-permute-start(f32[2,512,512]{2,1,0:T(8,128)} %get-tuple-element.25), channel_id=1, source_target_pairs={{0,4},{4,8},{8,12},{12,16},{16,20},{20,24},{24,28},{28,32},{32,36}... | collective-permute-start | bytes 6291464 | tf_op jit(solution)/shard_map/ppermute | solution.py:568
  26.5 62.3 %collective-permute-start.3 = (f32[2,512,512]{2,1,0:T(8,128)}, f32[2,512,512]{2,1,0:T(8,128)}, u32[]{:S(2)}, u32[]{:S(2)}) collective-permute-start(f32[2,512,512]{2,1,0:T(8,128)} %get-tuple-element.26), channel_id=1, source_target_pairs={{4,0},{8,4},{12,8},{16,12},{20,16},{24,20},{28,24},{32,28},{36,32}... | collective-permute-start | bytes 6291464 | tf_op jit(solution)/shard_map/ppermute | solution.py:568
  28.4 4.7 %collective-permute-start = (f32[64,8,256]{2,1,0:T(8,128)S(1)}, f32[64,8,256]{2,1,0:T(8,128)S(1)}, u32[]{:S(2)}, u32[]{:S(2)}) collective-permute-start(f32[64,8,256]{2,1,0:T(8,128)S(1)} %get-tuple-element.21), channel_id=1, source_target_pairs={{0,4},{4,0},{1,5},{5,1},{2,6},{6,2},{3,7},{7,3},{8,12},{12,8},{9,1... | collective-permute-start | bytes 1572872 | tf_op jit(solution)/shard_map/ppermute | solution.py:352
  33.2 37.9 %copy-start.3 = (f32[4,64,512]{2,1,0:T(8,128)S(1)}, f32[4,64,512]{2,1,0:T(8,128)}, u32[]{:S(2)}) copy-start(f32[4,64,512]{2,1,0:T(8,128)} %get-tuple-element.27) | copy-start | bytes 1572868
  33.2 40.8 %copy-start.2 = (f32[4,64,512]{2,1,0:T(8,128)S(1)}, f32[4,64,512]{2,1,0:T(8,128)}, u32[]{:S(2)}) copy-start(f32[4,64,512]{2,1,0:T(8,128)} %get-tuple-element.28) | copy-start | bytes 1572868
  62.3 19.8 %all-to-all-start.1 = ((f32[64,8,256]{2,1,0:T(8,128)}), f32[64,8,256]{2,1,0:T(8,128)S(1)}, u32[]{:S(2)}, u32[]{:S(2)}) async-start(f32[64,8,256]{2,1,0:T(8,128)} %sum_gram.1), calls=%async_computation.1 | async-start | bytes 1048576 | tf_op jit(solution)/shard_map/all_to_all | solution.py:409
  71.0 17.8 %collective-permute-start.4 = (f32[4,64,512]{2,1,0:T(8,128)S(1)}, f32[4,64,512]{2,1,0:T(8,128)S(1)}, u32[]{:S(2)}, u32[]{:S(2)}) collective-permute-start(f32[4,64,512]{2,1,0:T(8,128)S(1)} %copy-done.3), channel_id=1, source_target_pairs={{0,1},{1,2},{2,3},{4,5},{5,6},{6,7},{8,9},{9,10},{10,11},{12,13},{... | collective-permute-start | bytes 1572872 | tf_op jit(solution)/shard_map/ppermute | solution.py:568
  74.0 14.8 %collective-permute-start.5 = (f32[4,64,512]{2,1,0:T(8,128)S(1)}, f32[4,64,512]{2,1,0:T(8,128)S(1)}, u32[]{:S(2)}, u32[]{:S(2)}) collective-permute-start(f32[4,64,512]{2,1,0:T(8,128)S(1)} %copy-done.2), channel_id=1, source_target_pairs={{1,0},{2,1},{3,2},{5,4},{6,5},{7,6},{9,8},{10,9},{11,10},{13,12},{... | collective-permute-start | bytes 1572872 | tf_op jit(solution)/shard_map/ppermute | solution.py:568
  82.0 27.8 %collective-permute-start.1 = (f32[64,8,256]{2,1,0:T(8,128)S(1)}, f32[64,8,256]{2,1,0:T(8,128)S(1)}, u32[]{:S(2)}, u32[]{:S(2)}) collective-permute-start(f32[64,8,256]{2,1,0:T(8,128)S(1)} %all-to-all-done.1.mine), channel_id=1, source_target_pairs={{0,4},{4,0},{1,5},{5,1},{2,6},{6,2},{3,7},{7,3},{8,12},{12,8},{9,1... | collective-permute-start | bytes 1572872 | tf_op jit(solution)/shard_map/ppermute | solution.py:352
  88.8 0.8 copy-start
  88.8 1.0 copy-start.1
  99.1 35.5 %all-to-all-start.2 = ((f32[128,8,384]{2,1,0:T(8,128)}), f32[128,8,384]{2,1,0:T(8,128)S(1)}, u32[]{:S(2)}, u32[]{:S(2)}) async-start(f32[128,8,384]{2,1,0:T(8,128)} %bitcast.3), calls=%async_computation.2 | async-start | bytes 3145728 | tf_op jit(solution)/shard_map/all_to_all | solution.py:585
  152.4 3.4 %collective-permute-start.6 = (f32[64,8,256]{2,1,0:T(8,128)S(1)}, f32[64,8,256]{2,1,0:T(8,128)S(1)}, u32[]{:S(2)}, u32[]{:S(2)}) collective-permute-start(f32[64,8,256]{2,1,0:T(8,128)S(1)} %all_to_all.21.mine), channel_id=1, source_target_pairs={{0,4},{4,0},{1,5},{5,1},{2,6},{6,2},{3,7},{7,3},{8,12},{12,8},{9,1... | collective-permute-start | bytes 1572872 | tf_op jit(solution)/shard_map/ppermute | solution.py:352

commit v6 on v4

--- a/solution.py
+++ b/solution.py
@@ -209,7 +209,6 @@
     total_far, extra_far, total, extra, obs, ctrl, conduct_here, drive_here, sems, obs_sems, ctrl_sems,
 ):
     steps, rows, rank = ctrl.shape
-    planes = steps // 2
     small = [
         pltpu.make_async_copy(conduct, conduct_here, sems.at[0]),
         pltpu.make_async_copy(drive, drive_here, sems.at[1]),
@@ -234,47 +233,35 @@
         copy.wait()
     ctrl_copy(0).wait()
     ctrl_copy(1).wait()
-    empty = jnp.zeros((points, rank), F32)
-
-    @pl.loop(0, planes)
-    def _(p):
-        up = jnp.minimum(p + 1, planes - 1)
-        down = jnp.maximum(p - 1, 0)
-        has_up = (p + 1 < planes).astype(F32)
-        has_down = (p > 0).astype(F32)
-        for half in range(2):
-
-            @pl.when(p + 1 < planes)
-            def _():
-                ctrl_copy(2 * p + 2 + half).wait()
-
-            @pl.when(p + 2 < planes)
-            def _():
-                ctrl_copy(2 * p + 4 + half).start()
-
-            @pl.when(p + 1 < planes)
-            def _():
-                obs_copy(2 * p + 2 + half).start()
-
-            obs_copy(2 * p + half).wait()
-            center = ctrl[2 * p + half]
-            beside = has_up * ctrl[2 * up + half] + has_down * ctrl[2 * down + half]
-            if half == 0:
-                before = empty
-                after = ctrl[2 * p + 1, :points]
-            else:
-                before = ctrl[2 * p, rows - points :]
-                after = empty
-            beside = beside + jnp.concatenate([before, center[: rows - points]], axis=0)
-            beside = beside + jnp.concatenate([center[points:], after], axis=0)
-            place = lax.broadcasted_iota(jnp.int32, (rows, rank), 0) % points
-            beside = beside + jnp.where(place > 0, pltpu.roll(center, 1, 0), 0.0)
-            beside = beside + jnp.where(place < points - 1, pltpu.roll(center, rows - 1, 0), 0.0)
-            first = half * rows
-            scale = conduct_here[pl.ds(p, 1), first : first + rows] * (1.0 / 6.0)
-            applied = (beside - 6.0 * center).T * scale
-            some = plane_rows(drive_here, p, first, rows)
-            add_products(total, applied, obs[2 * p + half], extra, some)
+
+    @pl.loop(0, steps)
+    def _(i):
+        @pl.when(i + 2 < steps)
+        def _():
+            ctrl_copy(i + 2).wait()
+            obs_copy(i + 2).start()
+
+        @pl.when(i + 4 < steps)
+        def _():
+            ctrl_copy(i + 4).start()
+
+        obs_copy(i).wait()
+        half = i % 2
+        center = ctrl[i]
+        beside = (i + 2 < steps).astype(F32) * ctrl[jnp.minimum(i + 2, steps - 1)]
+        beside = beside + (i >= 2).astype(F32) * ctrl[jnp.maximum(i - 2, 0)]
+        before = half.astype(F32) * ctrl[jnp.maximum(i - 1, 0), rows - points :]
+        after = (1 - half).astype(F32) * ctrl[jnp.minimum(i + 1, steps - 1), :points]
+        beside = beside + jnp.concatenate([before, center[: rows - points]], axis=0)
+        beside = beside + jnp.concatenate([center[points:], after], axis=0)
+        place = lax.broadcasted_iota(jnp.int32, (rows, rank), 0) % points
+        beside = beside + jnp.where(place > 0, pltpu.roll(center, 1, 0), 0.0)
+        beside = beside + jnp.where(place < points - 1, pltpu.roll(center, rows - 1, 0), 0.0)
+        first = pl.multiple_of(half * rows, 128)
+        scale = conduct_here[pl.ds(i // 2, 1), pl.ds(first, rows)] * (1.0 / 6.0)
+        applied = (beside - 6.0 * center).T * scale
+        some = plane_rows(drive_here, i // 2, first, rows)
+        add_products(total, applied, obs[i], extra, some)
 
     results = [
         pltpu.make_async_copy(total, total_far, sems.at[0]),
@@ -317,8 +304,8 @@
 
 
 def outer_kernel(
-    points, core, obs, zlow, zhigh, ylow, yhigh, conduct, inner, extra_far, few_far,
-    own, other, z_field, y_field, z_obs, y_obs, conduct_here, total, extra, few_ctrl, sems, obs_sems,
+    points, obs, zlow, zhigh, ylow, yhigh, conduct, inner, extra_far, few_far,
+    out, z_field, y_field, z_obs, y_obs, conduct_here, total, extra, few_ctrl, sems, obs_sems,
 ):
     steps, rows, rank = obs.shape
     planes = steps // 2
@@ -331,65 +318,68 @@
     y_near = [
         pltpu.make_async_copy(
             obs.at[2 * p + i, pl.ds(i * (rows - points), points)],
-            y_obs.at[i, pl.ds(p * points, points)],
+            y_obs.at[pl.ds((planes * i + p) * points, points)],
             obs_sems.at[4 + planes * i + p],
         )
         for i in range(2)
         for p in range(planes)
     ]
-    z_near = [
-        pltpu.make_async_copy(
-            obs.at[i if i < 2 else steps - 4 + i], z_obs.at[i], obs_sems.at[i]
-        )
-        for i in range(4)
-    ]
     y_copies = [
         pltpu.make_async_copy(ylow, y_field.at[0], sems.at[1]),
         pltpu.make_async_copy(yhigh, y_field.at[1], sems.at[2]),
     ]
-    z_copies = [
-        pltpu.make_async_copy(face.at[half], z_field.at[2 * i + half], sems.at[3 + 2 * i + half])
-        for i, face in enumerate((zlow, zhigh))
-        for half in range(2)
-    ]
+
+    def z_far(i):
+        face = zlow if i < 2 else zhigh
+        return pltpu.make_async_copy(face.at[i % 2], z_field.at[i], sems.at[3 + i])
+
+    def z_near(i):
+        place = i if i < 2 else steps - 4 + i
+        return pltpu.make_async_copy(obs.at[place], z_obs.at[i], obs_sems.at[i])
+
     conduct_copy.start()
     for copy in y_copies + y_near + [inner_copy]:
         copy.start()
-    for far, near in zip(z_copies, z_near):
-        far.start()
-        near.start()
+    for i in range(4):
+        z_far(i).start()
+        z_near(i).start()
     for copy in few_copies:
         copy.start()
     conduct_copy.wait()
     scale = conduct_here[...] * (1.0 / 6.0)
     for copy in y_copies + y_near + [inner_copy]:
         copy.wait()
-    for i in range(2):
-        cells = i * (2 * rows - points)
-        near = y_obs[i]
-        turned = [
-            y_field[i, p].T * scale[p : p + 1, cells : cells + points] for p in range(planes)
-        ]
-        add_products(total, jnp.concatenate(turned, axis=1), near)
-    for i in range(2):
-        plane = (planes - 1) * i
-        for half in range(2):
-            z_copies[2 * i + half].wait()
-            z_near[2 * i + half].wait()
-            turned = z_field[2 * i + half].T
-            turned = turned * scale[plane : plane + 1, half * rows : (half + 1) * rows]
-            add_products(total, turned, z_obs[2 * i + half])
+    turned = [
+        y_field[i, p].T * scale[p : p + 1, i * (2 * rows - points) :][:, :points]
+        for i in range(2)
+        for p in range(planes)
+    ]
+    add_products(total, jnp.concatenate(turned, axis=1), y_obs[...])
+
+    @pl.loop(0, 4)
+    def _(block):
+        for i in range(4):
+
+            @pl.when(block == i)
+            def _():
+                z_far(i).wait()
+                z_near(i).wait()
+
+        plane = (planes - 1) * (block // 2)
+        first = pl.multiple_of((block % 2) * rows, 128)
+        lanes = conduct_here[pl.ds(plane, 1), pl.ds(first, rows)] * (1.0 / 6.0)
+        add_products(total, z_field[block].T * lanes, z_obs[block])
 
     for copy in few_copies:
         copy.wait()
     summed = jnp.concatenate([extra[0:4] + extra[4:8], few_ctrl[0:4] + few_ctrl[4:8]], axis=0)
     wide = jnp.concatenate([summed, jnp.zeros((120, rank), F32)], axis=0).T
     width = rank // 2
-    for slot, out in enumerate((own, other)):
-        side = core[0] ^ slot
-        out[:, :, :width] = half_of(total, side).reshape(out.shape[0], out.shape[1], width)
-        part = wide * (side == 0).astype(F32)
-        out[:, :, width:] = part.reshape(out.shape[0], out.shape[1], 128)
+    for side in range(2):
+        cols = total[:, side * width : (side + 1) * width]
+        out[:, side, :, :width] = cols.reshape(out.shape[0], out.shape[2], width)
+    out[:, 0, :, width:] = wide.reshape(out.shape[0], out.shape[2], 128)
+    out[:, 1, :, width:] = jnp.zeros((out.shape[0], out.shape[2], 128), F32)
 
 
 def with_outer(observe, faces, conduct, inner, extra, few_ctrl, points):
@@ -398,14 +388,14 @@
     vmem = pl.BlockSpec(memory_space=pltpu.VMEM)
     return pl.pallas_call(
         functools.partial(outer_kernel, points),
-        in_specs=[pl.BlockSpec(memory_space=pltpu.SMEM)] + [anywhere] * 9,
-        out_specs=[vmem] * 2,
-        out_shape=[jax.ShapeDtypeStruct((rank // 8, 8, rank // 2 + 128), F32)] * 2,
+        in_specs=[anywhere] * 9,
+        out_specs=vmem,
+        out_shape=jax.ShapeDtypeStruct((rank // 8, 2, 8, rank // 2 + 128), F32),
         scratch_shapes=[
             pltpu.VMEM((4, rows, rank), F32),
             pltpu.VMEM((2, steps // 2, points, rank), F32),
             pltpu.VMEM((4, rows, rank), F32),
-            pltpu.VMEM((2, steps // 2 * points, rank), F32),
+            pltpu.VMEM((steps * points, rank), F32),
             pltpu.VMEM(conduct.shape, F32),
             pltpu.VMEM((rank, rank), F32),
             pltpu.VMEM(extra.shape, F32),
@@ -418,7 +408,7 @@
             flops=30 * rows * rank * rank, bytes_accessed=7 << 20, transcendentals=0
         ),
         name="outer_operator",
-    )(core_index(), *map(in_hbm, (observe, *faces, conduct, inner, extra, few_ctrl)))
+    )(*map(in_hbm, (observe, *faces, conduct, inner, extra, few_ctrl)))
 
 
 def sum_kernel(parts, out):
@@ -474,7 +464,7 @@
         project_kernel,
         in_specs=[pl.BlockSpec(memory_space=pltpu.SMEM), vmem, vmem],
         out_specs=vmem,
-        out_shape=jax.ShapeDtypeStruct((arrived.shape[0], 8, 256), F32),
+        out_shape=jax.ShapeDtypeStruct((arrived.shape[0] // 2, 8, 256), F32),
         compiler_params=pltpu.CompilerParams(vmem_limit_bytes=8 << 20),
         cost_estimate=pl.CostEstimate(
             flops=arrived.size, bytes_accessed=8 * arrived.size, transcendentals=0
@@ -488,26 +478,30 @@
     return mine, swapped(mine)
 
 
+def lane(block, index):
+    where = jnp.full(block.shape, index, jnp.int32)
+    return jnp.take_along_axis(block, where, axis=1, mode="promise_in_bounds")
+
+
 def inverse_factor(work):
     size = work.shape[0]
-    for first in range(0, size, PANEL):
-        last = first + PANEL
-        panel = [work[first + 8 * g : first + 8 * g + 8, :] for g in range(PANEL // 8)]
-        groups = PANEL // 8
+    groups = PANEL // 8
+
+    @pl.loop(0, size // PANEL)
+    def _(turn):
+        first = pl.multiple_of(turn * PANEL, PANEL)
+        panel = [work[pl.ds(first + 8 * g, 8), :] for g in range(groups)]
         columns = {}
         for k in range(PANEL):
             for g in range(k // 8, groups):
-                columns[k, g] = jnp.broadcast_to(
-                    panel[g][:, first + k : first + k + 1], (8, 128)
-                )
+                columns[k, g] = lane(panel[g][:, :128], first + k)
         place = lax.broadcasted_iota(jnp.int32, (8, 128), 0)
+        wide_place = lax.broadcasted_iota(jnp.int32, (8, 256), 0)
         for j in range(PANEL):
             gj, sj = divmod(j, 8)
             pivot = jnp.broadcast_to(columns[j, gj][sj : sj + 1], (8, 128))
             scale = lax.rsqrt(pivot)
-            lower = {}
-            for g in range(gj, groups):
-                lower[g] = columns[j, g] * scale
+            lower = {g: columns[j, g] * scale for g in range(gj, groups)}
             row = jnp.broadcast_to(panel[gj][sj : sj + 1], (8, 256))
             row = row * jnp.concatenate([scale, scale], axis=1)
             for k in range(j + 1, PANEL):
@@ -521,17 +515,19 @@
                     weight = jnp.where(place > sj, weight, 0.0)
                 wide = jnp.concatenate([weight, weight], axis=1)
                 panel[g] = panel[g] - wide * row
-            wide_place = lax.broadcasted_iota(jnp.int32, (8, 256), 0)
             panel[gj] = jnp.where(wide_place == sj, row, panel[gj])
         for g in range(groups):
-            work[first + 8 * g : first + 8 * g + 8, :] = panel[g]
-        if last < size:
+            work[pl.ds(first + 8 * g, 8), :] = panel[g]
+
+        @pl.when(turn + 1 < size // PANEL)
+        def _():
             done = jnp.concatenate(panel, axis=0)
             u0, u1, u2 = split3(done)
             left = jnp.concatenate([u0, u0, u1, u1, u0, u2], axis=0)[:, :size]
             right = jnp.concatenate([u0, u1, u0, u1, u2, u0], axis=0)
             change = product(left, right, ((0,), (0,)))
-            work[last:, :] -= change[last:, :]
+            below = lax.broadcasted_iota(jnp.int32, change.shape, 0) >= first + PANEL
+            work[...] -= jnp.where(below, change, 0.0)
 
 
 def bases_kernel(core, mine, theirs, start, right_out, left_out, image_out, high, low, basis, work):
@@ -647,8 +643,9 @@
     inner, extra = inner_operator(observe, control, diffusivity, input_map, points)
     gram = gathered(summed_copies(arrived))
     faces = (zlow, zhigh, ylow, yhigh)
-    own, other = with_outer(observe, faces, diffusivity, inner, extra, few_ctrl, points)
-    oper = scattered(own, other)
+    oper = with_outer(observe, faces, diffusivity, inner, extra, few_ctrl, points)
+    tiles = oper.reshape(-1, *oper.shape[2:])
+    oper = lax.all_to_all(tiles, CHIPS + ("core",), 0, 0, tiled=True)
     right, left, image = bases(*gram, start_block)
     blocks = gathered(projected_copies(oper, left))
     mass, state, inputs, outputs = finish(order, right, left, image, *blocks)

time: 133 us -> 154 us (1.16)
  blocking collectives: 21.4 us -> 48.2 us
  starting transfers between devices: 49.6 us -> 33 us
  waiting for transfers between devices: 2.34 us -> 15.6 us
  Pallas kernels: 56.1 us -> 53.8 us
    all_to_all x0 -> x1, blocking collectives: none -> 32.4 us  [scattered(): return lax.all_to_all(both, CHIPS, 0, 0, tiled=True)]
    all_to_all x2 -> x1, starting transfers between devices: 22 us -> 3.72 us  [reduced(): oper = lax.all_to_all(tiles, CHIPS + ('core',), 0, 0, tiled=True)]
    all_to_all x1, waiting for transfers between devices: 0.01 us -> 6.73 us  [gathered(): mine = lax.all_to_all(copies, CHIPS, 0, 0, tiled=True)]
    all_to_all x2 -> x1, waiting for transfers between devices: 1.26 us -> 7.92 us  [reduced(): oper = lax.all_to_all(tiles, CHIPS + ('core',), 0, 0, tiled=True)]
    all_to_all x1, blocking collectives: 21.4 us -> 15.8 us  [gathered(): mine = lax.all_to_all(copies, CHIPS, 0, 0, tiled=True)]
    ppermute x4 -> x3, starting transfers between devices: 7.61 us -> 10.7 us  [swapped(): return lax.ppermute(value, 'core', [(0, 1), (1, 0)])]
    pallas_call x1, Pallas kernels: 18.7 us -> 16.2 us  [bases(): pl.pallas_call(bases_kernel, in_specs=[pl.BlockSpec(memory_space=pltpu.SM...]
    pallas_call x2 -> x1, Pallas kernels: 1.8 us -> 0.06 us  [scattered(): pl.pallas_call(add_kernel, out_shape=jax.ShapeDtypeStruct(own.shape, F32)...]
  transfers between devices with their start and end apart: 11 -> 9, of which waited for: 3 -> 3; matrix products, arithmetic and copies ran while one was open for 0% -> 0% of each run, Pallas kernels for 33% -> 27%
where the time goes in v6:
time: 154 us
  Pallas kernels  53.8 us (35%)
  blocking collectives  48.2 us (31%)
  starting transfers between devices  33 us (21%)
  waiting for transfers between devices  15.6 us (10%)
  local copies, waits for them, and re-layouts  1.65 us (1%)
    all_to_all x1, blocking collectives, scattered(): return lax.all_to_all(both, CHIPS, 0, 0, tiled=True)  32.4 us
    pallas_call x1, Pallas kernels, bases(): pl.pallas_call(bases_kernel, in_specs=[pl.BlockSpec(memory_space=pltpu.SM...  16.2 us
    all_to_all x1, blocking collectives, gathered(): mine = lax.all_to_all(copies, CHIPS, 0, 0, tiled=True)  15.8 us
    pallas_call x1, Pallas kernels, inner_operator(): pl.pallas_call(functools.partial(inner_kernel, points), in_specs=[anywher...  14.4 us
    pallas_call x1, Pallas kernels, local_gram(): pl.pallas_call(gram_kernel, in_specs=[pl.BlockSpec(memory_space=pltpu.SME...  10.9 us
    ppermute x3, starting transfers between devices, swapped(): return lax.ppermute(value, 'core', [(0, 1), (1, 0)])  10.7 us
    pallas_call x1, Pallas kernels, with_outer(): pl.pallas_call(functools.partial(outer_kernel, points), in_specs=[anywher...  9.7 us
    all_to_all x1, starting transfers between devices, gathered(): mine = lax.all_to_all(copies, CHIPS, 0, 0, tiled=True)  8.72 us
  transfers between devices with their start and end apart: 9, of which 3 were waited for; matrix products, arithmetic and copies ran while one was open for 0% of the time, Pallas kernels for 27%

profile of v6, /device:TPU:1, one launch (start us, length us, event | category | flops | bytes accessed | tf_op | source)
XLA Modules:
  0.0 153.7 jit_solution(9862381634570120286)
XLA Ops:
  0.6 10.9 %local_gram.1 = (f32[64,8,256]{2,1,0:T(8,128)S(1)}, f32[64,8,256]{2,1,0:T(8,128)S(1)}, f32[16,512]{1,0:T(8,128)}, f32[2,512,512]{2,1,0:T(8,128)}, f32[2,512,512]...) custom-call(s32[1]{0:T(128)} %bitcast.core.side, f32[8,512,512]{2,1,0:T(8,128)} %bitcast.5, ...), custom_call_target="tpu_custom_call" | custom-call | flops 6442450944 | bytes 25165824 | tf_op jit(solution)/shard_map/local_gram/pallas_call | solution.py:173
  11.5 1.5 collective-permute-start
  13.0 3.2 %collective-permute-start.2 = (f32[2,512,512]{2,1,0:T(8,128)}, f32[2,512,512]{2,1,0:T(8,128)}, u32[]{:S(2)}, u32[]{:S(2)}) collective-permute-start(f32[2,512,512]{2,1,0:T(8,128)} %get-tuple-element.25), channel_id=1, source_target_pairs={{0,4},{4,8},{8,12},{12,16},{16,20},{20,24},{24,28},{28,32},{32,36}... | collective-permute-start | bytes 6291464 | tf_op jit(solution)/shard_map/ppermute | solution.py:629
  16.2 2.4 %collective-permute-start.3 = (f32[2,512,512]{2,1,0:T(8,128)}, f32[2,512,512]{2,1,0:T(8,128)}, u32[]{:S(2)}, u32[]{:S(2)}) collective-permute-start(f32[2,512,512]{2,1,0:T(8,128)} %get-tuple-element.26), channel_id=1, source_target_pairs={{4,0},{8,4},{12,8},{16,12},{20,16},{24,20},{28,24},{32,28},{36,32}... | collective-permute-start | bytes 6291464 | tf_op jit(solution)/shard_map/ppermute | solution.py:629
  18.7 32.4 %all_to_all.20.parts = f32[64,8,256]{2,1,0:T(8,128)S(1)} all-to-all(f32[64,8,256]{2,1,0:T(8,128)S(1)} %shard_map.102), channel_id=1, replica_groups=mesh['chip'=16,'core'=2,'sub'=4] {'chip','sub'}, dimensions={0} | all-to-all | bytes 1048576 | tf_op jit(solution)/shard_map/all_to_all | solution.py:437
  51.1 0.9 sum_gram.1
  52.0 8.7 %all-to-all-start.1 = ((f32[64,8,256]{2,1,0:T(8,128)}), f32[64,8,256]{2,1,0:T(8,128)S(1)}, u32[]{:S(2)}, u32[]{:S(2)}) async-start(f32[64,8,256]{2,1,0:T(8,128)} %sum_gram.1), calls=%async_computation.1 | async-start | bytes 1048576 | tf_op jit(solution)/shard_map/all_to_all | solution.py:477
  60.7 2.9 %collective-permute-start.4 = (f32[4,64,512]{2,1,0:T(8,128)S(1)}, f32[4,64,512]{2,1,0:T(8,128)S(1)}, u32[]{:S(2)}, u32[]{:S(2)}) collective-permute-start(f32[4,64,512]{2,1,0:T(8,128)S(1)} %copy-done.6), channel_id=1, source_target_pairs={{0,1},{1,2},{2,3},{4,5},{5,6},{6,7},{8,9},{9,10},{10,11},{12,13},{... | collective-permute-start | bytes 1572872 | tf_op jit(solution)/shard_map/ppermute | solution.py:629
  63.7 1.3 collective-permute-start.5
  65.0 6.7 %all-to-all-done.1.mine = f32[64,8,256]{2,1,0:T(8,128)S(1)} async-done(((f32[64,8,256]{2,1,0:T(8,128)}), f32[64,8,256]{2,1,0:T(8,128)S(1)}, u32[]{:S(2)}, u32[]{:S(2)}) %all-to-all-start.1) | async-done | bytes 524320 | tf_op jit(solution)/shard_map/all_to_all | solution.py:477
  71.7 6.8 %collective-permute-start.1 = (f32[64,8,256]{2,1,0:T(8,128)S(1)}, f32[64,8,256]{2,1,0:T(8,128)S(1)}, u32[]{:S(2)}, u32[]{:S(2)}) collective-permute-start(f32[64,8,256]{2,1,0:T(8,128)S(1)} %all-to-all-done.1.mine), channel_id=1, source_target_pairs={{0,4},{4,0},{1,5},{5,1},{2,6},{6,2},{3,7},{7,3},{8,12},{12,8},{9,1... | collective-permute-start | bytes 1572872 | tf_op jit(solution)/shard_map/ppermute | solution.py:420
  78.5 14.4 %inner_operator.1 = (f32[512,512]{1,0:T(8,128)}, f32[16,512]{1,0:T(8,128)}) custom-call(f32[8,512,512]{2,1,0:T(8,128)} %bitcast.6, f32[8,512,512]{2,1,0:T(8,128)} %bitcast.9, f32[4,1024]{1,0:T(4,128)} %conduct.3, f32[4,4,1024]{2,1,0:T(4,128)} %drive.1), custom_call_target="tpu_custom_call" | custom-call | flops 6442450944 | bytes 18874368 | tf_op jit(solution)/shard_map/inner_operator/pallas_call | solution.py:279
  93.0 0.7 copy-done.3
  93.7 0.2 copy-done.4
  93.9 9.7 %outer_operator.1 = f32[64,2,8,384]{3,2,1,0:T(8,128)} custom-call(f32[8,512,512]{2,1,0:T(8,128)} %bitcast.7, f32[2,512,512]{2,1,0:T(8,128)} %collective-permute-done.2.zlow, f32[2,512,512]{2,1,0:T(8,128)} %collective-permute-done.3.zhigh, f32[4,64,512]{2,1,0:T(8,128)} %copy-done.3, f32[4,64,512]{2,1,0:T(8,128)} %copy-done.4, f32[4,1024]{1,0:T(4,128)} %conduct.3, ...), custom_call_target="tpu_custom_call" | custom-call | flops 4026531840 | bytes 7340032 | tf_op jit(solution)/shard_map/outer_operator/pallas_call | solution.py:389
  103.6 3.7 %all-to-all-start.2 = ((f32[128,8,384]{2,1,0:T(8,128)}), f32[128,8,384]{2,1,0:T(8,128)S(1)}, u32[]{:S(2)}, u32[]{:S(2)}) async-start(f32[128,8,384]{2,1,0:T(8,128)} %bitcast.3), calls=%async_computation.2 | async-start | bytes 3145728 | tf_op jit(solution)/shard_map/all_to_all | solution.py:648
  107.4 16.2 %bases.1 = (f32[128,512]{1,0:T(8,128)S(1)}, f32[128,512]{1,0:T(8,128)S(1)}, f32[128,512]{1,0:T(8,128)S(1)}) custom-call(s32[1]{0:T(128)} %bitcast.core.side, f32[64,8,256]{2,1,0:T(8,128)S(1)} %all-to-all-done.1.mine, f32[64,8,256]{2,1,0:T(8,128)S(1)} %collective-permute-done.1.theirs, f32[512,128]{1,0:T(8,128)S(1)} %copy-done), custom_call_target="tpu_custom_call" | custom-call | flops 20000000000 | bytes 4194304 | tf_op jit(solution)/shard_map/bases/pallas_call | solution.py:573
  123.6 0.7 copy-done.1
  124.3 7.9 %all-to-all-done.2.parts = f32[128,8,384]{2,1,0:T(8,128)S(1)} async-done(((f32[128,8,384]{2,1,0:T(8,128)}), f32[128,8,384]{2,1,0:T(8,128)S(1)}, u32[]{:S(2)}, u32[]{:S(2)}) %all-to-all-start.2) | async-done | bytes 1572896 | tf_op jit(solution)/shard_map/all_to_all | solution.py:648
  132.2 0.3 project.1
  132.5 15.8 %all_to_all.21.mine = f32[64,8,256]{2,1,0:T(8,128)S(1)} all-to-all(f32[64,8,256]{2,1,0:T(8,128)S(1)} %project.1), channel_id=1, replica_groups=mesh['chip'=16,'core'=2,'sub'=4] {'chip','sub'}, dimensions={0} | all-to-all | bytes 1048576 | tf_op jit(solution)/shard_map/all_to_all | solution.py:477
  148.3 2.5 %collective-permute-start.6 = (f32[64,8,256]{2,1,0:T(8,128)S(1)}, f32[64,8,256]{2,1,0:T(8,128)S(1)}, u32[]{:S(2)}, u32[]{:S(2)}) collective-permute-start(f32[64,8,256]{2,1,0:T(8,128)S(1)} %all_to_all.21.mine), channel_id=1, source_target_pairs={{0,4},{4,0},{1,5},{5,1},{2,6},{6,2},{3,7},{7,3},{8,12},{12,8},{9,1... | collective-permute-start | bytes 1572872 | tf_op jit(solution)/shard_map/ppermute | solution.py:420
  151.4 0.9 collective-permute-done.6.theirs
  152.3 1.3 finish.1
  (18 shorter events, 0.1 us)
Async XLA Ops:
  11.5 7.1 %collective-permute-start = (f32[64,8,256]{2,1,0:T(8,128)S(1)}, f32[64,8,256]{2,1,0:T(8,128)S(1)}, u32[]{:S(2)}, u32[]{:S(2)}) collective-permute-start(f32[64,8,256]{2,1,0:T(8,128)S(1)} %get-tuple-element.21), channel_id=1, source_target_pairs={{0,4},{4,0},{1,5},{5,1},{2,6},{6,2},{3,7},{7,3},{8,12},{12,8},{9,1... | collective-permute-start | bytes 1572872 | tf_op jit(solution)/shard_map/ppermute | solution.py:420
  13.0 80.0 %collective-permute-start.2 = (f32[2,512,512]{2,1,0:T(8,128)}, f32[2,512,512]{2,1,0:T(8,128)}, u32[]{:S(2)}, u32[]{:S(2)}) collective-permute-start(f32[2,512,512]{2,1,0:T(8,128)} %get-tuple-element.25), channel_id=1, source_target_pairs={{0,4},{4,8},{8,12},{12,16},{16,20},{20,24},{24,28},{28,32},{32,36}... | collective-permute-start | bytes 6291464 | tf_op jit(solution)/shard_map/ppermute | solution.py:629
  16.2 76.8 %collective-permute-start.3 = (f32[2,512,512]{2,1,0:T(8,128)}, f32[2,512,512]{2,1,0:T(8,128)}, u32[]{:S(2)}, u32[]{:S(2)}) collective-permute-start(f32[2,512,512]{2,1,0:T(8,128)} %get-tuple-element.26), channel_id=1, source_target_pairs={{4,0},{8,4},{12,8},{16,12},{20,16},{24,20},{28,24},{32,28},{36,32}... | collective-permute-start | bytes 6291464 | tf_op jit(solution)/shard_map/ppermute | solution.py:629
  18.6 42.1 %copy-start.6 = (f32[4,64,512]{2,1,0:T(8,128)S(1)}, f32[4,64,512]{2,1,0:T(8,128)}, u32[]{:S(2)}) copy-start(f32[4,64,512]{2,1,0:T(8,128)} %get-tuple-element.27) | copy-start | bytes 1572868
  18.6 45.0 %copy-start.5 = (f32[4,64,512]{2,1,0:T(8,128)S(1)}, f32[4,64,512]{2,1,0:T(8,128)}, u32[]{:S(2)}) copy-start(f32[4,64,512]{2,1,0:T(8,128)} %get-tuple-element.28) | copy-start | bytes 1572868
  52.0 19.7 %all-to-all-start.1 = ((f32[64,8,256]{2,1,0:T(8,128)}), f32[64,8,256]{2,1,0:T(8,128)S(1)}, u32[]{:S(2)}, u32[]{:S(2)}) async-start(f32[64,8,256]{2,1,0:T(8,128)} %sum_gram.1), calls=%async_computation.1 | async-start | bytes 1048576 | tf_op jit(solution)/shard_map/all_to_all | solution.py:477
  60.7 32.2 %collective-permute-start.4 = (f32[4,64,512]{2,1,0:T(8,128)S(1)}, f32[4,64,512]{2,1,0:T(8,128)S(1)}, u32[]{:S(2)}, u32[]{:S(2)}) collective-permute-start(f32[4,64,512]{2,1,0:T(8,128)S(1)} %copy-done.6), channel_id=1, source_target_pairs={{0,1},{1,2},{2,3},{4,5},{5,6},{6,7},{8,9},{9,10},{10,11},{12,13},{... | collective-permute-start | bytes 1572872 | tf_op jit(solution)/shard_map/ppermute | solution.py:629
  63.7 29.2 %collective-permute-start.5 = (f32[4,64,512]{2,1,0:T(8,128)S(1)}, f32[4,64,512]{2,1,0:T(8,128)S(1)}, u32[]{:S(2)}, u32[]{:S(2)}) collective-permute-start(f32[4,64,512]{2,1,0:T(8,128)S(1)} %copy-done.5), channel_id=1, source_target_pairs={{1,0},{2,1},{3,2},{5,4},{6,5},{7,6},{9,8},{10,9},{11,10},{13,12},{... | collective-permute-start | bytes 1572872 | tf_op jit(solution)/shard_map/ppermute | solution.py:629
  71.7 35.6 %collective-permute-start.1 = (f32[64,8,256]{2,1,0:T(8,128)S(1)}, f32[64,8,256]{2,1,0:T(8,128)S(1)}, u32[]{:S(2)}, u32[]{:S(2)}) collective-permute-start(f32[64,8,256]{2,1,0:T(8,128)S(1)} %all-to-all-done.1.mine), channel_id=1, source_target_pairs={{0,4},{4,0},{1,5},{5,1},{2,6},{6,2},{3,7},{7,3},{8,12},{12,8},{9,1... | collective-permute-start | bytes 1572872 | tf_op jit(solution)/shard_map/ppermute | solution.py:420
  92.9 0.8 copy-start.3
  92.9 1.0 copy-start.4
  103.6 3.7 %copy-start = (f32[512,128]{1,0:T(8,128)S(1)}, f32[512,128]{1,0:T(8,128)}, u32[]{:S(2)}) copy-start(f32[512,128]{1,0:T(8,128)} %start.1) | copy-start | bytes 786436
  103.6 28.6 %all-to-all-start.2 = ((f32[128,8,384]{2,1,0:T(8,128)}), f32[128,8,384]{2,1,0:T(8,128)S(1)}, u32[]{:S(2)}, u32[]{:S(2)}) async-start(f32[128,8,384]{2,1,0:T(8,128)} %bitcast.3), calls=%async_computation.2 | async-start | bytes 3145728 | tf_op jit(solution)/shard_map/all_to_all | solution.py:648
  123.6 0.7 copy-start.1
  132.2 20.1 %copy-start.2 = (f32[128,512]{1,0:T(8,128)S(1)}, f32[128,512]{1,0:T(8,128)}, u32[]{:S(2)}) copy-start(f32[128,512]{1,0:T(8,128)} %copy-done.1) | copy-start | bytes 786436
  148.3 4.0 %collective-permute-start.6 = (f32[64,8,256]{2,1,0:T(8,128)S(1)}, f32[64,8,256]{2,1,0:T(8,128)S(1)}, u32[]{:S(2)}, u32[]{:S(2)}) collective-permute-start(f32[64,8,256]{2,1,0:T(8,128)S(1)} %all_to_all.21.mine), channel_id=1, source_target_pairs={{0,4},{4,0},{1,5},{5,1},{2,6},{6,2},{3,7},{7,3},{8,12},{12,8},{9,1... | collective-permute-start | bytes 1572872 | tf_op jit(solution)/shard_map/ppermute | solution.py:420

commit v7 on v6

--- a/solution.py
+++ b/solution.py
@@ -75,11 +75,6 @@
     return rows_split(chosen)
 
 
-def half_of(total, side):
-    width = total.shape[1] // 2
-    return total[:, pl.ds(pl.multiple_of(side * width, 128), width)]
-
-
 def core_index():
     return lax.axis_index("core").reshape(1).astype(jnp.int32)
 
@@ -89,8 +84,8 @@
 
 
 def gram_kernel(
-    core, obs, ctrl, sense,
-    own, other, few_far, zlow, zhigh, ylow, yhigh,
+    obs, ctrl, sense,
+    gram, few_far, zlow, zhigh, ylow, yhigh,
     obs_here, ctrl_here, total, extra, sense_here, obs_sems, ctrl_sems, z_sems, low_sems, high_sems, other_sems,
 ):
     steps, rows, _ = obs.shape
@@ -154,8 +149,10 @@
 
     few_copy = pltpu.make_async_copy(extra, few_far, other_sems.at[0])
     few_copy.start()
-    for slot, out in enumerate((own, other)):
-        out[...] = half_of(total, core[0] ^ slot).reshape(out.shape)
+    width = total.shape[1] // 2
+    for side in range(2):
+        cols = total[:, side * width : (side + 1) * width]
+        gram[:, side] = cols.reshape(gram.shape[0], gram.shape[2], width)
     few_copy.wait()
     for i in range(4):
         z_copy(i).wait()
@@ -172,11 +169,10 @@
     edge = pltpu.HBM((steps // 2, points, rank), F32)
     return pl.pallas_call(
         gram_kernel,
-        in_specs=[pl.BlockSpec(memory_space=pltpu.SMEM)] + [anywhere] * 3,
-        out_specs=[vmem] * 2 + [anywhere] * 5,
+        in_specs=[anywhere] * 3,
+        out_specs=[vmem] + [anywhere] * 5,
         out_shape=[
-            jax.ShapeDtypeStruct((rank // 8, 8, rank // 2), F32),
-            jax.ShapeDtypeStruct((rank // 8, 8, rank // 2), F32),
+            jax.ShapeDtypeStruct((rank // 8, 2, 8, rank // 2), F32),
             pltpu.HBM((16, rank), F32),
             face,
             face,
@@ -201,7 +197,7 @@
             flops=6 * steps * rows * rank * rank, bytes_accessed=24 << 20, transcendentals=0
         ),
         name="local_gram",
-    )(core_index(), in_hbm(observe), in_hbm(control), in_hbm(sense))
+    )(in_hbm(observe), in_hbm(control), in_hbm(sense))
 
 
 def inner_kernel(
@@ -304,13 +300,13 @@
 
 
 def outer_kernel(
-    points, obs, zlow, zhigh, ylow, yhigh, conduct, inner, extra_far, few_far,
-    out, z_field, y_field, z_obs, y_obs, conduct_here, total, extra, few_ctrl, sems, obs_sems,
+    points, obs, zlow, zhigh, conduct, inner, extra_far, few_far, ylow, yhigh,
+    out, z_field, z_obs, y_obs, conduct_here, total, extra, few_ctrl, inner_here, sems, obs_sems,
 ):
     steps, rows, rank = obs.shape
     planes = steps // 2
     conduct_copy = pltpu.make_async_copy(conduct, conduct_here, sems.at[0])
-    inner_copy = pltpu.make_async_copy(inner, total, sems.at[7])
+    inner_copy = pltpu.make_async_copy(inner, inner_here, sems.at[7])
     few_copies = [
         pltpu.make_async_copy(extra_far, extra, sems.at[8]),
         pltpu.make_async_copy(few_far, few_ctrl, sems.at[9]),
@@ -324,10 +320,6 @@
         for i in range(2)
         for p in range(planes)
     ]
-    y_copies = [
-        pltpu.make_async_copy(ylow, y_field.at[0], sems.at[1]),
-        pltpu.make_async_copy(yhigh, y_field.at[1], sems.at[2]),
-    ]
 
     def z_far(i):
         face = zlow if i < 2 else zhigh
@@ -338,22 +330,25 @@
         return pltpu.make_async_copy(obs.at[place], z_obs.at[i], obs_sems.at[i])
 
     conduct_copy.start()
-    for copy in y_copies + y_near + [inner_copy]:
+    for copy in y_near:
         copy.start()
     for i in range(4):
         z_far(i).start()
         z_near(i).start()
+        if i == 1:
+            inner_copy.start()
     for copy in few_copies:
         copy.start()
     conduct_copy.wait()
     scale = conduct_here[...] * (1.0 / 6.0)
-    for copy in y_copies + y_near + [inner_copy]:
+    for copy in y_near:
         copy.wait()
     turned = [
-        y_field[i, p].T * scale[p : p + 1, i * (2 * rows - points) :][:, :points]
+        (yhigh if i else ylow)[p].T * scale[p : p + 1, i * (2 * rows - points) :][:, :points]
         for i in range(2)
         for p in range(planes)
     ]
+    total[...] = jnp.zeros_like(total)
     add_products(total, jnp.concatenate(turned, axis=1), y_obs[...])
 
     @pl.loop(0, 4)
@@ -370,13 +365,14 @@
         lanes = conduct_here[pl.ds(plane, 1), pl.ds(first, rows)] * (1.0 / 6.0)
         add_products(total, z_field[block].T * lanes, z_obs[block])
 
-    for copy in few_copies:
+    for copy in few_copies + [inner_copy]:
         copy.wait()
     summed = jnp.concatenate([extra[0:4] + extra[4:8], few_ctrl[0:4] + few_ctrl[4:8]], axis=0)
     wide = jnp.concatenate([summed, jnp.zeros((120, rank), F32)], axis=0).T
     width = rank // 2
     for side in range(2):
-        cols = total[:, side * width : (side + 1) * width]
+        place = slice(side * width, (side + 1) * width)
+        cols = total[:, place] + inner_here[:, place]
         out[:, side, :, :width] = cols.reshape(out.shape[0], out.shape[2], width)
     out[:, 0, :, width:] = wide.reshape(out.shape[0], out.shape[2], 128)
     out[:, 1, :, width:] = jnp.zeros((out.shape[0], out.shape[2], 128), F32)
@@ -388,18 +384,18 @@
     vmem = pl.BlockSpec(memory_space=pltpu.VMEM)
     return pl.pallas_call(
         functools.partial(outer_kernel, points),
-        in_specs=[anywhere] * 9,
+        in_specs=[anywhere] * 7 + [vmem] * 2,
         out_specs=vmem,
         out_shape=jax.ShapeDtypeStruct((rank // 8, 2, 8, rank // 2 + 128), F32),
         scratch_shapes=[
             pltpu.VMEM((4, rows, rank), F32),
-            pltpu.VMEM((2, steps // 2, points, rank), F32),
             pltpu.VMEM((4, rows, rank), F32),
             pltpu.VMEM((steps * points, rank), F32),
             pltpu.VMEM(conduct.shape, F32),
             pltpu.VMEM((rank, rank), F32),
             pltpu.VMEM(extra.shape, F32),
             pltpu.VMEM(few_ctrl.shape, F32),
+            pltpu.VMEM((rank, rank), F32),
             pltpu.SemaphoreType.DMA((10,)),
             pltpu.SemaphoreType.DMA((4 + steps,)),
         ],
@@ -408,7 +404,7 @@
             flops=30 * rows * rank * rank, bytes_accessed=7 << 20, transcendentals=0
         ),
         name="outer_operator",
-    )(*map(in_hbm, (observe, *faces, conduct, inner, extra, few_ctrl)))
+    )(*map(in_hbm, (observe, *faces[:2], conduct, inner, extra, few_ctrl)), *faces[2:])
 
 
 def sum_kernel(parts, out):
@@ -420,27 +416,15 @@
     return lax.ppermute(value, "core", [(0, 1), (1, 0)])
 
 
-def add_kernel(first, second, out):
-    out[...] = first[...] + second[...]
-
-
-def scattered(own, other):
-    other = swapped(other)
-    both = pl.pallas_call(
-        add_kernel,
-        out_shape=jax.ShapeDtypeStruct(own.shape, F32),
-        compiler_params=pltpu.CompilerParams(vmem_limit_bytes=6 << 20),
-        cost_estimate=pl.CostEstimate(
-            flops=own.size, bytes_accessed=12 * own.size, transcendentals=0
-        ),
-    )(own, other)
-    return lax.all_to_all(both, CHIPS, 0, 0, tiled=True)
+def scattered(parts):
+    tiles = parts.reshape(-1, *parts.shape[2:])
+    return lax.all_to_all(tiles, CHIPS + ("core",), 0, 0, tiled=True)
 
 
 def summed_copies(arrived):
     return pl.pallas_call(
         sum_kernel,
-        out_shape=jax.ShapeDtypeStruct(arrived.shape, F32),
+        out_shape=jax.ShapeDtypeStruct((arrived.shape[0] // 2, *arrived.shape[1:]), F32),
         compiler_params=pltpu.CompilerParams(vmem_limit_bytes=6 << 20),
         cost_estimate=pl.CostEstimate(
             flops=arrived.size, bytes_accessed=8 * arrived.size, transcendentals=0
@@ -530,7 +514,12 @@
             work[...] -= jnp.where(below, change, 0.0)
 
 
-def bases_kernel(core, mine, theirs, start, right_out, left_out, image_out, high, low, basis, work):
+def bases_kernel(
+    core, mine, theirs, start, right_out, left_out, image_out,
+    high, low, basis, work, right, image, sems,
+):
+    right_copy = pltpu.make_async_copy(right, right_out, sems.at[0])
+    image_copy = pltpu.make_async_copy(image, image_out, sems.at[1])
     rank = high.shape[0]
     half = rank // 2
     for slot, part in enumerate((mine, theirs)):
@@ -551,9 +540,13 @@
             def _():
                 bh, bl = split2(basis[...])
                 small = product(bh, low[...], contract) + product(bl, high[...], contract)
-                image_out[...] = product(bh, high[...], contract) + small
-
-        held = image_out[...]
+                image[...] = product(bh, high[...], contract) + small
+
+        @pl.when(turn == 3)
+        def _():
+            image_copy.start()
+
+        held = image[...]
         work[:, :size] = product6(held, held, ((1,), (1,)))
         work[:, size:] = eye
         inverse_factor(work)
@@ -561,24 +554,32 @@
 
         @pl.when(turn == 2)
         def _():
-            right_out[...] = basis[...]
+            right[...] = basis[...]
+            right_copy.start()
 
     left_out[...] = basis[...]
+    right_copy.wait()
+    image_copy.wait()
 
 
 def bases(mine, theirs, start):
     rank, size = start.shape
     shape = jax.ShapeDtypeStruct((size, rank), F32)
     vmem = pl.BlockSpec(memory_space=pltpu.VMEM)
+    anywhere = pl.BlockSpec(memory_space=pltpu.HBM)
     return pl.pallas_call(
         bases_kernel,
         in_specs=[pl.BlockSpec(memory_space=pltpu.SMEM)] + [vmem] * 3,
-        out_shape=[shape, shape, shape],
+        out_specs=[anywhere, vmem, anywhere],
+        out_shape=[pltpu.HBM((size, rank), F32), shape, pltpu.HBM((size, rank), F32)],
         scratch_shapes=[
             pltpu.VMEM((rank, rank), BF16),
             pltpu.VMEM((rank, rank), BF16),
             pltpu.VMEM((size, rank), F32),
             pltpu.VMEM((size, 2 * size), F32),
+            pltpu.VMEM((size, rank), F32),
+            pltpu.VMEM((size, rank), F32),
+            pltpu.SemaphoreType.DMA((2,)),
         ],
         compiler_params=pltpu.CompilerParams(vmem_limit_bytes=16 << 20),
         cost_estimate=pl.CostEstimate(
@@ -634,18 +635,17 @@
     halves = (2 * planes, lines * points // 2, rank)
     observe = factor_obs.reshape(halves)
     control = factor_ctrl.reshape(halves)
-    own, other, few_ctrl, zlow, zhigh, ylow, yhigh = local_gram(
+    gram, few_ctrl, zlow, zhigh, ylow, yhigh = local_gram(
         observe, control, output_map, points
     )
-    arrived = scattered(own, other)
+    arrived = scattered(gram)
     zlow, zhigh = from_neighbours(zlow, zhigh, ("chip", "core"))
     ylow, yhigh = from_neighbours(ylow, yhigh, "sub")
     inner, extra = inner_operator(observe, control, diffusivity, input_map, points)
     gram = gathered(summed_copies(arrived))
     faces = (zlow, zhigh, ylow, yhigh)
     oper = with_outer(observe, faces, diffusivity, inner, extra, few_ctrl, points)
-    tiles = oper.reshape(-1, *oper.shape[2:])
-    oper = lax.all_to_all(tiles, CHIPS + ("core",), 0, 0, tiled=True)
+    oper = scattered(oper)
     right, left, image = bases(*gram, start_block)
     blocks = gathered(projected_copies(oper, left))
     mass, state, inputs, outputs = finish(order, right, left, image, *blocks)

time: 154 us -> 146 us (0.948)
  blocking collectives: 48.2 us -> 15.8 us
  waiting for transfers between devices: 15.6 us -> 39.6 us
  local copies, waits for them, and re-layouts: 1.65 us -> 0.02 us
    all_to_all x1 -> x0, blocking collectives: 32.4 us -> none  [scattered(): return lax.all_to_all(both, CHIPS, 0, 0, tiled=True)]
    all_to_all x1 -> x2, waiting for transfers between devices: 7.92 us -> 22.1 us  [scattered(): return lax.all_to_all(tiles, CHIPS + ('core',), 0, 0, tiled=True)]
    all_to_all x1 -> x2, starting transfers between devices: 3.72 us -> 17 us  [scattered(): return lax.all_to_all(tiles, CHIPS + ('core',), 0, 0, tiled=True)]
    all_to_all x1, waiting for transfers between devices: 6.73 us -> 16.6 us  [gathered(): mine = lax.all_to_all(copies, CHIPS, 0, 0, tiled=True)]
    ppermute x3 -> x2, starting transfers between devices: 10.7 us -> 2.86 us  [swapped(): return lax.ppermute(value, 'core', [(0, 1), (1, 0)])]
    all_to_all x1, starting transfers between devices: 8.72 us -> 4.63 us  [gathered(): mine = lax.all_to_all(copies, CHIPS, 0, 0, tiled=True)]
    unnamed x14 -> x10, local copies, waits for them, and re-layouts: 1.65 us -> 0.02 us
    pallas_call x3 -> x2, Pallas kernels: 11.8 us -> 13 us  [the longest x1 11.9 us: local_gram(): pl.pallas_call(gram_kernel, in_specs=[anywhere] * 3, out_specs=[vmem] + [...]
  transfers between devices with their start and end apart: 9 -> 9, of which waited for: 3 -> 4; matrix products, arithmetic and copies ran while one was open for 0% -> 0% of each run, Pallas kernels for 27% -> 28%
where the time goes in v7:
time: 146 us
  Pallas kernels  54.6 us (37%)
  waiting for transfers between devices  39.6 us (27%)
  starting transfers between devices  34.3 us (23%)
  blocking collectives  15.8 us (11%)
  between operations  1.49 us (1%)
    all_to_all x2, waiting for transfers between devices, scattered(): return lax.all_to_all(tiles, CHIPS + ('core',), 0, 0, tiled=True)  22.1 us
    all_to_all x2, starting transfers between devices, scattered(): return lax.all_to_all(tiles, CHIPS + ('core',), 0, 0, tiled=True)  17 us
    all_to_all x1, waiting for transfers between devices, gathered(): mine = lax.all_to_all(copies, CHIPS, 0, 0, tiled=True)  16.6 us
    pallas_call x1, Pallas kernels, bases(): pl.pallas_call(bases_kernel, in_specs=[pl.BlockSpec(memory_space=pltpu.SM...  16.2 us
    all_to_all x1, blocking collectives, gathered(): mine = lax.all_to_all(copies, CHIPS, 0, 0, tiled=True)  15.8 us
    pallas_call x1, Pallas kernels, inner_operator(): pl.pallas_call(functools.partial(inner_kernel, points), in_specs=[anywher...  14.4 us
    pallas_call x1, Pallas kernels, local_gram(): pl.pallas_call(gram_kernel, in_specs=[anywhere] * 3, out_specs=[vmem] + [...  11.9 us
    pallas_call x1, Pallas kernels, with_outer(): pl.pallas_call(functools.partial(outer_kernel, points), in_specs=[anywher...  9.37 us
  transfers between devices with their start and end apart: 9, of which 4 were waited for; matrix products, arithmetic and copies ran while one was open for 0% of the time, Pallas kernels for 28%

profile of v7, /device:TPU:1, one launch (start us, length us, event | category | flops | bytes accessed | tf_op | source)
XLA Modules:
  0.0 145.9 jit_solution(13096628117760015166)
XLA Ops:
  0.6 11.9 %local_gram.1 = (f32[64,2,8,256]{3,2,1,0:T(8,128)}, f32[16,512]{1,0:T(8,128)}, f32[2,512,512]{2,1,0:T(8,128)}, f32[2,512,512]{2,1,0:T(8,128)}, f32[4,64,512]{2,1,0:T(8,128)}, /*index=5*/f32[4,64,512]{2,1,0:T(8,128)}) custom-call(f32[8,512,512]{2,1,0:T(8,128)} %bitcast.6, f32[8,512,512]{2,1,0:T(8,128)} %bitcast.9, f32[4,4,1024]{2,1,0:T(4,128)} %sense.1), custom_call_target="tpu_custom_call" | custom-call | flops 6442450944 | bytes 25165824 | tf_op jit(solution)/shard_map/local_gram/pallas_call | solution.py:170
  12.6 11.5 %all-to-all-start = ((f32[128,8,256]{2,1,0:T(8,128)}), f32[128,8,256]{2,1,0:T(8,128)S(1)}, u32[]{:S(2)}, u32[]{:S(2)}) async-start(f32[128,8,256]{2,1,0:T(8,128)} %bitcast.3), calls=%async_computation | async-start | bytes 2097152 | tf_op jit(solution)/shard_map/all_to_all | solution.py:421
  24.1 3.5 %collective-permute-start.1 = (f32[2,512,512]{2,1,0:T(8,128)}, f32[2,512,512]{2,1,0:T(8,128)}, u32[]{:S(2)}, u32[]{:S(2)}) collective-permute-start(f32[2,512,512]{2,1,0:T(8,128)} %get-tuple-element.23), channel_id=1, source_target_pairs={{0,4},{4,8},{8,12},{12,16},{16,20},{20,24},{24,28},{28,32},{32,36}... | collective-permute-start | bytes 6291464 | tf_op jit(solution)/shard_map/ppermute | solution.py:630
  27.7 2.1 %collective-permute-start.2 = (f32[2,512,512]{2,1,0:T(8,128)}, f32[2,512,512]{2,1,0:T(8,128)}, u32[]{:S(2)}, u32[]{:S(2)}) collective-permute-start(f32[2,512,512]{2,1,0:T(8,128)} %get-tuple-element.24), channel_id=1, source_target_pairs={{4,0},{8,4},{12,8},{16,12},{20,16},{24,20},{28,24},{32,28},{36,32}... | collective-permute-start | bytes 6291464 | tf_op jit(solution)/shard_map/ppermute | solution.py:630
  29.8 13.6 %all-to-all-done.parts = f32[128,8,256]{2,1,0:T(8,128)S(1)} async-done(((f32[128,8,256]{2,1,0:T(8,128)}), f32[128,8,256]{2,1,0:T(8,128)S(1)}, u32[]{:S(2)}, u32[]{:S(2)}) %all-to-all-start) | async-done | bytes 1048608 | tf_op jit(solution)/shard_map/all_to_all | solution.py:421
  43.3 1.0 sum_gram.1
  44.4 4.6 %all-to-all-start.1 = ((f32[64,8,256]{2,1,0:T(8,128)}), f32[64,8,256]{2,1,0:T(8,128)S(1)}, u32[]{:S(2)}, u32[]{:S(2)}) async-start(f32[64,8,256]{2,1,0:T(8,128)} %sum_gram.1), calls=%async_computation.1 | async-start | bytes 1048576 | tf_op jit(solution)/shard_map/all_to_all | solution.py:461
  49.0 2.9 %collective-permute-start.3 = (f32[4,64,512]{2,1,0:T(8,128)S(1)}, f32[4,64,512]{2,1,0:T(8,128)S(1)}, u32[]{:S(2)}, u32[]{:S(2)}) collective-permute-start(f32[4,64,512]{2,1,0:T(8,128)S(1)} %copy-done.4), channel_id=1, source_target_pairs={{0,1},{1,2},{2,3},{4,5},{5,6},{6,7},{8,9},{9,10},{10,11},{12,13},{... | collective-permute-start | bytes 1572872 | tf_op jit(solution)/shard_map/ppermute | solution.py:630
  52.0 1.3 collective-permute-start.4
  53.2 16.6 %all-to-all-done.1.mine = f32[64,8,256]{2,1,0:T(8,128)S(1)} async-done(((f32[64,8,256]{2,1,0:T(8,128)}), f32[64,8,256]{2,1,0:T(8,128)S(1)}, u32[]{:S(2)}, u32[]{:S(2)}) %all-to-all-start.1) | async-done | bytes 524320 | tf_op jit(solution)/shard_map/all_to_all | solution.py:461
  69.8 0.4 collective-permute-start
  70.2 14.4 %inner_operator.1 = (f32[512,512]{1,0:T(8,128)}, f32[16,512]{1,0:T(8,128)}) custom-call(f32[8,512,512]{2,1,0:T(8,128)} %bitcast.7, f32[8,512,512]{2,1,0:T(8,128)} %bitcast.10, f32[4,1024]{1,0:T(4,128)} %conduct.3, f32[4,4,1024]{2,1,0:T(4,128)} %drive.1), custom_call_target="tpu_custom_call" | custom-call | flops 6442450944 | bytes 18874368 | tf_op jit(solution)/shard_map/inner_operator/pallas_call | solution.py:275
  84.6 0.0 collective-permute-done.4.yhigh
  84.6 0.0 collective-permute-done.1.zlow
  84.7 9.4 %outer_operator.1 = f32[64,2,8,384]{3,2,1,0:T(8,128)} custom-call(f32[8,512,512]{2,1,0:T(8,128)} %bitcast.8, f32[2,512,512]{2,1,0:T(8,128)} %collective-permute-done.1.zlow, f32[2,512,512]{2,1,0:T(8,128)} %collective-permute-done.2.zhigh, f32[4,1024]{1,0:T(4,128)} %conduct.3, f32[512,512]{1,0:T(8,128)} %get-tuple-element.25.inner, ...), custom_call_target="tpu_custom_call" | custom-call | flops 4026531840 | bytes 7340032 | tf_op jit(solution)/shard_map/outer_operator/pallas_call | solution.py:385
  94.0 0.0 copy-start
  94.1 5.5 %all-to-all-start.2 = ((f32[128,8,384]{2,1,0:T(8,128)}), f32[128,8,384]{2,1,0:T(8,128)S(1)}, u32[]{:S(2)}, u32[]{:S(2)}) async-start(f32[128,8,384]{2,1,0:T(8,128)} %bitcast.4), calls=%async_computation.2 | async-start | bytes 3145728 | tf_op jit(solution)/shard_map/all_to_all | solution.py:421
  99.6 16.2 %bases.1 = (f32[128,512]{1,0:T(8,128)}, f32[128,512]{1,0:T(8,128)S(1)}, f32[128,512]{1,0:T(8,128)}) custom-call(s32[1]{0:T(128)} %bitcast.core.side, f32[64,8,256]{2,1,0:T(8,128)S(1)} %all-to-all-done.1.mine, f32[64,8,256]{2,1,0:T(8,128)S(1)} %collective-permute-done.theirs, f32[512,128]{1,0:T(8,128)S(1)} %copy-done), custom_call_target="tpu_custom_call" | custom-call | flops 20000000000 | bytes 4194304 | tf_op jit(solution)/shard_map/bases/pallas_call | solution.py:570
  115.8 8.6 %all-to-all-done.2.parts = f32[128,8,384]{2,1,0:T(8,128)S(1)} async-done(((f32[128,8,384]{2,1,0:T(8,128)}), f32[128,8,384]{2,1,0:T(8,128)S(1)}, u32[]{:S(2)}, u32[]{:S(2)}) %all-to-all-start.2) | async-done | bytes 1572896 | tf_op jit(solution)/shard_map/all_to_all | solution.py:421
  124.4 0.3 project.1
  124.7 15.8 %all_to_all.20.mine = f32[64,8,256]{2,1,0:T(8,128)S(1)} all-to-all(f32[64,8,256]{2,1,0:T(8,128)S(1)} %project.1), channel_id=1, replica_groups=mesh['chip'=16,'core'=2,'sub'=4] {'chip','sub'}, dimensions={0} | all-to-all | bytes 1048576 | tf_op jit(solution)/shard_map/all_to_all | solution.py:461
  140.5 2.5 %collective-permute-start.5 = (f32[64,8,256]{2,1,0:T(8,128)S(1)}, f32[64,8,256]{2,1,0:T(8,128)S(1)}, u32[]{:S(2)}, u32[]{:S(2)}) collective-permute-start(f32[64,8,256]{2,1,0:T(8,128)S(1)} %all_to_all.20.mine), channel_id=1, source_target_pairs={{0,4},{4,0},{1,5},{5,1},{2,6},{6,2},{3,7},{7,3},{8,12},{12,8},{9,1... | collective-permute-start | bytes 1572872 | tf_op jit(solution)/shard_map/ppermute | solution.py:416
  143.6 0.9 collective-permute-done.5.theirs
  144.5 1.3 finish.1
  (12 shorter events, 0.0 us)
Async XLA Ops:
  12.6 36.4 %copy-start.4 = (f32[4,64,512]{2,1,0:T(8,128)S(1)}, f32[4,64,512]{2,1,0:T(8,128)}, u32[]{:S(2)}) copy-start(f32[4,64,512]{2,1,0:T(8,128)} %get-tuple-element.28) | copy-start | bytes 1572868
  12.6 39.4 %copy-start.3 = (f32[4,64,512]{2,1,0:T(8,128)S(1)}, f32[4,64,512]{2,1,0:T(8,128)}, u32[]{:S(2)}) copy-start(f32[4,64,512]{2,1,0:T(8,128)} %get-tuple-element.29) | copy-start | bytes 1572868
  12.6 30.7 %all-to-all-start = ((f32[128,8,256]{2,1,0:T(8,128)}), f32[128,8,256]{2,1,0:T(8,128)S(1)}, u32[]{:S(2)}, u32[]{:S(2)}) async-start(f32[128,8,256]{2,1,0:T(8,128)} %bitcast.3), calls=%async_computation | async-start | bytes 2097152 | tf_op jit(solution)/shard_map/all_to_all | solution.py:421
  24.1 60.5 %collective-permute-start.1 = (f32[2,512,512]{2,1,0:T(8,128)}, f32[2,512,512]{2,1,0:T(8,128)}, u32[]{:S(2)}, u32[]{:S(2)}) collective-permute-start(f32[2,512,512]{2,1,0:T(8,128)} %get-tuple-element.23), channel_id=1, source_target_pairs={{0,4},{4,8},{8,12},{12,16},{16,20},{20,24},{24,28},{28,32},{32,36}... | collective-permute-start | bytes 6291464 | tf_op jit(solution)/shard_map/ppermute | solution.py:630
  27.7 57.0 %collective-permute-start.2 = (f32[2,512,512]{2,1,0:T(8,128)}, f32[2,512,512]{2,1,0:T(8,128)}, u32[]{:S(2)}, u32[]{:S(2)}) collective-permute-start(f32[2,512,512]{2,1,0:T(8,128)} %get-tuple-element.24), channel_id=1, source_target_pairs={{4,0},{8,4},{12,8},{16,12},{20,16},{24,20},{28,24},{32,28},{36,32}... | collective-permute-start | bytes 6291464 | tf_op jit(solution)/shard_map/ppermute | solution.py:630
  44.4 25.5 %all-to-all-start.1 = ((f32[64,8,256]{2,1,0:T(8,128)}), f32[64,8,256]{2,1,0:T(8,128)S(1)}, u32[]{:S(2)}, u32[]{:S(2)}) async-start(f32[64,8,256]{2,1,0:T(8,128)} %sum_gram.1), calls=%async_computation.1 | async-start | bytes 1048576 | tf_op jit(solution)/shard_map/all_to_all | solution.py:461
  49.0 35.6 %collective-permute-start.3 = (f32[4,64,512]{2,1,0:T(8,128)S(1)}, f32[4,64,512]{2,1,0:T(8,128)S(1)}, u32[]{:S(2)}, u32[]{:S(2)}) collective-permute-start(f32[4,64,512]{2,1,0:T(8,128)S(1)} %copy-done.4), channel_id=1, source_target_pairs={{0,1},{1,2},{2,3},{4,5},{5,6},{6,7},{8,9},{9,10},{10,11},{12,13},{... | collective-permute-start | bytes 1572872 | tf_op jit(solution)/shard_map/ppermute | solution.py:630
  52.0 32.7 %collective-permute-start.4 = (f32[4,64,512]{2,1,0:T(8,128)S(1)}, f32[4,64,512]{2,1,0:T(8,128)S(1)}, u32[]{:S(2)}, u32[]{:S(2)}) collective-permute-start(f32[4,64,512]{2,1,0:T(8,128)S(1)} %copy-done.3), channel_id=1, source_target_pairs={{1,0},{2,1},{3,2},{5,4},{6,5},{7,6},{9,8},{10,9},{11,10},{13,12},{... | collective-permute-start | bytes 1572872 | tf_op jit(solution)/shard_map/ppermute | solution.py:630
  69.8 29.7 %collective-permute-start = (f32[64,8,256]{2,1,0:T(8,128)S(1)}, f32[64,8,256]{2,1,0:T(8,128)S(1)}, u32[]{:S(2)}, u32[]{:S(2)}) collective-permute-start(f32[64,8,256]{2,1,0:T(8,128)S(1)} %all-to-all-done.1.mine), channel_id=1, source_target_pairs={{0,4},{4,0},{1,5},{5,1},{2,6},{6,2},{3,7},{7,3},{8,12},{12,8},{9,1... | collective-permute-start | bytes 1572872 | tf_op jit(solution)/shard_map/ppermute | solution.py:416
  94.0 5.5 %copy-start = (f32[512,128]{1,0:T(8,128)S(1)}, f32[512,128]{1,0:T(8,128)}, u32[]{:S(2)}) copy-start(f32[512,128]{1,0:T(8,128)} %start.1) | copy-start | bytes 786436
  94.1 30.3 %all-to-all-start.2 = ((f32[128,8,384]{2,1,0:T(8,128)}), f32[128,8,384]{2,1,0:T(8,128)S(1)}, u32[]{:S(2)}, u32[]{:S(2)}) async-start(f32[128,8,384]{2,1,0:T(8,128)} %bitcast.4), calls=%async_computation.2 | async-start | bytes 3145728 | tf_op jit(solution)/shard_map/all_to_all | solution.py:421
  115.8 28.7 %copy-start.1 = (f32[128,512]{1,0:T(8,128)S(1)}, f32[128,512]{1,0:T(8,128)}, u32[]{:S(2)}) copy-start(f32[128,512]{1,0:T(8,128)} %get-tuple-element.20.right) | copy-start | bytes 786436
  115.8 28.7 %copy-start.2 = (f32[128,512]{1,0:T(8,128)S(1)}, f32[128,512]{1,0:T(8,128)}, u32[]{:S(2)}) copy-start(f32[128,512]{1,0:T(8,128)} %get-tuple-element.22.image) | copy-start | bytes 786436
  140.5 4.0 %collective-permute-start.5 = (f32[64,8,256]{2,1,0:T(8,128)S(1)}, f32[64,8,256]{2,1,0:T(8,128)S(1)}, u32[]{:S(2)}, u32[]{:S(2)}) collective-permute-start(f32[64,8,256]{2,1,0:T(8,128)S(1)} %all_to_all.20.mine), channel_id=1, source_target_pairs={{0,4},{4,0},{1,5},{5,1},{2,6},{6,2},{3,7},{7,3},{8,12},{12,8},{9,1... | collective-permute-start | bytes 1572872 | tf_op jit(solution)/shard_map/ppermute | solution.py:416

commit v8 on v7

--- a/solution.py
+++ b/solution.py
@@ -300,17 +300,13 @@
 
 
 def outer_kernel(
-    points, obs, zlow, zhigh, conduct, inner, extra_far, few_far, ylow, yhigh,
-    out, z_field, z_obs, y_obs, conduct_here, total, extra, few_ctrl, inner_here, sems, obs_sems,
+    points, obs, zlow, zhigh, conduct, inner, ylow, yhigh,
+    out, z_field, z_obs, y_obs, conduct_here, total, inner_here, sems, obs_sems,
 ):
     steps, rows, rank = obs.shape
     planes = steps // 2
     conduct_copy = pltpu.make_async_copy(conduct, conduct_here, sems.at[0])
     inner_copy = pltpu.make_async_copy(inner, inner_here, sems.at[7])
-    few_copies = [
-        pltpu.make_async_copy(extra_far, extra, sems.at[8]),
-        pltpu.make_async_copy(few_far, few_ctrl, sems.at[9]),
-    ]
     y_near = [
         pltpu.make_async_copy(
             obs.at[2 * p + i, pl.ds(i * (rows - points), points)],
@@ -337,8 +333,6 @@
         z_near(i).start()
         if i == 1:
             inner_copy.start()
-    for copy in few_copies:
-        copy.start()
     conduct_copy.wait()
     scale = conduct_here[...] * (1.0 / 6.0)
     for copy in y_near:
@@ -365,38 +359,31 @@
         lanes = conduct_here[pl.ds(plane, 1), pl.ds(first, rows)] * (1.0 / 6.0)
         add_products(total, z_field[block].T * lanes, z_obs[block])
 
-    for copy in few_copies + [inner_copy]:
-        copy.wait()
-    summed = jnp.concatenate([extra[0:4] + extra[4:8], few_ctrl[0:4] + few_ctrl[4:8]], axis=0)
-    wide = jnp.concatenate([summed, jnp.zeros((120, rank), F32)], axis=0).T
+    inner_copy.wait()
     width = rank // 2
     for side in range(2):
         place = slice(side * width, (side + 1) * width)
         cols = total[:, place] + inner_here[:, place]
-        out[:, side, :, :width] = cols.reshape(out.shape[0], out.shape[2], width)
-    out[:, 0, :, width:] = wide.reshape(out.shape[0], out.shape[2], 128)
-    out[:, 1, :, width:] = jnp.zeros((out.shape[0], out.shape[2], 128), F32)
-
-
-def with_outer(observe, faces, conduct, inner, extra, few_ctrl, points):
+        out[:, side] = cols.reshape(out.shape[0], out.shape[2], width)
+
+
+def with_outer(observe, faces, conduct, inner, points):
     steps, rows, rank = observe.shape
     anywhere = pl.BlockSpec(memory_space=pltpu.HBM)
     vmem = pl.BlockSpec(memory_space=pltpu.VMEM)
     return pl.pallas_call(
         functools.partial(outer_kernel, points),
-        in_specs=[anywhere] * 7 + [vmem] * 2,
+        in_specs=[anywhere] * 5 + [vmem] * 2,
         out_specs=vmem,
-        out_shape=jax.ShapeDtypeStruct((rank // 8, 2, 8, rank // 2 + 128), F32),
+        out_shape=jax.ShapeDtypeStruct((rank // 8, 2, 8, rank // 2), F32),
         scratch_shapes=[
             pltpu.VMEM((4, rows, rank), F32),
             pltpu.VMEM((4, rows, rank), F32),
             pltpu.VMEM((steps * points, rank), F32),
             pltpu.VMEM(conduct.shape, F32),
             pltpu.VMEM((rank, rank), F32),
-            pltpu.VMEM(extra.shape, F32),
-            pltpu.VMEM(few_ctrl.shape, F32),
             pltpu.VMEM((rank, rank), F32),
-            pltpu.SemaphoreType.DMA((10,)),
+            pltpu.SemaphoreType.DMA((8,)),
             pltpu.SemaphoreType.DMA((4 + steps,)),
         ],
         compiler_params=pltpu.CompilerParams(vmem_limit_bytes=36 << 20),
@@ -404,7 +391,7 @@
             flops=30 * rows * rank * rank, bytes_accessed=7 << 20, transcendentals=0
         ),
         name="outer_operator",
-    )(*map(in_hbm, (observe, *faces[:2], conduct, inner, extra, few_ctrl)), *faces[2:])
+    )(*map(in_hbm, (observe, *faces[:2], conduct, inner)), *faces[2:])
 
 
 def sum_kernel(parts, out):
@@ -433,20 +420,20 @@
     )(arrived)
 
 
-def project_kernel(side, parts, left, out):
+def project_kernel(side, parts, left, few, out):
     block = jnp.sum(parts[...], axis=0)
     half = left.shape[1] // 2
     mine = jnp.where(side[0] == 0, left[:, :half], left[:, half:])
-    turned = product3(block[:, :half], mine, ((1,), (1,)))
-    whole = jnp.concatenate([turned, block[:, half:]], axis=1)
+    turned = product3(block, mine, ((1,), (1,)))
+    whole = jnp.concatenate([turned, few[...]], axis=1)
     out[...] = jnp.broadcast_to(whole[None], out.shape)
 
 
-def projected_copies(arrived, left):
+def projected_copies(arrived, left, few):
     vmem = pl.BlockSpec(memory_space=pltpu.VMEM)
     return pl.pallas_call(
         project_kernel,
-        in_specs=[pl.BlockSpec(memory_space=pltpu.SMEM), vmem, vmem],
+        in_specs=[pl.BlockSpec(memory_space=pltpu.SMEM), vmem, vmem, vmem],
         out_specs=vmem,
         out_shape=jax.ShapeDtypeStruct((arrived.shape[0] // 2, 8, 256), F32),
         compiler_params=pltpu.CompilerParams(vmem_limit_bytes=8 << 20),
@@ -454,7 +441,7 @@
             flops=arrived.size, bytes_accessed=8 * arrived.size, transcendentals=0
         ),
         name="project",
-    )(core_index(), arrived, left)
+    )(core_index(), arrived, left, few)
 
 
 def gathered(copies):
@@ -515,9 +502,16 @@
 
 
 def bases_kernel(
-    core, mine, theirs, start, right_out, left_out, image_out,
-    high, low, basis, work, right, image, sems,
+    core, mine, theirs, start, drive_far, sense_far,
+    right_out, left_out, image_out, few_out,
+    high, low, basis, work, right, image, drive, sense, sems,
 ):
+    small = [
+        pltpu.make_async_copy(drive_far, drive, sems.at[2]),
+        pltpu.make_async_copy(sense_far, sense, sems.at[3]),
+    ]
+    for copy in small:
+        copy.start()
     right_copy = pltpu.make_async_copy(right, right_out, sems.at[0])
     image_copy = pltpu.make_async_copy(image, image_out, sems.at[1])
     rank = high.shape[0]
@@ -558,20 +552,32 @@
             right_copy.start()
 
     left_out[...] = basis[...]
+    for copy in small:
+        copy.wait()
+    rows = jnp.concatenate([drive[0:4] + drive[4:8], sense[0:4] + sense[4:8]], axis=0)
+    both = ((1,), (1,))
+    place = lax.broadcasted_iota(jnp.int32, few_out.shape, 0)
+    by_left, by_right = product3(rows, basis[...], both), product3(rows, right[...], both)
+    few_out[...] = jnp.where(place < 4, by_left, by_right)
     right_copy.wait()
     image_copy.wait()
 
 
-def bases(mine, theirs, start):
+def bases(mine, theirs, start, drive, sense):
     rank, size = start.shape
     shape = jax.ShapeDtypeStruct((size, rank), F32)
     vmem = pl.BlockSpec(memory_space=pltpu.VMEM)
     anywhere = pl.BlockSpec(memory_space=pltpu.HBM)
     return pl.pallas_call(
         bases_kernel,
-        in_specs=[pl.BlockSpec(memory_space=pltpu.SMEM)] + [vmem] * 3,
-        out_specs=[anywhere, vmem, anywhere],
-        out_shape=[pltpu.HBM((size, rank), F32), shape, pltpu.HBM((size, rank), F32)],
+        in_specs=[pl.BlockSpec(memory_space=pltpu.SMEM)] + [vmem] * 3 + [anywhere] * 2,
+        out_specs=[anywhere, vmem, anywhere, vmem],
+        out_shape=[
+            pltpu.HBM((size, rank), F32),
+            shape,
+            pltpu.HBM((size, rank), F32),
+            jax.ShapeDtypeStruct((8, size), F32),
+        ],
         scratch_shapes=[
             pltpu.VMEM((rank, rank), BF16),
             pltpu.VMEM((rank, rank), BF16),
@@ -579,27 +585,31 @@
             pltpu.VMEM((size, 2 * size), F32),
             pltpu.VMEM((size, rank), F32),
             pltpu.VMEM((size, rank), F32),
-            pltpu.SemaphoreType.DMA((2,)),
+            pltpu.VMEM(drive.shape, F32),
+            pltpu.VMEM(sense.shape, F32),
+            pltpu.SemaphoreType.DMA((4,)),
         ],
         compiler_params=pltpu.CompilerParams(vmem_limit_bytes=16 << 20),
         cost_estimate=pl.CostEstimate(
             flops=20_000_000_000, bytes_accessed=4 << 20, transcendentals=0
         ),
         name="bases",
-    )(core_index(), mine, theirs, start)
+    )(core_index(), mine, theirs, start, in_hbm(drive), in_hbm(sense))
 
 
 def finish_kernel(order, right, left, image, mine, theirs, mass, state, inputs, outputs):
     size, rank = right.shape
-    blocks = (mine[...] + theirs[...]).reshape(rank, size + 128)
-    turned, few = blocks[:, :size], blocks[:, size:]
+    blocks = (mine[...] + theirs[...]).reshape(rank, 2 * size)
+    turned = blocks[:, :size]
+    few = jnp.sum(blocks[:, size:].reshape(rank // 8, 8, size), axis=0)
     kept_col = lax.broadcasted_iota(jnp.int32, (size, size), 0) < order[0]
     kept_row = lax.broadcasted_iota(jnp.int32, (size, size), 1) < order[0]
     kept = jnp.logical_and(kept_col, kept_row).astype(F32)
     mass[...] = kept * product6(left[...], image[...], ((1,), (1,)))
     state[...] = kept * product3(right[...], turned).T
-    inputs[...] = (kept_row.astype(F32) * product3(left[...], few).T)[:4]
-    outputs[...] = (kept_row.astype(F32) * product3(right[...], few).T)[4:8]
+    few = kept_row[:8].astype(F32) * few
+    inputs[...] = few[:4]
+    outputs[...] = few[4:]
 
 
 def finish(order, right, left, image, mine, theirs):
@@ -644,10 +654,10 @@
     inner, extra = inner_operator(observe, control, diffusivity, input_map, points)
     gram = gathered(summed_copies(arrived))
     faces = (zlow, zhigh, ylow, yhigh)
-    oper = with_outer(observe, faces, diffusivity, inner, extra, few_ctrl, points)
+    oper = with_outer(observe, faces, diffusivity, inner, points)
     oper = scattered(oper)
-    right, left, image = bases(*gram, start_block)
-    blocks = gathered(projected_copies(oper, left))
+    right, left, image, few = bases(*gram, start_block, extra, few_ctrl)
+    blocks = gathered(projected_copies(oper, left, few))
     mass, state, inputs, outputs = finish(order, right, left, image, *blocks)
     return mass, state, inputs.T, outputs
 

time: 146 us -> 143 us (0.979)
  waiting for transfers between devices: 39.6 us -> 33.7 us
  blocking collectives: 15.8 us -> 20.2 us
    all_to_all x2, waiting for transfers between devices: 22.1 us -> 16.2 us  [scattered(): return lax.all_to_all(tiles, CHIPS + ('core',), 0, 0, tiled=True)]
    all_to_all x1, blocking collectives: 15.8 us -> 20.2 us  [gathered(): mine = lax.all_to_all(copies, CHIPS, 0, 0, tiled=True)]
where the time goes in v8:
time: 143 us
  Pallas kernels  53.9 us (38%)
  starting transfers between devices  33.7 us (24%)
  waiting for transfers between devices  33.7 us (24%)
  blocking collectives  20.2 us (14%)
  between operations  1.49 us (1%)
    all_to_all x1, blocking collectives, gathered(): mine = lax.all_to_all(copies, CHIPS, 0, 0, tiled=True)  20.2 us
    all_to_all x2, starting transfers between devices, scattered(): return lax.all_to_all(tiles, CHIPS + ('core',), 0, 0, tiled=True)  17 us
    all_to_all x1, waiting for transfers between devices, gathered(): mine = lax.all_to_all(copies, CHIPS, 0, 0, tiled=True)  16.6 us
    pallas_call x1, Pallas kernels, bases(): pl.pallas_call(bases_kernel, in_specs=[pl.BlockSpec(memory_space=pltpu.SM...  16.6 us
    all_to_all x2, waiting for transfers between devices, scattered(): return lax.all_to_all(tiles, CHIPS + ('core',), 0, 0, tiled=True)  16.2 us
    pallas_call x1, Pallas kernels, inner_operator(): pl.pallas_call(functools.partial(inner_kernel, points), in_specs=[anywher...  14.4 us
    pallas_call x1, Pallas kernels, local_gram(): pl.pallas_call(gram_kernel, in_specs=[anywhere] * 3, out_specs=[vmem] + [...  11.9 us
    pallas_call x1, Pallas kernels, with_outer(): pl.pallas_call(functools.partial(outer_kernel, points), in_specs=[anywher...  8.43 us
  transfers between devices with their start and end apart: 9, of which 4 were waited for; matrix products, arithmetic and copies ran while one was open for 0% of the time, Pallas kernels for 28%

profile of v8, /device:TPU:1, one launch (start us, length us, event | category | flops | bytes accessed | tf_op | source)
XLA Modules:
  0.0 142.9 jit_solution(10084012201783961889)
XLA Ops:
  0.6 11.9 %local_gram.1 = (f32[64,2,8,256]{3,2,1,0:T(8,128)}, f32[16,512]{1,0:T(8,128)}, f32[2,512,512]{2,1,0:T(8,128)}, f32[2,512,512]{2,1,0:T(8,128)}, f32[4,64,512]{2,1,0:T(8,128)}, /*index=5*/f32[4,64,512]{2,1,0:T(8,128)}) custom-call(f32[8,512,512]{2,1,0:T(8,128)} %bitcast.6, f32[8,512,512]{2,1,0:T(8,128)} %bitcast.9, f32[4,4,1024]{2,1,0:T(4,128)} %sense.1), custom_call_target="tpu_custom_call" | custom-call | flops 6442450944 | bytes 25165824 | tf_op jit(solution)/shard_map/local_gram/pallas_call | solution.py:170
  12.6 11.5 %all-to-all-start = ((f32[128,8,256]{2,1,0:T(8,128)}), f32[128,8,256]{2,1,0:T(8,128)S(1)}, u32[]{:S(2)}, u32[]{:S(2)}) async-start(f32[128,8,256]{2,1,0:T(8,128)} %bitcast.3), calls=%async_computation | async-start | bytes 2097152 | tf_op jit(solution)/shard_map/all_to_all | solution.py:408
  24.1 3.5 %collective-permute-start.1 = (f32[2,512,512]{2,1,0:T(8,128)}, f32[2,512,512]{2,1,0:T(8,128)}, u32[]{:S(2)}, u32[]{:S(2)}) collective-permute-start(f32[2,512,512]{2,1,0:T(8,128)} %get-tuple-element.26), channel_id=1, source_target_pairs={{0,4},{4,8},{8,12},{12,16},{16,20},{20,24},{24,28},{28,32},{32,36}... | collective-permute-start | bytes 6291464 | tf_op jit(solution)/shard_map/ppermute | solution.py:640
  27.7 2.1 %collective-permute-start.2 = (f32[2,512,512]{2,1,0:T(8,128)}, f32[2,512,512]{2,1,0:T(8,128)}, u32[]{:S(2)}, u32[]{:S(2)}) collective-permute-start(f32[2,512,512]{2,1,0:T(8,128)} %get-tuple-element.27), channel_id=1, source_target_pairs={{4,0},{8,4},{12,8},{16,12},{20,16},{24,20},{28,24},{32,28},{36,32}... | collective-permute-start | bytes 6291464 | tf_op jit(solution)/shard_map/ppermute | solution.py:640
  29.8 13.6 %all-to-all-done.parts = f32[128,8,256]{2,1,0:T(8,128)S(1)} async-done(((f32[128,8,256]{2,1,0:T(8,128)}), f32[128,8,256]{2,1,0:T(8,128)S(1)}, u32[]{:S(2)}, u32[]{:S(2)}) %all-to-all-start) | async-done | bytes 1048608 | tf_op jit(solution)/shard_map/all_to_all | solution.py:408
  43.3 1.0 sum_gram.1
  44.4 4.6 %all-to-all-start.1 = ((f32[64,8,256]{2,1,0:T(8,128)}), f32[64,8,256]{2,1,0:T(8,128)S(1)}, u32[]{:S(2)}, u32[]{:S(2)}) async-start(f32[64,8,256]{2,1,0:T(8,128)} %sum_gram.1), calls=%async_computation.1 | async-start | bytes 1048576 | tf_op jit(solution)/shard_map/all_to_all | solution.py:448
  49.0 2.9 %collective-permute-start.3 = (f32[4,64,512]{2,1,0:T(8,128)S(1)}, f32[4,64,512]{2,1,0:T(8,128)S(1)}, u32[]{:S(2)}, u32[]{:S(2)}) collective-permute-start(f32[4,64,512]{2,1,0:T(8,128)S(1)} %copy-done.4), channel_id=1, source_target_pairs={{0,1},{1,2},{2,3},{4,5},{5,6},{6,7},{8,9},{9,10},{10,11},{12,13},{... | collective-permute-start | bytes 1572872 | tf_op jit(solution)/shard_map/ppermute | solution.py:640
  52.0 1.3 collective-permute-start.4
  53.2 16.6 %all-to-all-done.1.mine = f32[64,8,256]{2,1,0:T(8,128)S(1)} async-done(((f32[64,8,256]{2,1,0:T(8,128)}), f32[64,8,256]{2,1,0:T(8,128)S(1)}, u32[]{:S(2)}, u32[]{:S(2)}) %all-to-all-start.1) | async-done | bytes 524320 | tf_op jit(solution)/shard_map/all_to_all | solution.py:448
  69.8 0.4 collective-permute-start
  70.2 14.4 %inner_operator.1 = (f32[512,512]{1,0:T(8,128)}, f32[16,512]{1,0:T(8,128)}) custom-call(f32[8,512,512]{2,1,0:T(8,128)} %bitcast.7, f32[8,512,512]{2,1,0:T(8,128)} %bitcast.10, f32[4,1024]{1,0:T(4,128)} %conduct.3, f32[4,4,1024]{2,1,0:T(4,128)} %drive.1), custom_call_target="tpu_custom_call" | custom-call | flops 6442450944 | bytes 18874368 | tf_op jit(solution)/shard_map/inner_operator/pallas_call | solution.py:275
  84.6 0.0 collective-permute-done.4.yhigh
  84.6 0.0 collective-permute-done.1.zlow
  84.7 8.4 %outer_operator.1 = f32[64,2,8,256]{3,2,1,0:T(8,128)} custom-call(f32[8,512,512]{2,1,0:T(8,128)} %bitcast.8, f32[2,512,512]{2,1,0:T(8,128)} %collective-permute-done.1.zlow, f32[2,512,512]{2,1,0:T(8,128)} %collective-permute-done.2.zhigh, f32[4,1024]{1,0:T(4,128)} %conduct.3, f32[512,512]{1,0:T(8,128)} %get-tuple-element.28.inner, ...), custom_call_target="tpu_custom_call" | custom-call | flops 4026531840 | bytes 7340032 | tf_op jit(solution)/shard_map/outer_operator/pallas_call | solution.py:374
  93.1 0.0 copy-start
  93.1 5.5 %all-to-all-start.2 = ((f32[128,8,256]{2,1,0:T(8,128)}), f32[128,8,256]{2,1,0:T(8,128)S(1)}, u32[]{:S(2)}, u32[]{:S(2)}) async-start(f32[128,8,256]{2,1,0:T(8,128)} %bitcast.4), calls=%async_computation.2 | async-start | bytes 2097152 | tf_op jit(solution)/shard_map/all_to_all | solution.py:408
  98.6 16.6 %bases.1 = (f32[128,512]{1,0:T(8,128)}, f32[128,512]{1,0:T(8,128)S(1)}, f32[128,512]{1,0:T(8,128)}, f32[8,128]{1,0:T(8,128)S(1)}) custom-call(s32[1]{0:T(128)} %bitcast.core.side, f32[64,8,256]{2,1,0:T(8,128)S(1)} %all-to-all-done.1.mine, f32[64,8,256]{2,1,0:T(8,128)S(1)} %collective-permute-done.theirs, f32[512,128]{1,0:T(8,128)S(1)} %copy-done, ...), custom_call_target="tpu_custom_call" | custom-call | flops 20000000000 | bytes 4194304 | tf_op jit(solution)/shard_map/bases/pallas_call | solution.py:571
  115.2 2.6 %all-to-all-done.2.parts = f32[128,8,256]{2,1,0:T(8,128)S(1)} async-done(((f32[128,8,256]{2,1,0:T(8,128)}), f32[128,8,256]{2,1,0:T(8,128)S(1)}, u32[]{:S(2)}, u32[]{:S(2)}) %all-to-all-start.2) | async-done | bytes 1048608 | tf_op jit(solution)/shard_map/all_to_all | solution.py:408
  117.8 0.3 project.1
  118.2 20.2 %all_to_all.20.mine = f32[64,8,256]{2,1,0:T(8,128)S(1)} all-to-all(f32[64,8,256]{2,1,0:T(8,128)S(1)} %project.1), channel_id=1, replica_groups=mesh['chip'=16,'core'=2,'sub'=4] {'chip','sub'}, dimensions={0} | all-to-all | bytes 1048576 | tf_op jit(solution)/shard_map/all_to_all | solution.py:448
  138.3 1.9 %collective-permute-start.5 = (f32[64,8,256]{2,1,0:T(8,128)S(1)}, f32[64,8,256]{2,1,0:T(8,128)S(1)}, u32[]{:S(2)}, u32[]{:S(2)}) collective-permute-start(f32[64,8,256]{2,1,0:T(8,128)S(1)} %all_to_all.20.mine), channel_id=1, source_target_pairs={{0,4},{4,0},{1,5},{5,1},{2,6},{6,2},{3,7},{7,3},{8,12},{12,8},{9,1... | collective-permute-start | bytes 1572872 | tf_op jit(solution)/shard_map/ppermute | solution.py:403
  140.9 0.9 collective-permute-done.5.theirs
  141.7 1.2 finish.1
  (12 shorter events, 0.0 us)
Async XLA Ops:
  12.6 36.4 %copy-start.4 = (f32[4,64,512]{2,1,0:T(8,128)S(1)}, f32[4,64,512]{2,1,0:T(8,128)}, u32[]{:S(2)}) copy-start(f32[4,64,512]{2,1,0:T(8,128)} %get-tuple-element.29) | copy-start | bytes 1572868
  12.6 39.4 %copy-start.3 = (f32[4,64,512]{2,1,0:T(8,128)S(1)}, f32[4,64,512]{2,1,0:T(8,128)}, u32[]{:S(2)}) copy-start(f32[4,64,512]{2,1,0:T(8,128)} %get-tuple-element.30) | copy-start | bytes 1572868
  12.6 30.7 %all-to-all-start = ((f32[128,8,256]{2,1,0:T(8,128)}), f32[128,8,256]{2,1,0:T(8,128)S(1)}, u32[]{:S(2)}, u32[]{:S(2)}) async-start(f32[128,8,256]{2,1,0:T(8,128)} %bitcast.3), calls=%async_computation | async-start | bytes 2097152 | tf_op jit(solution)/shard_map/all_to_all | solution.py:408
  24.1 60.5 %collective-permute-start.1 = (f32[2,512,512]{2,1,0:T(8,128)}, f32[2,512,512]{2,1,0:T(8,128)}, u32[]{:S(2)}, u32[]{:S(2)}) collective-permute-start(f32[2,512,512]{2,1,0:T(8,128)} %get-tuple-element.26), channel_id=1, source_target_pairs={{0,4},{4,8},{8,12},{12,16},{16,20},{20,24},{24,28},{28,32},{32,36}... | collective-permute-start | bytes 6291464 | tf_op jit(solution)/shard_map/ppermute | solution.py:640
  27.7 57.0 %collective-permute-start.2 = (f32[2,512,512]{2,1,0:T(8,128)}, f32[2,512,512]{2,1,0:T(8,128)}, u32[]{:S(2)}, u32[]{:S(2)}) collective-permute-start(f32[2,512,512]{2,1,0:T(8,128)} %get-tuple-element.27), channel_id=1, source_target_pairs={{4,0},{8,4},{12,8},{16,12},{20,16},{24,20},{28,24},{32,28},{36,32}... | collective-permute-start | bytes 6291464 | tf_op jit(solution)/shard_map/ppermute | solution.py:640
  44.4 25.5 %all-to-all-start.1 = ((f32[64,8,256]{2,1,0:T(8,128)}), f32[64,8,256]{2,1,0:T(8,128)S(1)}, u32[]{:S(2)}, u32[]{:S(2)}) async-start(f32[64,8,256]{2,1,0:T(8,128)} %sum_gram.1), calls=%async_computation.1 | async-start | bytes 1048576 | tf_op jit(solution)/shard_map/all_to_all | solution.py:448
  49.0 35.6 %collective-permute-start.3 = (f32[4,64,512]{2,1,0:T(8,128)S(1)}, f32[4,64,512]{2,1,0:T(8,128)S(1)}, u32[]{:S(2)}, u32[]{:S(2)}) collective-permute-start(f32[4,64,512]{2,1,0:T(8,128)S(1)} %copy-done.4), channel_id=1, source_target_pairs={{0,1},{1,2},{2,3},{4,5},{5,6},{6,7},{8,9},{9,10},{10,11},{12,13},{... | collective-permute-start | bytes 1572872 | tf_op jit(solution)/shard_map/ppermute | solution.py:640
  52.0 32.7 %collective-permute-start.4 = (f32[4,64,512]{2,1,0:T(8,128)S(1)}, f32[4,64,512]{2,1,0:T(8,128)S(1)}, u32[]{:S(2)}, u32[]{:S(2)}) collective-permute-start(f32[4,64,512]{2,1,0:T(8,128)S(1)} %copy-done.3), channel_id=1, source_target_pairs={{1,0},{2,1},{3,2},{5,4},{6,5},{7,6},{9,8},{10,9},{11,10},{13,12},{... | collective-permute-start | bytes 1572872 | tf_op jit(solution)/shard_map/ppermute | solution.py:640
  69.8 28.8 %collective-permute-start = (f32[64,8,256]{2,1,0:T(8,128)S(1)}, f32[64,8,256]{2,1,0:T(8,128)S(1)}, u32[]{:S(2)}, u32[]{:S(2)}) collective-permute-start(f32[64,8,256]{2,1,0:T(8,128)S(1)} %all-to-all-done.1.mine), channel_id=1, source_target_pairs={{0,4},{4,0},{1,5},{5,1},{2,6},{6,2},{3,7},{7,3},{8,12},{12,8},{9,1... | collective-permute-start | bytes 1572872 | tf_op jit(solution)/shard_map/ppermute | solution.py:403
  93.1 5.5 %copy-start = (f32[512,128]{1,0:T(8,128)S(1)}, f32[512,128]{1,0:T(8,128)}, u32[]{:S(2)}) copy-start(f32[512,128]{1,0:T(8,128)} %start.1) | copy-start | bytes 786436
  93.1 24.7 %all-to-all-start.2 = ((f32[128,8,256]{2,1,0:T(8,128)}), f32[128,8,256]{2,1,0:T(8,128)S(1)}, u32[]{:S(2)}, u32[]{:S(2)}) async-start(f32[128,8,256]{2,1,0:T(8,128)} %bitcast.4), calls=%async_computation.2 | async-start | bytes 2097152 | tf_op jit(solution)/shard_map/all_to_all | solution.py:408
  115.2 26.5 %copy-start.1 = (f32[128,512]{1,0:T(8,128)S(1)}, f32[128,512]{1,0:T(8,128)}, u32[]{:S(2)}) copy-start(f32[128,512]{1,0:T(8,128)} %get-tuple-element.23.right) | copy-start | bytes 786436
  115.2 26.5 %copy-start.2 = (f32[128,512]{1,0:T(8,128)S(1)}, f32[128,512]{1,0:T(8,128)}, u32[]{:S(2)}) copy-start(f32[128,512]{1,0:T(8,128)} %get-tuple-element.25.image) | copy-start | bytes 786436
  138.3 3.4 %collective-permute-start.5 = (f32[64,8,256]{2,1,0:T(8,128)S(1)}, f32[64,8,256]{2,1,0:T(8,128)S(1)}, u32[]{:S(2)}, u32[]{:S(2)}) collective-permute-start(f32[64,8,256]{2,1,0:T(8,128)S(1)} %all_to_all.20.mine), channel_id=1, source_target_pairs={{0,4},{4,0},{1,5},{5,1},{2,6},{6,2},{3,7},{7,3},{8,12},{12,8},{9,1... | collective-permute-start | bytes 1572872 | tf_op jit(solution)/shard_map/ppermute | solution.py:403

commit v9 on v8

--- a/solution.py
+++ b/solution.py
@@ -204,14 +204,14 @@
     points, obs_far, ctrl_far, conduct, drive,
     total_far, extra_far, total, extra, obs, ctrl, conduct_here, drive_here, sems, obs_sems, ctrl_sems,
 ):
-    steps, rows, rank = ctrl.shape
+    steps, rows, rank = obs.shape
     small = [
         pltpu.make_async_copy(conduct, conduct_here, sems.at[0]),
         pltpu.make_async_copy(drive, drive_here, sems.at[1]),
     ]
 
     def ctrl_copy(i):
-        return pltpu.make_async_copy(ctrl_far.at[i], ctrl.at[i], ctrl_sems.at[i])
+        return pltpu.make_async_copy(ctrl_far.at[i], ctrl.at[i + 2], ctrl_sems.at[i])
 
     def obs_copy(i):
         return pltpu.make_async_copy(obs_far.at[i], obs.at[i], obs_sems.at[i])
@@ -225,6 +225,8 @@
     obs_copy(1).start()
     total[...] = jnp.zeros_like(total)
     extra[...] = jnp.zeros_like(extra)
+    for i in (0, 1, steps + 2, steps + 3):
+        ctrl[i] = jnp.zeros((rows, rank), F32)
     for copy in small:
         copy.wait()
     ctrl_copy(0).wait()
@@ -243,11 +245,10 @@
 
         obs_copy(i).wait()
         half = i % 2
-        center = ctrl[i]
-        beside = (i + 2 < steps).astype(F32) * ctrl[jnp.minimum(i + 2, steps - 1)]
-        beside = beside + (i >= 2).astype(F32) * ctrl[jnp.maximum(i - 2, 0)]
-        before = half.astype(F32) * ctrl[jnp.maximum(i - 1, 0), rows - points :]
-        after = (1 - half).astype(F32) * ctrl[jnp.minimum(i + 1, steps - 1), :points]
+        center = ctrl[i + 2]
+        beside = ctrl[i + 4] + ctrl[i]
+        before = half.astype(F32) * ctrl[i + 1, rows - points :]
+        after = (1 - half).astype(F32) * ctrl[i + 3, :points]
         beside = beside + jnp.concatenate([before, center[: rows - points]], axis=0)
         beside = beside + jnp.concatenate([center[points:], after], axis=0)
         place = lax.broadcasted_iota(jnp.int32, (rows, rank), 0) % points
@@ -284,14 +285,14 @@
             pltpu.VMEM((rank, rank), F32),
             pltpu.VMEM((16, rank), F32),
             pltpu.VMEM((steps, rows, rank), F32),
-            pltpu.VMEM((steps, rows, rank), F32),
+            pltpu.VMEM((steps + 4, rows, rank), F32),
             pltpu.VMEM(conduct.shape, F32),
             pltpu.VMEM(drive.shape, F32),
             pltpu.SemaphoreType.DMA((2,)),
             pltpu.SemaphoreType.DMA((steps,)),
             pltpu.SemaphoreType.DMA((steps,)),
         ],
-        compiler_params=pltpu.CompilerParams(vmem_limit_bytes=36 << 20),
+        compiler_params=pltpu.CompilerParams(vmem_limit_bytes=40 << 20),
         cost_estimate=pl.CostEstimate(
             flops=6 * steps * rows * rank * rank, bytes_accessed=18 << 20, transcendentals=0
         ),
@@ -425,23 +426,40 @@
     half = left.shape[1] // 2
     mine = jnp.where(side[0] == 0, left[:, :half], left[:, half:])
     turned = product3(block, mine, ((1,), (1,)))
-    whole = jnp.concatenate([turned, few[...]], axis=1)
-    out[...] = jnp.broadcast_to(whole[None], out.shape)
+    out[...] = jnp.concatenate([turned, few[...]], axis=1)
+
+
+def spread_kernel(side, mine, theirs, out):
+    both = mine[...] + theirs[...]
+    half = both.shape[1] // 2
+    chosen = jnp.where(side[0] == 0, both[:, :half], both[:, half:])
+    out[...] = jnp.broadcast_to(chosen[None], out.shape)
 
 
 def projected_copies(arrived, left, few):
+    smem = pl.BlockSpec(memory_space=pltpu.SMEM)
     vmem = pl.BlockSpec(memory_space=pltpu.VMEM)
-    return pl.pallas_call(
+    cost = pl.CostEstimate(
+        flops=arrived.size, bytes_accessed=8 * arrived.size, transcendentals=0
+    )
+    mine = pl.pallas_call(
         project_kernel,
-        in_specs=[pl.BlockSpec(memory_space=pltpu.SMEM), vmem, vmem, vmem],
+        in_specs=[smem, vmem, vmem, vmem],
         out_specs=vmem,
-        out_shape=jax.ShapeDtypeStruct((arrived.shape[0] // 2, 8, 256), F32),
+        out_shape=jax.ShapeDtypeStruct((8, 256), F32),
         compiler_params=pltpu.CompilerParams(vmem_limit_bytes=8 << 20),
-        cost_estimate=pl.CostEstimate(
-            flops=arrived.size, bytes_accessed=8 * arrived.size, transcendentals=0
-        ),
+        cost_estimate=cost,
         name="project",
     )(core_index(), arrived, left, few)
+    return pl.pallas_call(
+        spread_kernel,
+        in_specs=[smem, vmem, vmem],
+        out_specs=vmem,
+        out_shape=jax.ShapeDtypeStruct((arrived.shape[0] // 2, 8, 128), F32),
+        compiler_params=pltpu.CompilerParams(vmem_limit_bytes=4 << 20),
+        cost_estimate=cost,
+        name="spread",
+    )(core_index(), mine, swapped(mine))
 
 
 def gathered(copies):
@@ -597,11 +615,11 @@
     )(core_index(), mine, theirs, start, in_hbm(drive), in_hbm(sense))
 
 
-def finish_kernel(order, right, left, image, mine, theirs, mass, state, inputs, outputs):
+def finish_kernel(order, side, right, left, image, mine, theirs, mass, state, inputs, outputs):
     size, rank = right.shape
-    blocks = (mine[...] + theirs[...]).reshape(rank, 2 * size)
-    turned = blocks[:, :size]
-    few = jnp.sum(blocks[:, size:].reshape(rank // 8, 8, size), axis=0)
+    first = side[0] == 0
+    turned = jnp.where(first, mine[...], theirs[...]).reshape(rank, size)
+    few = jnp.sum(jnp.where(first, theirs[...], mine[...]), axis=0)
     kept_col = lax.broadcasted_iota(jnp.int32, (size, size), 0) < order[0]
     kept_row = lax.broadcasted_iota(jnp.int32, (size, size), 1) < order[0]
     kept = jnp.logical_and(kept_col, kept_row).astype(F32)
@@ -617,7 +635,7 @@
     vmem = pl.BlockSpec(memory_space=pltpu.VMEM)
     return pl.pallas_call(
         finish_kernel,
-        in_specs=[pl.BlockSpec(memory_space=pltpu.SMEM)] + [vmem] * 5,
+        in_specs=[pl.BlockSpec(memory_space=pltpu.SMEM)] * 2 + [vmem] * 5,
         out_specs=[vmem] * 4,
         out_shape=[
             jax.ShapeDtypeStruct((size, size), F32),
@@ -630,7 +648,7 @@
             flops=1_000_000_000, bytes_accessed=4 << 20, transcendentals=0
         ),
         name="finish",
-    )(order, right, left, image, mine, theirs)
+    )(order, core_index(), right, left, image, mine, theirs)
 
 
 def from_neighbours(low_face, high_face, axis):

time: 143 us -> 141 us (0.986)
  blocking collectives: 20.2 us -> 17.2 us
    all_to_all x1, blocking collectives: 20.2 us -> 17.2 us  [gathered(): mine = lax.all_to_all(copies, CHIPS, 0, 0, tiled=True)]
    ppermute x2 -> x3, starting transfers between devices: 2.28 us -> 2.94 us  [swapped(): return lax.ppermute(value, 'core', [(0, 1), (1, 0)])]
  transfers between devices with their start and end apart: 9 -> 10, of which waited for: 4 -> 5; matrix products, arithmetic and copies ran while one was open for 0% -> 0% of each run, Pallas kernels for 28% -> 29%
where the time goes in v9:
time: 141 us
  Pallas kernels  53.7 us (38%)
  starting transfers between devices  34.4 us (24%)
  waiting for transfers between devices  34.1 us (24%)
  blocking collectives  17.2 us (12%)
  between operations  1.49 us (1%)
    all_to_all x1, blocking collectives, gathered(): mine = lax.all_to_all(copies, CHIPS, 0, 0, tiled=True)  17.2 us
    all_to_all x2, starting transfers between devices, scattered(): return lax.all_to_all(tiles, CHIPS + ('core',), 0, 0, tiled=True)  17 us
    all_to_all x1, waiting for transfers between devices, gathered(): mine = lax.all_to_all(copies, CHIPS, 0, 0, tiled=True)  16.6 us
    pallas_call x1, Pallas kernels, bases(): pl.pallas_call(bases_kernel, in_specs=[pl.BlockSpec(memory_space=pltpu.SM...  16.6 us
    all_to_all x2, waiting for transfers between devices, scattered(): return lax.all_to_all(tiles, CHIPS + ('core',), 0, 0, tiled=True)  16.2 us
    pallas_call x1, Pallas kernels, inner_operator(): pl.pallas_call(functools.partial(inner_kernel, points), in_specs=[anywher...  14.3 us
    pallas_call x1, Pallas kernels, local_gram(): pl.pallas_call(gram_kernel, in_specs=[anywhere] * 3, out_specs=[vmem] + [...  11.9 us
    pallas_call x1, Pallas kernels, with_outer(): pl.pallas_call(functools.partial(outer_kernel, points), in_specs=[anywher...  8.43 us
  transfers between devices with their start and end apart: 10, of which 5 were waited for; matrix products, arithmetic and copies ran while one was open for 0% of the time, Pallas kernels for 29%

profile of v9, /device:TPU:1, one launch (start us, length us, event | category | flops | bytes accessed | tf_op | source)
XLA Modules:
  0.0 140.9 jit_solution(10291989987475065378)
XLA Ops:
  0.6 11.9 %local_gram.1 = (f32[64,2,8,256]{3,2,1,0:T(8,128)}, f32[16,512]{1,0:T(8,128)}, f32[2,512,512]{2,1,0:T(8,128)}, f32[2,512,512]{2,1,0:T(8,128)}, f32[4,64,512]{2,1,0:T(8,128)}, /*index=5*/f32[4,64,512]{2,1,0:T(8,128)}) custom-call(f32[8,512,512]{2,1,0:T(8,128)} %bitcast.6, f32[8,512,512]{2,1,0:T(8,128)} %bitcast.9, f32[4,4,1024]{2,1,0:T(4,128)} %sense.1), custom_call_target="tpu_custom_call" | custom-call | flops 6442450944 | bytes 25165824 | tf_op jit(solution)/shard_map/local_gram/pallas_call | solution.py:170
  12.6 11.5 %all-to-all-start = ((f32[128,8,256]{2,1,0:T(8,128)}), f32[128,8,256]{2,1,0:T(8,128)S(1)}, u32[]{:S(2)}, u32[]{:S(2)}) async-start(f32[128,8,256]{2,1,0:T(8,128)} %bitcast.3), calls=%async_computation | async-start | bytes 2097152 | tf_op jit(solution)/shard_map/all_to_all | solution.py:409
  24.1 3.5 %collective-permute-start.1 = (f32[2,512,512]{2,1,0:T(8,128)}, f32[2,512,512]{2,1,0:T(8,128)}, u32[]{:S(2)}, u32[]{:S(2)}) collective-permute-start(f32[2,512,512]{2,1,0:T(8,128)} %get-tuple-element.26), channel_id=1, source_target_pairs={{0,4},{4,8},{8,12},{12,16},{16,20},{20,24},{24,28},{28,32},{32,36}... | collective-permute-start | bytes 6291464 | tf_op jit(solution)/shard_map/ppermute | solution.py:658
  27.6 2.1 %collective-permute-start.2 = (f32[2,512,512]{2,1,0:T(8,128)}, f32[2,512,512]{2,1,0:T(8,128)}, u32[]{:S(2)}, u32[]{:S(2)}) collective-permute-start(f32[2,512,512]{2,1,0:T(8,128)} %get-tuple-element.27), channel_id=1, source_target_pairs={{4,0},{8,4},{12,8},{16,12},{20,16},{24,20},{28,24},{32,28},{36,32}... | collective-permute-start | bytes 6291464 | tf_op jit(solution)/shard_map/ppermute | solution.py:658
  29.8 13.6 %all-to-all-done.parts = f32[128,8,256]{2,1,0:T(8,128)S(1)} async-done(((f32[128,8,256]{2,1,0:T(8,128)}), f32[128,8,256]{2,1,0:T(8,128)S(1)}, u32[]{:S(2)}, u32[]{:S(2)}) %all-to-all-start) | async-done | bytes 1048608 | tf_op jit(solution)/shard_map/all_to_all | solution.py:409
  43.3 1.0 sum_gram.1
  44.3 4.6 %all-to-all-start.1 = ((f32[64,8,256]{2,1,0:T(8,128)}), f32[64,8,256]{2,1,0:T(8,128)S(1)}, u32[]{:S(2)}, u32[]{:S(2)}) async-start(f32[64,8,256]{2,1,0:T(8,128)} %sum_gram.1), calls=%async_computation.1 | async-start | bytes 1048576 | tf_op jit(solution)/shard_map/all_to_all | solution.py:466
  49.0 2.9 %collective-permute-start.3 = (f32[4,64,512]{2,1,0:T(8,128)S(1)}, f32[4,64,512]{2,1,0:T(8,128)S(1)}, u32[]{:S(2)}, u32[]{:S(2)}) collective-permute-start(f32[4,64,512]{2,1,0:T(8,128)S(1)} %copy-done.4), channel_id=1, source_target_pairs={{0,1},{1,2},{2,3},{4,5},{5,6},{6,7},{8,9},{9,10},{10,11},{12,13},{... | collective-permute-start | bytes 1572872 | tf_op jit(solution)/shard_map/ppermute | solution.py:658
  51.9 1.3 collective-permute-start.4
  53.2 16.6 %all-to-all-done.1.mine = f32[64,8,256]{2,1,0:T(8,128)S(1)} async-done(((f32[64,8,256]{2,1,0:T(8,128)}), f32[64,8,256]{2,1,0:T(8,128)S(1)}, u32[]{:S(2)}, u32[]{:S(2)}) %all-to-all-start.1) | async-done | bytes 524320 | tf_op jit(solution)/shard_map/all_to_all | solution.py:466
  69.8 0.4 collective-permute-start
  70.2 14.3 %inner_operator.1 = (f32[512,512]{1,0:T(8,128)}, f32[16,512]{1,0:T(8,128)}) custom-call(f32[8,512,512]{2,1,0:T(8,128)} %bitcast.7, f32[8,512,512]{2,1,0:T(8,128)} %bitcast.10, f32[4,1024]{1,0:T(4,128)} %conduct.3, f32[4,4,1024]{2,1,0:T(4,128)} %drive.1), custom_call_target="tpu_custom_call" | custom-call | flops 6442450944 | bytes 18874368 | tf_op jit(solution)/shard_map/inner_operator/pallas_call | solution.py:276
  84.6 8.4 %outer_operator.1 = f32[64,2,8,256]{3,2,1,0:T(8,128)} custom-call(f32[8,512,512]{2,1,0:T(8,128)} %bitcast.8, f32[2,512,512]{2,1,0:T(8,128)} %collective-permute-done.1.zlow, f32[2,512,512]{2,1,0:T(8,128)} %collective-permute-done.2.zhigh, f32[4,1024]{1,0:T(4,128)} %conduct.3, f32[512,512]{1,0:T(8,128)} %get-tuple-element.28.inner, ...), custom_call_target="tpu_custom_call" | custom-call | flops 4026531840 | bytes 7340032 | tf_op jit(solution)/shard_map/outer_operator/pallas_call | solution.py:375
  93.0 0.0 copy-start
  93.1 5.5 %all-to-all-start.2 = ((f32[128,8,256]{2,1,0:T(8,128)}), f32[128,8,256]{2,1,0:T(8,128)S(1)}, u32[]{:S(2)}, u32[]{:S(2)}) async-start(f32[128,8,256]{2,1,0:T(8,128)} %bitcast.4), calls=%async_computation.2 | async-start | bytes 2097152 | tf_op jit(solution)/shard_map/all_to_all | solution.py:409
  98.6 16.6 %bases.1 = (f32[128,512]{1,0:T(8,128)}, f32[128,512]{1,0:T(8,128)S(1)}, f32[128,512]{1,0:T(8,128)}, f32[8,128]{1,0:T(8,128)S(1)}) custom-call(s32[1]{0:T(128)} %bitcast.core.side, f32[64,8,256]{2,1,0:T(8,128)S(1)} %all-to-all-done.1.mine, f32[64,8,256]{2,1,0:T(8,128)S(1)} %collective-permute-done.theirs, f32[512,128]{1,0:T(8,128)S(1)} %copy-done, ...), custom_call_target="tpu_custom_call" | custom-call | flops 20000000000 | bytes 4194304 | tf_op jit(solution)/shard_map/bases/pallas_call | solution.py:589
  115.2 2.6 %all-to-all-done.2.parts = f32[128,8,256]{2,1,0:T(8,128)S(1)} async-done(((f32[128,8,256]{2,1,0:T(8,128)}), f32[128,8,256]{2,1,0:T(8,128)S(1)}, u32[]{:S(2)}, u32[]{:S(2)}) %all-to-all-start.2) | async-done | bytes 1048608 | tf_op jit(solution)/shard_map/all_to_all | solution.py:409
  117.8 0.3 project.1.mine
  118.0 1.0 collective-permute-start.5
  119.0 0.8 collective-permute-done.5.theirs
  119.9 17.2 %all_to_all.20.mine = f32[64,8,128]{2,1,0:T(8,128)S(1)} all-to-all(f32[64,8,128]{2,1,0:T(8,128)S(1)} %spread.1), channel_id=1, replica_groups=mesh['chip'=16,'core'=2,'sub'=4] {'chip','sub'}, dimensions={0} | all-to-all | bytes 524288 | tf_op jit(solution)/shard_map/all_to_all | solution.py:466
  137.1 1.5 %collective-permute-start.6 = (f32[64,8,128]{2,1,0:T(8,128)S(1)}, f32[64,8,128]{2,1,0:T(8,128)S(1)}, u32[]{:S(2)}, u32[]{:S(2)}) collective-permute-start(f32[64,8,128]{2,1,0:T(8,128)S(1)} %all_to_all.20.mine), channel_id=1, source_target_pairs={{0,4},{4,0},{1,5},{5,1},{2,6},{6,2},{3,7},{7,3},{8,12},{12,8},{9,1... | collective-permute-start | bytes 786440 | tf_op jit(solution)/shard_map/ppermute | solution.py:404
  139.2 0.5 collective-permute-done.6.theirs
  139.7 1.2 finish.1
  (15 shorter events, 0.1 us)
Async XLA Ops:
  12.6 36.4 %copy-start.4 = (f32[4,64,512]{2,1,0:T(8,128)S(1)}, f32[4,64,512]{2,1,0:T(8,128)}, u32[]{:S(2)}) copy-start(f32[4,64,512]{2,1,0:T(8,128)} %get-tuple-element.29) | copy-start | bytes 1572868
  12.6 39.3 %copy-start.3 = (f32[4,64,512]{2,1,0:T(8,128)S(1)}, f32[4,64,512]{2,1,0:T(8,128)}, u32[]{:S(2)}) copy-start(f32[4,64,512]{2,1,0:T(8,128)} %get-tuple-element.30) | copy-start | bytes 1572868
  12.6 30.7 %all-to-all-start = ((f32[128,8,256]{2,1,0:T(8,128)}), f32[128,8,256]{2,1,0:T(8,128)S(1)}, u32[]{:S(2)}, u32[]{:S(2)}) async-start(f32[128,8,256]{2,1,0:T(8,128)} %bitcast.3), calls=%async_computation | async-start | bytes 2097152 | tf_op jit(solution)/shard_map/all_to_all | solution.py:409
  24.1 60.5 %collective-permute-start.1 = (f32[2,512,512]{2,1,0:T(8,128)}, f32[2,512,512]{2,1,0:T(8,128)}, u32[]{:S(2)}, u32[]{:S(2)}) collective-permute-start(f32[2,512,512]{2,1,0:T(8,128)} %get-tuple-element.26), channel_id=1, source_target_pairs={{0,4},{4,8},{8,12},{12,16},{16,20},{20,24},{24,28},{28,32},{32,36}... | collective-permute-start | bytes 6291464 | tf_op jit(solution)/shard_map/ppermute | solution.py:658
  27.6 56.9 %collective-permute-start.2 = (f32[2,512,512]{2,1,0:T(8,128)}, f32[2,512,512]{2,1,0:T(8,128)}, u32[]{:S(2)}, u32[]{:S(2)}) collective-permute-start(f32[2,512,512]{2,1,0:T(8,128)} %get-tuple-element.27), channel_id=1, source_target_pairs={{4,0},{8,4},{12,8},{16,12},{20,16},{24,20},{28,24},{32,28},{36,32}... | collective-permute-start | bytes 6291464 | tf_op jit(solution)/shard_map/ppermute | solution.py:658
  44.3 25.5 %all-to-all-start.1 = ((f32[64,8,256]{2,1,0:T(8,128)}), f32[64,8,256]{2,1,0:T(8,128)S(1)}, u32[]{:S(2)}, u32[]{:S(2)}) async-start(f32[64,8,256]{2,1,0:T(8,128)} %sum_gram.1), calls=%async_computation.1 | async-start | bytes 1048576 | tf_op jit(solution)/shard_map/all_to_all | solution.py:466
  49.0 35.6 %collective-permute-start.3 = (f32[4,64,512]{2,1,0:T(8,128)S(1)}, f32[4,64,512]{2,1,0:T(8,128)S(1)}, u32[]{:S(2)}, u32[]{:S(2)}) collective-permute-start(f32[4,64,512]{2,1,0:T(8,128)S(1)} %copy-done.4), channel_id=1, source_target_pairs={{0,1},{1,2},{2,3},{4,5},{5,6},{6,7},{8,9},{9,10},{10,11},{12,13},{... | collective-permute-start | bytes 1572872 | tf_op jit(solution)/shard_map/ppermute | solution.py:658
  51.9 32.6 %collective-permute-start.4 = (f32[4,64,512]{2,1,0:T(8,128)S(1)}, f32[4,64,512]{2,1,0:T(8,128)S(1)}, u32[]{:S(2)}, u32[]{:S(2)}) collective-permute-start(f32[4,64,512]{2,1,0:T(8,128)S(1)} %copy-done.3), channel_id=1, source_target_pairs={{1,0},{2,1},{3,2},{5,4},{6,5},{7,6},{9,8},{10,9},{11,10},{13,12},{... | collective-permute-start | bytes 1572872 | tf_op jit(solution)/shard_map/ppermute | solution.py:658
  69.8 28.7 %collective-permute-start = (f32[64,8,256]{2,1,0:T(8,128)S(1)}, f32[64,8,256]{2,1,0:T(8,128)S(1)}, u32[]{:S(2)}, u32[]{:S(2)}) collective-permute-start(f32[64,8,256]{2,1,0:T(8,128)S(1)} %all-to-all-done.1.mine), channel_id=1, source_target_pairs={{0,4},{4,0},{1,5},{5,1},{2,6},{6,2},{3,7},{7,3},{8,12},{12,8},{9,1... | collective-permute-start | bytes 1572872 | tf_op jit(solution)/shard_map/ppermute | solution.py:404
  93.0 5.5 %copy-start = (f32[512,128]{1,0:T(8,128)S(1)}, f32[512,128]{1,0:T(8,128)}, u32[]{:S(2)}) copy-start(f32[512,128]{1,0:T(8,128)} %start.1) | copy-start | bytes 786436
  93.1 24.7 %all-to-all-start.2 = ((f32[128,8,256]{2,1,0:T(8,128)}), f32[128,8,256]{2,1,0:T(8,128)S(1)}, u32[]{:S(2)}, u32[]{:S(2)}) async-start(f32[128,8,256]{2,1,0:T(8,128)} %bitcast.4), calls=%async_computation.2 | async-start | bytes 2097152 | tf_op jit(solution)/shard_map/all_to_all | solution.py:409
  115.1 24.6 %copy-start.1 = (f32[128,512]{1,0:T(8,128)S(1)}, f32[128,512]{1,0:T(8,128)}, u32[]{:S(2)}) copy-start(f32[128,512]{1,0:T(8,128)} %get-tuple-element.23.right) | copy-start | bytes 786436
  115.1 24.6 %copy-start.2 = (f32[128,512]{1,0:T(8,128)S(1)}, f32[128,512]{1,0:T(8,128)}, u32[]{:S(2)}) copy-start(f32[128,512]{1,0:T(8,128)} %get-tuple-element.25.image) | copy-start | bytes 786436
  118.0 1.8 %collective-permute-start.5 = (f32[8,256]{1,0:T(8,128)S(1)}, f32[8,256]{1,0:T(8,128)S(1)}, u32[]{:S(2)}, u32[]{:S(2)}) collective-permute-start(f32[8,256]{1,0:T(8,128)S(1)} %project.1.mine), channel_id=1, source_target_pairs={{0,4},{4,0},{1,5},{5,1},{2,6},{6,2},{3,7},{7,3},{8,12},{12,8},{9,1... | collective-permute-start | bytes 24584 | tf_op jit(solution)/shard_map/ppermute | solution.py:404
  137.1 2.7 %collective-permute-start.6 = (f32[64,8,128]{2,1,0:T(8,128)S(1)}, f32[64,8,128]{2,1,0:T(8,128)S(1)}, u32[]{:S(2)}, u32[]{:S(2)}) collective-permute-start(f32[64,8,128]{2,1,0:T(8,128)S(1)} %all_to_all.20.mine), channel_id=1, source_target_pairs={{0,4},{4,0},{1,5},{5,1},{2,6},{6,2},{3,7},{7,3},{8,12},{12,8},{9,1... | collective-permute-start | bytes 786440 | tf_op jit(solution)/shard_map/ppermute | solution.py:404

commit v10 on v9

--- a/solution.py
+++ b/solution.py
@@ -109,6 +109,7 @@
         source = ctrl_here.at[2 * p + 1, pl.ds(rows - points, points)]
         return pltpu.make_async_copy(source, yhigh.at[p], high_sems.at[p])
 
+    late = steps // 2
     sense_copy = pltpu.make_async_copy(sense, sense_here, other_sems.at[0])
     for i in range(AHEAD):
         for copy in copies(i):
@@ -131,15 +132,21 @@
 
         for j in range(4):
 
-            @pl.when(i == (j if j < 2 else steps - 4 + j))
+            @pl.when(i == (j + late if j < 2 else steps - 4 + j))
             def _():
                 z_copy(j).start()
 
-        @pl.when(i % 2 == 0)
+        @pl.when(i == late)
+        def _():
+            for p in range(late // 2):
+                low_copy(p).start()
+                high_copy(p).start()
+
+        @pl.when(jnp.logical_and(i >= late, i % 2 == 0))
         def _():
             low_copy(i // 2).start()
 
-        @pl.when(i % 2 == 1)
+        @pl.when(jnp.logical_and(i > late, i % 2 == 1))
         def _():
             high_copy(i // 2).start()
 

time: 141 us -> 142 us (level)
  transfers between devices with their start and end apart: 10 -> 10, of which waited for: 5 -> 5; matrix products, arithmetic and copies ran while one was open for 0% -> 0% of each run, Pallas kernels for 29% -> 28%
where the time goes in v10:
time: 142 us
  Pallas kernels  54.4 us (38%)
  starting transfers between devices  34.4 us (24%)
  waiting for transfers between devices  34.1 us (24%)
  blocking collectives  17.2 us (12%)
  between operations  1.49 us (1%)
    all_to_all x1, blocking collectives, gathered(): mine = lax.all_to_all(copies, CHIPS, 0, 0, tiled=True)  17.2 us
    all_to_all x2, starting transfers between devices, scattered(): return lax.all_to_all(tiles, CHIPS + ('core',), 0, 0, tiled=True)  17 us
    all_to_all x1, waiting for transfers between devices, gathered(): mine = lax.all_to_all(copies, CHIPS, 0, 0, tiled=True)  16.6 us
    pallas_call x1, Pallas kernels, bases(): pl.pallas_call(bases_kernel, in_specs=[pl.BlockSpec(memory_space=pltpu.SM...  16.6 us
    all_to_all x2, waiting for transfers between devices, scattered(): return lax.all_to_all(tiles, CHIPS + ('core',), 0, 0, tiled=True)  16.2 us
    pallas_call x1, Pallas kernels, inner_operator(): pl.pallas_call(functools.partial(inner_kernel, points), in_specs=[anywher...  14.3 us
    pallas_call x1, Pallas kernels, local_gram(): pl.pallas_call(gram_kernel, in_specs=[anywhere] * 3, out_specs=[vmem] + [...  12.6 us
    pallas_call x1, Pallas kernels, with_outer(): pl.pallas_call(functools.partial(outer_kernel, points), in_specs=[anywher...  8.43 us
  transfers between devices with their start and end apart: 10, of which 5 were waited for; matrix products, arithmetic and copies ran while one was open for 0% of the time, Pallas kernels for 28%

profile of v10, /device:TPU:1, one launch (start us, length us, event | category | flops | bytes accessed | tf_op | source)
XLA Modules:
  0.0 141.6 jit_solution(3016297009899212596)
XLA Ops:
  0.6 12.6 %local_gram.1 = (f32[64,2,8,256]{3,2,1,0:T(8,128)}, f32[16,512]{1,0:T(8,128)}, f32[2,512,512]{2,1,0:T(8,128)}, f32[2,512,512]{2,1,0:T(8,128)}, f32[4,64,512]{2,1,0:T(8,128)}, /*index=5*/f32[4,64,512]{2,1,0:T(8,128)}) custom-call(f32[8,512,512]{2,1,0:T(8,128)} %bitcast.6, f32[8,512,512]{2,1,0:T(8,128)} %bitcast.9, f32[4,4,1024]{2,1,0:T(4,128)} %sense.1), custom_call_target="tpu_custom_call" | custom-call | flops 6442450944 | bytes 25165824 | tf_op jit(solution)/shard_map/local_gram/pallas_call | solution.py:177
  13.3 11.5 %all-to-all-start = ((f32[128,8,256]{2,1,0:T(8,128)}), f32[128,8,256]{2,1,0:T(8,128)S(1)}, u32[]{:S(2)}, u32[]{:S(2)}) async-start(f32[128,8,256]{2,1,0:T(8,128)} %bitcast.3), calls=%async_computation | async-start | bytes 2097152 | tf_op jit(solution)/shard_map/all_to_all | solution.py:416
  24.8 3.5 %collective-permute-start.1 = (f32[2,512,512]{2,1,0:T(8,128)}, f32[2,512,512]{2,1,0:T(8,128)}, u32[]{:S(2)}, u32[]{:S(2)}) collective-permute-start(f32[2,512,512]{2,1,0:T(8,128)} %get-tuple-element.26), channel_id=1, source_target_pairs={{0,4},{4,8},{8,12},{12,16},{16,20},{20,24},{24,28},{28,32},{32,36}... | collective-permute-start | bytes 6291464 | tf_op jit(solution)/shard_map/ppermute | solution.py:665
  28.3 2.1 %collective-permute-start.2 = (f32[2,512,512]{2,1,0:T(8,128)}, f32[2,512,512]{2,1,0:T(8,128)}, u32[]{:S(2)}, u32[]{:S(2)}) collective-permute-start(f32[2,512,512]{2,1,0:T(8,128)} %get-tuple-element.27), channel_id=1, source_target_pairs={{4,0},{8,4},{12,8},{16,12},{20,16},{24,20},{28,24},{32,28},{36,32}... | collective-permute-start | bytes 6291464 | tf_op jit(solution)/shard_map/ppermute | solution.py:665
  30.4 13.6 %all-to-all-done.parts = f32[128,8,256]{2,1,0:T(8,128)S(1)} async-done(((f32[128,8,256]{2,1,0:T(8,128)}), f32[128,8,256]{2,1,0:T(8,128)S(1)}, u32[]{:S(2)}, u32[]{:S(2)}) %all-to-all-start) | async-done | bytes 1048608 | tf_op jit(solution)/shard_map/all_to_all | solution.py:416
  44.0 1.0 sum_gram.1
  45.0 4.6 %all-to-all-start.1 = ((f32[64,8,256]{2,1,0:T(8,128)}), f32[64,8,256]{2,1,0:T(8,128)S(1)}, u32[]{:S(2)}, u32[]{:S(2)}) async-start(f32[64,8,256]{2,1,0:T(8,128)} %sum_gram.1), calls=%async_computation.1 | async-start | bytes 1048576 | tf_op jit(solution)/shard_map/all_to_all | solution.py:473
  49.7 2.9 %collective-permute-start.3 = (f32[4,64,512]{2,1,0:T(8,128)S(1)}, f32[4,64,512]{2,1,0:T(8,128)S(1)}, u32[]{:S(2)}, u32[]{:S(2)}) collective-permute-start(f32[4,64,512]{2,1,0:T(8,128)S(1)} %copy-done.4), channel_id=1, source_target_pairs={{0,1},{1,2},{2,3},{4,5},{5,6},{6,7},{8,9},{9,10},{10,11},{12,13},{... | collective-permute-start | bytes 1572872 | tf_op jit(solution)/shard_map/ppermute | solution.py:665
  52.6 1.3 collective-permute-start.4
  53.9 16.6 %all-to-all-done.1.mine = f32[64,8,256]{2,1,0:T(8,128)S(1)} async-done(((f32[64,8,256]{2,1,0:T(8,128)}), f32[64,8,256]{2,1,0:T(8,128)S(1)}, u32[]{:S(2)}, u32[]{:S(2)}) %all-to-all-start.1) | async-done | bytes 524320 | tf_op jit(solution)/shard_map/all_to_all | solution.py:473
  70.5 0.4 collective-permute-start
  70.9 14.3 %inner_operator.1 = (f32[512,512]{1,0:T(8,128)}, f32[16,512]{1,0:T(8,128)}) custom-call(f32[8,512,512]{2,1,0:T(8,128)} %bitcast.7, f32[8,512,512]{2,1,0:T(8,128)} %bitcast.10, f32[4,1024]{1,0:T(4,128)} %conduct.3, f32[4,4,1024]{2,1,0:T(4,128)} %drive.1), custom_call_target="tpu_custom_call" | custom-call | flops 6442450944 | bytes 18874368 | tf_op jit(solution)/shard_map/inner_operator/pallas_call | solution.py:283
  85.3 8.4 %outer_operator.1 = f32[64,2,8,256]{3,2,1,0:T(8,128)} custom-call(f32[8,512,512]{2,1,0:T(8,128)} %bitcast.8, f32[2,512,512]{2,1,0:T(8,128)} %collective-permute-done.1.zlow, f32[2,512,512]{2,1,0:T(8,128)} %collective-permute-done.2.zhigh, f32[4,1024]{1,0:T(4,128)} %conduct.3, f32[512,512]{1,0:T(8,128)} %get-tuple-element.28.inner, ...), custom_call_target="tpu_custom_call" | custom-call | flops 4026531840 | bytes 7340032 | tf_op jit(solution)/shard_map/outer_operator/pallas_call | solution.py:382
  93.7 0.0 copy-start
  93.7 5.5 %all-to-all-start.2 = ((f32[128,8,256]{2,1,0:T(8,128)}), f32[128,8,256]{2,1,0:T(8,128)S(1)}, u32[]{:S(2)}, u32[]{:S(2)}) async-start(f32[128,8,256]{2,1,0:T(8,128)} %bitcast.4), calls=%async_computation.2 | async-start | bytes 2097152 | tf_op jit(solution)/shard_map/all_to_all | solution.py:416
  99.2 16.6 %bases.1 = (f32[128,512]{1,0:T(8,128)}, f32[128,512]{1,0:T(8,128)S(1)}, f32[128,512]{1,0:T(8,128)}, f32[8,128]{1,0:T(8,128)S(1)}) custom-call(s32[1]{0:T(128)} %bitcast.core.side, f32[64,8,256]{2,1,0:T(8,128)S(1)} %all-to-all-done.1.mine, f32[64,8,256]{2,1,0:T(8,128)S(1)} %collective-permute-done.theirs, f32[512,128]{1,0:T(8,128)S(1)} %copy-done, ...), custom_call_target="tpu_custom_call" | custom-call | flops 20000000000 | bytes 4194304 | tf_op jit(solution)/shard_map/bases/pallas_call | solution.py:596
  115.8 2.6 %all-to-all-done.2.parts = f32[128,8,256]{2,1,0:T(8,128)S(1)} async-done(((f32[128,8,256]{2,1,0:T(8,128)}), f32[128,8,256]{2,1,0:T(8,128)S(1)}, u32[]{:S(2)}, u32[]{:S(2)}) %all-to-all-start.2) | async-done | bytes 1048608 | tf_op jit(solution)/shard_map/all_to_all | solution.py:416
  118.4 0.3 project.1.mine
  118.7 1.0 collective-permute-start.5
  119.7 0.8 collective-permute-done.5.theirs
  120.6 17.2 %all_to_all.20.mine = f32[64,8,128]{2,1,0:T(8,128)S(1)} all-to-all(f32[64,8,128]{2,1,0:T(8,128)S(1)} %spread.1), channel_id=1, replica_groups=mesh['chip'=16,'core'=2,'sub'=4] {'chip','sub'}, dimensions={0} | all-to-all | bytes 524288 | tf_op jit(solution)/shard_map/all_to_all | solution.py:473
  137.7 1.5 %collective-permute-start.6 = (f32[64,8,128]{2,1,0:T(8,128)S(1)}, f32[64,8,128]{2,1,0:T(8,128)S(1)}, u32[]{:S(2)}, u32[]{:S(2)}) collective-permute-start(f32[64,8,128]{2,1,0:T(8,128)S(1)} %all_to_all.20.mine), channel_id=1, source_target_pairs={{0,4},{4,0},{1,5},{5,1},{2,6},{6,2},{3,7},{7,3},{8,12},{12,8},{9,1... | collective-permute-start | bytes 786440 | tf_op jit(solution)/shard_map/ppermute | solution.py:411
  139.9 0.5 collective-permute-done.6.theirs
  140.4 1.2 finish.1
  (15 shorter events, 0.1 us)
Async XLA Ops:
  13.3 36.4 %copy-start.4 = (f32[4,64,512]{2,1,0:T(8,128)S(1)}, f32[4,64,512]{2,1,0:T(8,128)}, u32[]{:S(2)}) copy-start(f32[4,64,512]{2,1,0:T(8,128)} %get-tuple-element.29) | copy-start | bytes 1572868
  13.3 39.3 %copy-start.3 = (f32[4,64,512]{2,1,0:T(8,128)S(1)}, f32[4,64,512]{2,1,0:T(8,128)}, u32[]{:S(2)}) copy-start(f32[4,64,512]{2,1,0:T(8,128)} %get-tuple-element.30) | copy-start | bytes 1572868
  13.3 30.7 %all-to-all-start = ((f32[128,8,256]{2,1,0:T(8,128)}), f32[128,8,256]{2,1,0:T(8,128)S(1)}, u32[]{:S(2)}, u32[]{:S(2)}) async-start(f32[128,8,256]{2,1,0:T(8,128)} %bitcast.3), calls=%async_computation | async-start | bytes 2097152 | tf_op jit(solution)/shard_map/all_to_all | solution.py:416
  24.8 60.5 %collective-permute-start.1 = (f32[2,512,512]{2,1,0:T(8,128)}, f32[2,512,512]{2,1,0:T(8,128)}, u32[]{:S(2)}, u32[]{:S(2)}) collective-permute-start(f32[2,512,512]{2,1,0:T(8,128)} %get-tuple-element.26), channel_id=1, source_target_pairs={{0,4},{4,8},{8,12},{12,16},{16,20},{20,24},{24,28},{28,32},{32,36}... | collective-permute-start | bytes 6291464 | tf_op jit(solution)/shard_map/ppermute | solution.py:665
  28.3 56.9 %collective-permute-start.2 = (f32[2,512,512]{2,1,0:T(8,128)}, f32[2,512,512]{2,1,0:T(8,128)}, u32[]{:S(2)}, u32[]{:S(2)}) collective-permute-start(f32[2,512,512]{2,1,0:T(8,128)} %get-tuple-element.27), channel_id=1, source_target_pairs={{4,0},{8,4},{12,8},{16,12},{20,16},{24,20},{28,24},{32,28},{36,32}... | collective-permute-start | bytes 6291464 | tf_op jit(solution)/shard_map/ppermute | solution.py:665
  45.0 25.5 %all-to-all-start.1 = ((f32[64,8,256]{2,1,0:T(8,128)}), f32[64,8,256]{2,1,0:T(8,128)S(1)}, u32[]{:S(2)}, u32[]{:S(2)}) async-start(f32[64,8,256]{2,1,0:T(8,128)} %sum_gram.1), calls=%async_computation.1 | async-start | bytes 1048576 | tf_op jit(solution)/shard_map/all_to_all | solution.py:473
  49.7 35.6 %collective-permute-start.3 = (f32[4,64,512]{2,1,0:T(8,128)S(1)}, f32[4,64,512]{2,1,0:T(8,128)S(1)}, u32[]{:S(2)}, u32[]{:S(2)}) collective-permute-start(f32[4,64,512]{2,1,0:T(8,128)S(1)} %copy-done.4), channel_id=1, source_target_pairs={{0,1},{1,2},{2,3},{4,5},{5,6},{6,7},{8,9},{9,10},{10,11},{12,13},{... | collective-permute-start | bytes 1572872 | tf_op jit(solution)/shard_map/ppermute | solution.py:665
  52.6 32.6 %collective-permute-start.4 = (f32[4,64,512]{2,1,0:T(8,128)S(1)}, f32[4,64,512]{2,1,0:T(8,128)S(1)}, u32[]{:S(2)}, u32[]{:S(2)}) collective-permute-start(f32[4,64,512]{2,1,0:T(8,128)S(1)} %copy-done.3), channel_id=1, source_target_pairs={{1,0},{2,1},{3,2},{5,4},{6,5},{7,6},{9,8},{10,9},{11,10},{13,12},{... | collective-permute-start | bytes 1572872 | tf_op jit(solution)/shard_map/ppermute | solution.py:665
  70.5 28.7 %collective-permute-start = (f32[64,8,256]{2,1,0:T(8,128)S(1)}, f32[64,8,256]{2,1,0:T(8,128)S(1)}, u32[]{:S(2)}, u32[]{:S(2)}) collective-permute-start(f32[64,8,256]{2,1,0:T(8,128)S(1)} %all-to-all-done.1.mine), channel_id=1, source_target_pairs={{0,4},{4,0},{1,5},{5,1},{2,6},{6,2},{3,7},{7,3},{8,12},{12,8},{9,1... | collective-permute-start | bytes 1572872 | tf_op jit(solution)/shard_map/ppermute | solution.py:411
  93.7 5.5 %copy-start = (f32[512,128]{1,0:T(8,128)S(1)}, f32[512,128]{1,0:T(8,128)}, u32[]{:S(2)}) copy-start(f32[512,128]{1,0:T(8,128)} %start.1) | copy-start | bytes 786436
  93.7 24.7 %all-to-all-start.2 = ((f32[128,8,256]{2,1,0:T(8,128)}), f32[128,8,256]{2,1,0:T(8,128)S(1)}, u32[]{:S(2)}, u32[]{:S(2)}) async-start(f32[128,8,256]{2,1,0:T(8,128)} %bitcast.4), calls=%async_computation.2 | async-start | bytes 2097152 | tf_op jit(solution)/shard_map/all_to_all | solution.py:416
  115.8 24.6 %copy-start.1 = (f32[128,512]{1,0:T(8,128)S(1)}, f32[128,512]{1,0:T(8,128)}, u32[]{:S(2)}) copy-start(f32[128,512]{1,0:T(8,128)} %get-tuple-element.23.right) | copy-start | bytes 786436
  115.8 24.6 %copy-start.2 = (f32[128,512]{1,0:T(8,128)S(1)}, f32[128,512]{1,0:T(8,128)}, u32[]{:S(2)}) copy-start(f32[128,512]{1,0:T(8,128)} %get-tuple-element.25.image) | copy-start | bytes 786436
  118.7 1.8 %collective-permute-start.5 = (f32[8,256]{1,0:T(8,128)S(1)}, f32[8,256]{1,0:T(8,128)S(1)}, u32[]{:S(2)}, u32[]{:S(2)}) collective-permute-start(f32[8,256]{1,0:T(8,128)S(1)} %project.1.mine), channel_id=1, source_target_pairs={{0,4},{4,0},{1,5},{5,1},{2,6},{6,2},{3,7},{7,3},{8,12},{12,8},{9,1... | collective-permute-start | bytes 24584 | tf_op jit(solution)/shard_map/ppermute | solution.py:411
  137.7 2.7 %collective-permute-start.6 = (f32[64,8,128]{2,1,0:T(8,128)S(1)}, f32[64,8,128]{2,1,0:T(8,128)S(1)}, u32[]{:S(2)}, u32[]{:S(2)}) collective-permute-start(f32[64,8,128]{2,1,0:T(8,128)S(1)} %all_to_all.20.mine), channel_id=1, source_target_pairs={{0,4},{4,0},{1,5},{5,1},{2,6},{6,2},{3,7},{7,3},{8,12},{12,8},{9,1... | collective-permute-start | bytes 786440 | tf_op jit(solution)/shard_map/ppermute | solution.py:411
